TPU v7x, 32 devices: a whole 2x2x4 slice. The times are simulated.
32 devices in a mesh: emb: 8 (over z, x), seq: 4 (over y, core).
Axes of the slice: x: 2, y: 2, z: 4, core: 2. Of those that a mesh axis runs over, the one named last changes fastest.
Arguments:
- item_table: bfloat16 [32768, 512], P('emb'), may hold values from -6 to 6
- fetch_rows: int32 [8, 4, 8, 64], P('emb', 'seq'), may hold values from 0 to 4095
- event_slot: int32 [32768], P(('emb', 'seq')), may hold values from 0 to 511, as said below
- lengths: int32 [32, 8], P(('emb', 'seq')), may hold values from 1 to 512, 1024 in all within a row
- in_weight: bfloat16 [512, 2048], replicated, may hold values from -0.25 to 0.25
- out_weight: bfloat16 [512, 512], replicated, may hold values from -0.25 to 0.25
- out_grad: bfloat16 [32768, 512], P(('emb', 'seq')), may hold values from -6 to 6
Outputs:
- layer_out: bfloat16 [32768, 512], P(('emb', 'seq'))
- table_grad: float32 [32768, 512], P(('emb', 'seq'))
- in_weight_grad: float32 [512, 2048], replicated
- out_weight_grad: float32 [512, 512], replicated
Inputs may be any that keep to these rules, and one draw needn't show every extreme that they name: `event_slot`: within each buffer of 1024 events every slot 0 to 511 is named by at least one event.
All inputs are finite; a program needn't handle non-finite values.
Results may differ from a plain program's by a relative error of at most 0.02.
Values may be sent and summed in bfloat16 or wider, within the bound.
No kernel may reach another device: no remote copies, remote signals or barrier semaphores. Data moves between devices by JAX's collectives and lax.ppermute only.
A program may use at most 192 MiB of HBM per device.

v0:
```python
import jax
import jax.numpy as jnp
from jax import lax
from jax.sharding import PartitionSpec as P

HEADS = 4
MOST = 512


EPS = 1e-05


def normalize(rows_in):
    center = rows_in - jnp.mean(rows_in, axis=-1, keepdims=True)
    spread = jnp.mean(center * center, axis=-1, keepdims=True)
    return center * lax.rsqrt(spread + EPS)


def hstu_layer(events, in_weight, out_weight, lengths_row):
    rows_count, model_width = events.shape
    head_size = model_width // HEADS
    normed = normalize(events.astype(jnp.float32)).astype(jnp.bfloat16)
    hidden = jax.nn.silu(jnp.dot(normed, in_weight, preferred_element_type=jnp.float32))
    update_gate = hidden[:, :model_width]
    values = (
        hidden[:, model_width : 2 * model_width]
        .astype(jnp.bfloat16)
        .reshape(rows_count, HEADS, head_size)
    )
    queries = (
        hidden[:, 2 * model_width : 3 * model_width]
        .astype(jnp.bfloat16)
        .reshape(rows_count, HEADS, head_size)
    )
    key_rows = (
        hidden[:, 3 * model_width :].astype(jnp.bfloat16).reshape(rows_count, HEADS, head_size)
    )
    scores = jnp.einsum(
        "ihd,jhd->hij", queries, key_rows, preferred_element_type=jnp.float32
    ) * head_size ** (-0.5)
    places = jnp.arange(rows_count, dtype=jnp.int32)
    seq_ends = jnp.cumsum(lengths_row)
    segment = jnp.sum((places[:, None] >= seq_ends[None, :]).astype(jnp.int32), axis=1)
    allowed = (segment[:, None] == segment[None, :]) & (places[None, :] <= places[:, None])
    weights = jnp.where(allowed[None], jax.nn.silu(scores) / MOST, 0.0).astype(jnp.bfloat16)
    attended = jnp.einsum(
        "hij,jhd->ihd", weights, values, preferred_element_type=jnp.float32
    ).reshape(rows_count, model_width)
    gated_rows = (normalize(attended) * update_gate).astype(jnp.bfloat16)
    return (
        jnp.dot(gated_rows, out_weight, preferred_element_type=jnp.float32)
        + events.astype(jnp.float32)
    ).astype(jnp.bfloat16)


def on_device(item_table, fetch_rows, event_slot, lengths, in_weight, out_weight, out_grad):
    emb_count = lax.axis_size("emb")
    seq_count = lax.axis_size("seq")
    model_width = item_table.shape[1]
    shard_rows = item_table.shape[0]
    requests = fetch_rows.reshape(emb_count, -1)
    slot_count = requests.shape[0] * requests.shape[1]
    asked_rows = lax.all_to_all(requests, "emb", split_axis=0, concat_axis=0, tiled=True)
    found = item_table[asked_rows]
    fetched, asked_rows = (
        lax.all_to_all(found, "emb", split_axis=0, concat_axis=0, tiled=True),
        asked_rows,
    )
    slot_table = fetched.reshape(slot_count, model_width)
    events = slot_table[event_slot]
    lengths_row = lengths[0]

    def forward(rows_x, first, second):
        return hstu_layer(rows_x, first, second, lengths_row)

    layer_out, pullback = jax.vjp(forward, events, in_weight, out_weight)
    row_grad, first_grad, second_grad = pullback(out_grad)
    slot_grad = jax.ops.segment_sum(
        row_grad.astype(jnp.float32), event_slot, num_segments=slot_count
    )
    returned = lax.all_to_all(
        slot_grad.reshape(emb_count, -1, model_width).astype(jnp.bfloat16),
        "emb",
        split_axis=0,
        concat_axis=0,
        tiled=True,
    ).astype(jnp.float32)
    quarter = shard_rows // seq_count
    shared, shared_rows = (
        lax.all_gather(returned.astype(jnp.bfloat16), "seq", axis=0, tiled=True).astype(
            returned.dtype
        ),
        lax.all_gather(asked_rows, "seq", axis=0, tiled=True),
    )
    local_rows = shared_rows.reshape(-1) - lax.axis_index("seq") * quarter
    inside = (local_rows >= 0) & (local_rows < quarter)
    target = jnp.where(inside, local_rows, quarter)
    table_grad = jax.ops.segment_sum(
        shared.reshape(-1, model_width), target, num_segments=quarter + 1
    )[:quarter]
    in_total, out_total = lax.psum(
        (first_grad.astype(jnp.float32), second_grad.astype(jnp.float32)), ("emb", "seq")
    )
    return (layer_out, table_grad, in_total, out_total)


def solution(mesh):
    placed = (
        P("emb", None),
        P("emb", "seq", None, None),
        P(("emb", "seq")),
        P(("emb", "seq"), None),
        P(),
        P(),
        P(("emb", "seq"), None),
    )
    return jax.shard_map(
        on_device,
        mesh=mesh,
        in_specs=placed,
        out_specs=(P(("emb", "seq"), None), P(("emb", "seq"), None), P(), P()),
        check_vma=False,
    )
```

profile of v0, /device:TPU:0, one launch (start us, length us, event | category | flops | bytes accessed | tf_op | source)
XLA Modules:
  0.0 345.3 jit_solution(15317950688414619498)
XLA Ops:
  8.0 13.8 %all_to_all.25 = s32[8,1,64]{2,1,0:T(1,128)S(1)} all-to-all(s32[8,1,64]{2,1,0:T(1,128)} %bitcast.80), channel_id=1, replica_groups=mesh['emb'=8,'seq'=4] {'emb'}, dimensions={0} | all-to-all | bytes 4096 | tf_op jit(solution)/shard_map/all_to_all | solution.py:63
  22.0 5.4 %gather_fusion = bf16[512,512]{1,0:T(8,128)(2,1)} fusion(bf16[4096,512]{1,0:T(8,128)(2,1)} %param.7, s32[1024]{0:T(1024)S(1)} %pad_clamp_fusion), kind=kCustom, calls=%fused_computation | custom fusion | bytes 1050624 | tf_op jit(solution)/shard_map/gather | solution.py:64
  27.3 3.5 %all-to-all-start.1 = ((bf16[8,64,512]{2,1,0:T(8,128)(2,1)}), bf16[8,64,512]{2,1,0:T(8,128)(2,1)S(1)}, u32[]{:S(2)}, u32[]{:S(2)}) async-start(bf16[8,64,512]{2,1,0:T(8,128)(2,1)} %bitcast.2), calls=%async_computation.1 | async-start | bytes 1048576 | tf_op jit(solution)/shard_map/all_to_all | solution.py:66
  32.8 11.3 %all-to-all-done.1 = bf16[8,64,512]{2,1,0:T(8,128)(2,1)S(1)} async-done(((bf16[8,64,512]{2,1,0:T(8,128)(2,1)}), bf16[8,64,512]{2,1,0:T(8,128)(2,1)S(1)}, u32[]{:S(2)}, u32[]{:S(2)}) %all-to-all-start.1) | async-done | bytes 524320 | tf_op jit(solution)/shard_map/all_to_all | solution.py:66
  44.1 5.6 %gather_fusion.1 = bf16[1024,512]{1,0:T(8,128)(2,1)} fusion(bf16[512,512]{1,0:T(8,128)(2,1)S(1)} %bitcast.63, s32[1024]{0:T(1024)S(1)} %fusion.37), kind=kCustom, calls=%fused_computation.1 | custom fusion | bytes 2101248 | tf_op jit(solution)/shard_map/gather | solution.py:70
  51.1 1.7 fusion.14
  52.8 8.6 %fusion.44 = (bf16[1024,2048]{1,0:T(8,128)(2,1)S(1)}, f32[1024,2048]{1,0:T(8,128)}, f32[1024,2048]{1,0:T(8,128)}) fusion(bf16[512,2048]{1,0:T(8,128)(2,1)S(1)} %copy-done, bf16[1024,512]{1,0:T(8,128)(2,1)} %gather_fusion.1, f32[1024]{0:T(1024)S(1)} %fusion.38, f32[1024]{0:T(1024)S(1)} %broadcast_multiply_fusion.1), kind=kOutput, calls=%fused_computation.87 | convolution fusion | flops 2160066560 | bytes 24125440 | tf_op jit(solution)/shard_map/jvp()/dot_general | solution.py:23
  63.2 2.3 copy.89
  66.8 11.8 %select_convert_fusion = (bf16[4,1024,1024]{2,1,0:T(8,128)(2,1)S(1)}, f32[4,1024,1024]{2,1,0:T(8,128)}) fusion(pred[1024,1024]{1,0:T(8,128)(4,1)} %fusion.8, bf16[1024,4,128]{0,2,1:T(8,128)(2,1)} %bitcast.72, bf16[1024,4,128]{0,2,1:T(8,128)(2,1)} %bitcast.74), kind=kOutput, calls=%fused_computation.8 | convolution fusion | flops 1107296256 | bytes 28311552 | tf_op jit(solution)/shard_map/jvp(ihd,jhd->hij)/dot_general | solution.py:38
  78.5 2.9 fusion.46
  83.3 2.9 copy.84
  86.2 3.4 multiply_reduce_fusion
  89.7 3.6 %fusion.43 = (f32[1024]{0:T(1024)S(1)}, f32[1024,512]{1,0:T(8,128)S(1)}, bf16[1024,512]{1,0:T(8,128)(2,1)}, f32[1024,512]{1,0:T(8,128)}) fusion(f32[1024]{0:T(1024)S(1)} %get-tuple-element.15, f32[1024,512]{1,0:T(8,128)S(1)} %copy-done.5, f32[1024]{0:T(1024)S(1)} %broadcast_multiply_fusion, f32[1024]{0:T(1024)S(1)} %get-tuple-element.16, ...), kind=kLoop, calls=%fused_computation.86 | loop fusion | flops 6290432 | bytes 10502144 | tf_op jit(solution)/shard_map/transpose(jvp())/reduce_sum | solution.py:14
  96.0 15.0 %fusion.2 = bf16[4,1024,1024]{2,1,0:T(8,128)(2,1)} fusion(f32[4,1024,1024]{2,1,0:T(8,128)} %get-tuple-element.19, pred[1024,1024]{1,0:T(8,128)(4,1)} %fusion.8, bf16[4,128,1024]{2,1,0:T(8,128)(2,1)S(1)} %bitcast.67, bf16[128,4,8,128]{3,2,1,0:T(8,128)(2,1)} %get-tuple-element.11), kind=kOutput, calls=%fused_computation.7 | convolution fusion | flops 1136656384 | bytes 28311552 | tf_op jit(solution)/shard_map/transpose(jvp(hij,jhd->ihd))/dot_general | solution.py:46
  111.0 5.8 %fusion.49 = bf16[4,1024,128]{1,2,0:T(8,128)(2,1)} fusion(bf16[4,1024,1024]{2,1,0:T(8,128)(2,1)} %fusion.2, bf16[1024,4,128]{0,2,1:T(8,128)(2,1)S(1)} %bitcast.73), kind=kOutput, calls=%fused_computation.91 | convolution fusion | flops 1073741824 | bytes 10485760 | tf_op jit(solution)/shard_map/transpose(jvp(ihd,jhd->hij))/dot_general | solution.py:38
  116.8 7.5 %fusion.48 = bf16[4,1024,128]{1,2,0:T(8,128)(2,1)} fusion(bf16[4,1024,1024]{2,1,0:T(8,128)(2,1)} %fusion.2, bf16[1024,4,128]{0,2,1:T(8,128)(2,1)S(1)} %bitcast.75), kind=kOutput, calls=%fused_computation.90 | convolution fusion | flops 1073741824 | bytes 10485760 | tf_op jit(solution)/shard_map/transpose(jvp(ihd,jhd->hij))/dot_general | solution.py:38
  124.4 2.3 fusion.47
  126.7 2.4 copy.86
  129.1 2.3 copy.87
  132.7 7.2 %fusion.4 = bf16[1024,2048]{1,0:T(8,128)(2,1)S(1)} fusion(f32[1024,2048]{1,0:T(8,128)} %get-tuple-element.17, f32[1024,512]{1,0:T(8,128)} %get-tuple-element.14, bf16[1024,512]{1,0:T(8,128)(2,1)} %copy.88, bf16[1024,512]{1,0:T(8,128)(2,1)} %copy.87, bf16[1024,512]{1,0:T(8,128)(2,1)} %copy.86), kind=kLoop, calls=%fused_computation.12 | loop fusion | flops 33554432 | bytes 17825792 | tf_op jit(solution)/shard_map/transpose(jvp(jit(silu)))/add_any | solution.py:23
  139.9 2.5 fusion.16
  144.3 9.1 %scatter_custom_fusion = f32[512,512]{1,0:T(8,128)} fusion(s32[1024]{0:T(1024)S(1)} %copy-done.14, bf16[1024,512]{1,0:T(8,128)(2,1)} %param.13, bf16[1024,512]{1,0:T(8,128)(2,1)S(1)} %copy-done.1, bf16[1024,512]{1,0:T(8,128)(2,1)} %copy-done.7, f32[1024]{0:T(1024)S(1)} %negate_multiply_fusion, f32[1024]{0:T(1024)S(1)} %multiply_multiply_fusion, ...), kind=kCustom, calls=%fused_computation.40 | custom fusion | flops 6291456 | bytes 4210692 | tf_op jit(solution)/shard_map/scatter-add | solution.py:78
  154.7 17.4 %all_to_all.26 = bf16[8,64,512]{2,1,0:T(8,128)(2,1)} all-to-all(bf16[8,64,512]{2,1,0:T(8,128)(2,1)S(1)} %bitcast.70), channel_id=1, replica_groups=mesh['emb'=8,'seq'=4] {'emb'}, dimensions={0} | all-to-all | bytes 1048576 | tf_op jit(solution)/shard_map/all_to_all | solution.py:81
  172.2 3.4 fusion.23
  175.6 4.6 %fusion.13 = f32[512,2048]{1,0:T(8,128)} fusion(bf16[1024,2048]{1,0:T(8,128)(2,1)S(1)} %copy-done.4, bf16[1024,512]{1,0:T(8,128)(2,1)S(1)} %copy-done.1, f32[1024]{0:T(1024)S(1)} %fusion.38, f32[1024]{0:T(1024)S(1)} %broadcast_multiply_fusion.1), kind=kOutput, calls=%fused_computation.29 | convolution fusion | flops 2150629376 | bytes 9445376 | tf_op jit(solution)/shard_map/transpose(jvp())/dot_general | solution.py:23
  180.2 5.4 %all-gather = s32[32,1,64]{2,1,0:T(1,128)S(1)} all-gather(s32[8,1,64]{2,1,0:T(1,128)S(1)} %all_to_all.25), channel_id=2, replica_groups=mesh['emb'=8,'seq'=4] {'seq'}, dimensions={0}, use_global_device_ids=true | all-gather | bytes 10240 | tf_op jit(solution)/shard_map/all_gather | solution.py:93
  185.8 3.1 fusion.17
  188.8 5.5 %all-gather.3.cloned.1.call-done = bf16[32,64,512]{2,1,0:T(8,128)(2,1)} async-done(((bf16[8,64,512]{2,1,0:T(8,128)(2,1)}), bf16[32,64,512]{2,1,0:T(8,128)(2,1)}) %all-gather.3.cloned.1.call-update) | async-done | bytes 2097168 | tf_op jit(solution)/shard_map/all_gather | solution.py:90
  194.3 15.0 %scatter_custom_fusion.1 = f32[1025,512]{1,0:T(8,128)} fusion(s32[2048]{0:T(1024)S(1)} %bitcast.79, bf16[2048,512]{1,0:T(8,128)(2,1)} %bitcast.71, f32[]{:T(128)} %constant.22.clone.1), kind=kCustom, calls=%fused_computation.15 | custom fusion | flops 2097152 | bytes 4196356 | tf_op jit(solution)/shard_map/scatter-add | solution.py:98
  209.3 3.1 slice.31
  212.5 119.4 %all-reduce.7.cloned.1.call-done = (f32[512,2048]{1,0:T(8,128)}, f32[512,512]{1,0:T(8,128)}) async-done(((f32[512,2048]{1,0:T(8,128)}, f32[512,512]{1,0:T(8,128)}), (f32[512,2048]{1,0:T(8,128)}, f32[512,512]{1,0:T(8,128)})) %all-reduce.7.cloned.1.call-update) | async-done | bytes 5242896 | tf_op jit(solution)/shard_map/psum | solution.py:101
  331.8 4.8 %copy.104 = f32[512,2048]{1,0:T(8,128)} copy(f32[512,2048]{1,0:T(8,128)} %get-tuple-element.28) | data formatting | bytes 8388608
  (68 shorter events, 16.8 us)
Async XLA Ops:
  8.0 44.8 %copy-start = (bf16[512,2048]{1,0:T(8,128)(2,1)S(1)}, bf16[512,2048]{1,0:T(8,128)(2,1)}, u32[]{:S(2)}) copy-start(bf16[512,2048]{1,0:T(8,128)(2,1)} %param.11) | copy-start | bytes 6291460
  8.0 22.9 %copy-start.15 = (s32[1,8]{1,0:T(1,128)S(1)}, s32[1,8]{1,0:T(1,128)}, u32[]{:S(2)}) copy-start(s32[1,8]{1,0:T(1,128)} %param.10) | copy-start | bytes 100
  8.0 23.2 %copy-start.14 = (s32[1024]{0:T(1024)S(1)}, s32[1024]{0:T(1024)}, u32[]{:S(2)}) copy-start(s32[1024]{0:T(1024)} %param.9) | copy-start | bytes 12292
  27.3 16.8 %all-to-all-start.1 = ((bf16[8,64,512]{2,1,0:T(8,128)(2,1)}), bf16[8,64,512]{2,1,0:T(8,128)(2,1)S(1)}, u32[]{:S(2)}, u32[]{:S(2)}) async-start(bf16[8,64,512]{2,1,0:T(8,128)(2,1)} %bitcast.2), calls=%async_computation.1 | async-start | bytes 1048576 | tf_op jit(solution)/shard_map/all_to_all | solution.py:66
  30.8 163.5 %all-gather.3.cloned.1.call-start = ((), (), s32[]{:S(2)}) async-start(), calls=%async_computation.3 | async-start | bytes 2621440 | tf_op jit(solution)/shard_map/all_gather | solution.py:90
  66.8 11.8 %copy-start.10 = (bf16[128,4,8,128]{3,2,1,0:T(8,128)(2,1)S(1)}, bf16[128,4,8,128]{3,2,1,0:T(8,128)(2,1)}, u32[]{:S(2)}) copy-start(bf16[128,4,8,128]{3,2,1,0:T(8,128)(2,1)} %get-tuple-element.11) | copy-start | bytes 3145732
  78.5 3.2 copy-start.2
  81.7 1.3 copy-start.6
  81.7 4.5 %copy-start.9 = (bf16[1024,512]{1,0:T(8,128)(2,1)S(1)}, bf16[1024,512]{1,0:T(8,128)(2,1)}, u32[]{:S(2)}) copy-start(bf16[1024,512]{1,0:T(8,128)(2,1)} %param.13) | copy-start | bytes 3145732
  86.2 3.4 copy-start.5
  96.0 15.0 %copy-start.11 = (bf16[1024,512]{0,1:T(8,128)(2,1)S(1)}, bf16[1024,512]{0,1:T(8,128)(2,1)}, u32[]{:S(2)}) copy-start(bf16[1024,512]{0,1:T(8,128)(2,1)} %copy.89) | copy-start | bytes 3145732
  111.0 5.8 %copy-start.12 = (bf16[1024,512]{0,1:T(8,128)(2,1)S(1)}, bf16[1024,512]{0,1:T(8,128)(2,1)}, u32[]{:S(2)}) copy-start(bf16[1024,512]{0,1:T(8,128)(2,1)} %copy.90) | copy-start | bytes 3145732
  111.0 13.3 %slice-start = ((s8[8388608]{0:T(1024)(128)(4,1)}), s8[4194304]{0:T(1024)(128)(4,1)S(1)}, s32[]{:S(2)}) async-start(s8[8388608]{0:T(1024)(128)(4,1)} %bitcast.64), calls=%async_computation.5 | async-start | bytes 8388608
  116.8 7.5 %slice-start.1 = ((s8[8388608]{0:T(1024)(128)(4,1)}), s8[4194304]{0:T(1024)(128)(4,1)S(1)}, s32[]{:S(2)}) async-start(s8[8388608]{0:T(1024)(128)(4,1)} %bitcast.64), calls=%async_computation.6 | async-start | bytes 8388608
  126.7 4.7 %copy-start.8 = (bf16[4,128,1024]{2,1,0:T(8,128)(2,1)S(1)}, bf16[4,128,1024]{2,1,0:T(8,128)(2,1)}, u32[]{:S(2)}) copy-start(bf16[4,128,1024]{2,1,0:T(8,128)(2,1)} %fusion.47) | copy-start | bytes 3145732
  132.7 7.2 %copy-start.1 = (bf16[1024,512]{1,0:T(8,128)(2,1)S(1)}, bf16[1024,512]{1,0:T(8,128)(2,1)}, u32[]{:S(2)}) copy-start(bf16[1024,512]{1,0:T(8,128)(2,1)} %gather_fusion.1) | copy-start | bytes 3145732
  139.8 2.5 copy-start.3
  142.3 1.0 copy-start.7
  172.1 159.7 %all-reduce.7.cloned.1.call-start = ((), (), s32[]{:S(2)}) async-start(), calls=%async_computation.4 | async-start | bytes 10485760 | tf_op jit(solution)/shard_map/psum | solution.py:101
  172.1 3.4 copy-start.4
  331.8 4.8 %copy-start.13 = (f32[512,512]{1,0:T(8,128)S(1)}, f32[512,512]{1,0:T(8,128)}, u32[]{:S(2)}) copy-start(f32[512,512]{1,0:T(8,128)} %get-tuple-element.29) | copy-start | bytes 3145732
Sparse Core Ops, SparseCore 0:
  172.2 22.0 all-gather.2
Sparse Core Ops, SparseCore 1:
  180.3 151.5 all-reduce.6
where the time goes:
time: 348 us; the launch traced here: 345 us
  waiting for transfers between devices  136 us (39%)
  matrix products  70.9 us (20%)
  other arithmetic  43.8 us (13%)
  local copies, waits for them, and re-layouts  38.2 us (11%)
  blocking collectives  36.6 us (11%)
  between operations  16 us (5%)
  starting transfers between devices  3.58 us (1%)
    psum x1, waiting for transfers between devices, on_device(): lax.psum((first_grad.astype(jnp.float32), second_grad.astype(jnp.float32)...  119 us
    dot_general x3, matrix products, hstu_layer(): jnp.einsum('ihd,jhd->hij', queries, key_rows, preferred_element_type=jnp....  25.1 us
    dot_general x3, matrix products, hstu_layer(): jnp.einsum('hij,jhd->ihd', weights, values, preferred_element_type=jnp.fl...  20.2 us
    all_to_all x1, blocking collectives, on_device(): lax.all_to_all(slot_grad.reshape(emb_count, -1, model_width).astype(jnp.b...  17.4 us
    dot_general x3, matrix products, hstu_layer(): jnp.dot(normed, in_weight, preferred_element_type=jnp.float32)  15.7 us
    scatter-add x1, other arithmetic, on_device(): jax.ops.segment_sum(shared.reshape(-1, model_width), target, num_segments...  15 us
    all_to_all x1, blocking collectives, on_device(): lax.all_to_all(requests, 'emb', split_axis=0, concat_axis=0, tiled=True)  13.8 us
    all_to_all x1, waiting for transfers between devices, on_device(): lax.all_to_all(found, 'emb', split_axis=0, concat_axis=0, tiled=True)  11.3 us
  transfers between devices with their start and end apart: 3, of which 3 were waited for; matrix products, arithmetic and copies ran while one was open for 9% of the time, Pallas kernels for 0%

commit v1 on v0

v1 whole, which is shorter than its diff:
```python
import functools

import jax
import jax.numpy as jnp
from jax import lax
from jax.experimental import pallas as pl
from jax.experimental.pallas import tpu as pltpu
from jax.sharding import PartitionSpec as P

HEADS = 4
MOST = 512
EPS = 1e-05
BLOCK = 256
VMEM = pl.BlockSpec(memory_space=pltpu.VMEM)
SMEM = pl.BlockSpec(memory_space=pltpu.SMEM)
BF = jnp.bfloat16
F32 = jnp.float32


def mm(a, b):
    return jnp.dot(a, b, preferred_element_type=F32)


def mm_t(a, b):
    return lax.dot_general(a, b, (((1,), (1,)), ((), ())), preferred_element_type=F32)


def tt_mm(a, b):
    return lax.dot_general(a, b, (((0,), (0,)), ((), ())), preferred_element_type=F32)


def center_rows(x):
    center = x - jnp.mean(x, axis=-1, keepdims=True)
    spread = jnp.mean(center * center, axis=-1, keepdims=True)
    inverse = lax.rsqrt(spread + EPS)
    return center * inverse, inverse


def center_back(grad, normed, inverse):
    along = jnp.mean(grad * normed, axis=-1, keepdims=True)
    return inverse * (grad - jnp.mean(grad, axis=-1, keepdims=True) - normed * along)


def history_ends(len_ref):
    ends, total = [], 0
    for k in range(len_ref.shape[1]):
        total = total + len_ref[0, k]
        ends.append(total)
    return ends


def history_start(ends, place):
    start = jnp.zeros_like(place)
    for end in ends:
        start = jnp.maximum(start, jnp.where(place >= end, end, 0))
    return start


def first_kernel(
    len_ref, slot_row, slot_col, rows_ref, win_ref, wout_ref, og_ref,
    out_ref, vqk_ref, datt_ref, dsil_ref, nt_ref, wg_ref, dn_ref, res_ref,
    hid, gate, ev, att, gated, dgate,
):
    slots, width = rows_ref.shape
    tokens = og_ref.shape[0]
    head = width // HEADS
    half_scale = 0.5 * head**-0.5
    normed, _ = center_rows(rows_ref[...].astype(F32))
    normed = normed.astype(BF)
    nt_ref[...] = normed.T
    for j in range(4):
        cols = slice(j * width, (j + 1) * width)
        pre = mm(normed, win_ref[:, cols])
        sig = 0.5 + 0.5 * jnp.tanh(0.5 * pre)
        act = pre * sig
        hid[:, cols] = act.astype(BF)
        dsil_ref[:, cols] = (sig + act * (1.0 - sig)).astype(BF)

    def spread(i, _):
        span = pl.ds(pl.multiple_of(i * BLOCK, BLOCK), BLOCK)
        lane = lax.broadcasted_iota(jnp.int32, (BLOCK, slots), 1)
        pick = jnp.where(slot_col[span, :] == lane, 1.0, 0.0).astype(BF)
        ev[span, :] = mm(pick, rows_ref[...]).astype(BF)
        gate[span, :] = mm(pick, hid[:, :width]).astype(BF)
        for j in range(3):
            vqk_ref[span, j * width : (j + 1) * width] = mm(
                pick, hid[:, (j + 1) * width : (j + 2) * width]
            ).astype(BF)
        return 0

    lax.fori_loop(0, tokens // BLOCK, spread, 0)
    ends = history_ends(len_ref)

    def rows_step(i, _):
        base = pl.multiple_of(i * BLOCK, BLOCK)
        span = pl.ds(base, BLOCK)
        start = history_start(ends, base + lax.broadcasted_iota(jnp.int32, (BLOCK, 1), 0))
        place = base + lax.broadcasted_iota(jnp.int32, (BLOCK, BLOCK), 0)
        att[...] = jnp.zeros_like(att)

        def keys_step(j, _):
            key_base = pl.multiple_of(j * BLOCK, BLOCK)
            keys = pl.ds(key_base, BLOCK)
            other = key_base + lax.broadcasted_iota(jnp.int32, (BLOCK, BLOCK), 1)
            allowed = (other >= start) & (other <= place)
            for h in range(HEADS):
                lo = h * head
                q = vqk_ref[span, width + lo : width + lo + head]
                k = vqk_ref[keys, 2 * width + lo : 2 * width + lo + head]
                v = vqk_ref[keys, lo : lo + head]
                u = mm_t(q, k) * half_scale
                w = jnp.where(allowed, u + u * jnp.tanh(u), 0.0).astype(BF)
                att[:, lo : lo + head] += mm(w, v)
            return 0

        lax.fori_loop(history_start(ends, base) // BLOCK, i + 1, keys_step, 0)
        normed_att, inverse = center_rows(att[...] * (1.0 / MOST))
        g = gate[span, :].astype(F32)
        gated_rows = (normed_att * g).astype(BF)
        gated[span, :] = gated_rows
        out_ref[span, :] = (mm(gated_rows, wout_ref[...]) + ev[span, :].astype(F32)).astype(BF)
        dgated = mm_t(og_ref[span, :], wout_ref[...])
        dgate[span, :] = (dgated * normed_att).astype(BF)
        datt = center_back(dgated * g, normed_att, inverse)
        datt_ref[span, :] = (datt * (1.0 / MOST)).astype(BF)
        return 0

    lax.fori_loop(0, tokens // BLOCK, rows_step, 0)
    wg_ref[:width, :] = tt_mm(gated[...], og_ref[...]).astype(BF)
    put = jnp.where(
        slot_row[...] == lax.broadcasted_iota(jnp.int32, (slots, tokens), 0), 1.0, 0.0
    ).astype(BF)
    dpre = (mm(put, dgate[...]) * dsil_ref[:, :width].astype(F32)).astype(BF)
    wg_ref[width:, :] = mm(nt_ref[...], dpre).astype(BF)
    dn_ref[...] = mm_t(dpre, win_ref[:, :width])
    res_ref[...] = mm(put, og_ref[...])


def second_kernel(
    len_ref, slot_row, rows_ref, vqk_ref, datt_ref, dsil_ref, win_ref, dn_ref, res_ref,
    dpre_ref, grad_ref, dvqk,
):
    slots, width = rows_ref.shape
    tokens = datt_ref.shape[0]
    head = width // HEADS
    half_scale = 0.5 * head**-0.5
    ends = history_ends(len_ref)
    dvqk[...] = jnp.zeros_like(dvqk)

    def rows_step(i, _):
        base = pl.multiple_of(i * BLOCK, BLOCK)
        span = pl.ds(base, BLOCK)
        start = history_start(ends, base + lax.broadcasted_iota(jnp.int32, (1, BLOCK), 1))
        place = base + lax.broadcasted_iota(jnp.int32, (BLOCK, BLOCK), 1)

        def keys_step(j, _):
            key_base = pl.multiple_of(j * BLOCK, BLOCK)
            keys = pl.ds(key_base, BLOCK)
            other = key_base + lax.broadcasted_iota(jnp.int32, (BLOCK, BLOCK), 0)
            allowed = (other >= start) & (other <= place)
            for h in range(HEADS):
                lo = h * head
                vs = slice(lo, lo + head)
                qs = slice(width + lo, width + lo + head)
                ks = slice(2 * width + lo, 2 * width + lo + head)
                q, k, v = vqk_ref[span, qs], vqk_ref[keys, ks], vqk_ref[keys, vs]
                da = datt_ref[span, vs]
                u = mm_t(k, q) * half_scale
                th = jnp.tanh(u)
                w = jnp.where(allowed, u + u * th, 0.0).astype(BF)
                slope = (half_scale + half_scale * th) * (1.0 + u - u * th)
                ds = jnp.where(allowed, mm_t(v, da) * slope, 0.0).astype(BF)
                dvqk[keys, vs] += mm(w, da)
                dvqk[keys, ks] += mm(ds, q)
                dvqk[span, qs] += tt_mm(ds, k)
            return 0

        lax.fori_loop(history_start(ends, base) // BLOCK, i + 1, keys_step, 0)
        return 0

    lax.fori_loop(0, tokens // BLOCK, rows_step, 0)
    put = jnp.where(
        slot_row[...] == lax.broadcasted_iota(jnp.int32, (slots, tokens), 0), 1.0, 0.0
    ).astype(BF)
    dn = dn_ref[...]
    for j in range(3):
        cols = slice(j * width, (j + 1) * width)
        later = slice((j + 1) * width, (j + 2) * width)
        dpre = (mm(put, dvqk[:, cols].astype(BF)) * dsil_ref[:, later].astype(F32)).astype(BF)
        dpre_ref[:, cols] = dpre
        dn = dn + mm_t(dpre, win_ref[:, later])
    normed, inverse = center_rows(rows_ref[...].astype(F32))
    grad_ref[...] = (center_back(dn, normed, inverse) + res_ref[...]).astype(BF)


def third_kernel(nt_ref, dpre_ref, wg_ref):
    wg_ref[...] = mm(nt_ref[...], dpre_ref[...]).astype(BF)


def table_kernel(count, *refs):
    places, rows, out = refs[:count], refs[count : 2 * count], refs[-1]
    height = min(BLOCK, out.shape[0])

    def step(i, _):
        base = pl.multiple_of(i * height, height)
        total = None
        for place, row in zip(places, rows):
            at = base + lax.broadcasted_iota(jnp.int32, (height, place.shape[1]), 0)
            put = jnp.where(place[...] == at, 1.0, 0.0).astype(BF)
            part = mm(put, row[...])
            total = part if total is None else total + part
        out[pl.ds(base, height), :] = total
        return 0

    lax.fori_loop(0, out.shape[0] // height, step, 0)


def call(kernel, outs, scratch, specs, flops):
    return pl.pallas_call(
        kernel,
        out_shape=[jax.ShapeDtypeStruct(s, d) for s, d in outs],
        in_specs=specs,
        out_specs=[VMEM] * len(outs),
        scratch_shapes=[pltpu.VMEM(s, d) for s, d in scratch],
        compiler_params=pltpu.CompilerParams(vmem_limit_bytes=56 * 2**20),
        cost_estimate=pl.CostEstimate(flops=flops, bytes_accessed=10**7, transcendentals=0),
    )


AXES = ("emb", "seq")


def swap(x, seq_count, total, partner):
    return lax.ppermute(x, AXES, [(d, partner(d)) for d in range(total)])


def reduce_plan(emb_count, seq_count):
    total = emb_count * seq_count
    seq_bits = seq_count.bit_length() - 1
    emb_bits = emb_count.bit_length() - 1
    me = lax.axis_index("emb") * seq_count + lax.axis_index("seq")
    bit = lambda d, b: (d >> b) & 1
    pair = lambda b: (lambda d: d ^ (1 << b), bit(me, b))
    plan = []
    first = 0 if seq_bits else None
    plan.append(pair(0))
    a, b = seq_bits, 1
    plan.append(
        (lambda d: d ^ (1 << a if bit(d, 0) == 0 else 1 << b), jnp.where(bit(me, 0) == 0, bit(me, a), bit(me, b)))
    )
    plan.append(
        (lambda d: d ^ (1 << b if bit(d, 0) == 0 else 1 << a), jnp.where(bit(me, 0) == 0, bit(me, b), bit(me, a)))
    )
    rest = [k for k in range(1, seq_bits + emb_bits) if k not in (a, b)]
    return plan, rest, me, total


def weight_sum(x, emb_count, seq_count):
    plan, rest, me, total = reduce_plan(emb_count, seq_count)
    columns = x.shape[1]
    for partner, place in plan:
        halves = x.reshape(2, x.shape[0] // 2, columns)
        keep = lax.dynamic_index_in_dim(halves, place, 0, keepdims=False)
        give = lax.dynamic_index_in_dim(halves, 1 - place, 0, keepdims=False)
        got = swap(give, seq_count, total, partner)
        x = (keep.astype(F32) + got.astype(F32)).astype(BF)
    count = 1 << len(rest)
    spread = lambda m: sum(((m >> i) & 1) << b for i, b in enumerate(rest))
    place = sum(((me >> b) & 1) << i for i, b in enumerate(rest))
    parts = x.reshape(count, x.shape[0] // count, columns)
    total_x = lax.dynamic_index_in_dim(parts, place, 0, keepdims=False).astype(F32)
    for m in range(1, count):
        give = lax.dynamic_index_in_dim(parts, place ^ m, 0, keepdims=False)
        total_x = total_x + swap(give, seq_count, total, lambda d: d ^ spread(m)).astype(F32)
    x = total_x.astype(BF)
    whole = jnp.zeros((count,) + x.shape, BF)
    whole = lax.dynamic_update_index_in_dim(whole, x, place, 0)
    for m in range(1, count):
        whole = lax.dynamic_update_index_in_dim(
            whole, swap(x, seq_count, total, lambda d: d ^ spread(m)), place ^ m, 0
        )
    x = whole.reshape(-1, columns)
    for partner, place in plan[::-1]:
        got = swap(x, seq_count, total, partner)
        whole = jnp.zeros((2,) + x.shape, BF)
        whole = lax.dynamic_update_index_in_dim(whole, x, place, 0)
        whole = lax.dynamic_update_index_in_dim(whole, got, 1 - place, 0)
        x = whole.reshape(-1, columns)
    return x.astype(F32)


def on_device(item_table, fetch_rows, event_slot, lengths, in_weight, out_weight, out_grad):
    emb_count = lax.axis_size("emb")
    seq_count = lax.axis_size("seq")
    shard_rows, width = item_table.shape
    requests = fetch_rows.reshape(emb_count, -1)
    slots = requests.shape[0] * requests.shape[1]
    tokens = event_slot.shape[0]
    asked = lax.all_to_all(requests, "emb", split_axis=0, concat_axis=0, tiled=True)
    found = item_table[asked]
    fetched = lax.all_to_all(found, "emb", split_axis=0, concat_axis=0, tiled=True)
    rows = fetched.reshape(slots, width)
    slot_row, slot_col = event_slot.reshape(1, tokens), event_slot.reshape(tokens, 1)

    layer_out, vqk, datt, dsil, nt, wg1, dn, res = call(
        first_kernel,
        [
            ((tokens, width), BF), ((tokens, 3 * width), BF), ((tokens, width), BF), ((slots, 4 * width), BF),
            ((width, slots), BF), ((2 * width, width), BF), ((slots, width), F32), ((slots, width), F32),
        ],
        [
            ((slots, 4 * width), BF), ((tokens, width), BF), ((tokens, width), BF), ((BLOCK, width), F32),
            ((tokens, width), BF), ((tokens, width), BF),
        ],
        [SMEM] + [VMEM] * 6,
        10**10,
    )(lengths, slot_row, slot_col, rows, in_weight, out_weight, out_grad)
    wg1 = weight_sum(wg1, emb_count, seq_count)

    dpre, slot_grad = call(
        second_kernel,
        [((slots, 3 * width), BF), ((slots, width), BF)],
        [((tokens, 3 * width), F32)],
        [SMEM] + [VMEM] * 8,
        10**10,
    )(lengths, slot_row, rows, vqk, datt, dsil, in_weight, dn, res)
    (wg2,) = call(third_kernel, [((width, 3 * width), BF)], [], [VMEM] * 2, 10**9)(nt, dpre)
    wg2 = weight_sum(wg2, emb_count, seq_count)

    returned = lax.all_to_all(
        slot_grad.reshape(emb_count, -1, width), "emb", split_axis=0, concat_axis=0, tiled=True
    )
    arrays, places = [returned.reshape(slots, width)], [asked.reshape(1, slots)]
    for b in reversed(range(seq_count.bit_length() - 1)):
        other = [(s, s ^ (1 << b)) for s in range(seq_count)]
        places += [lax.ppermute(p, "seq", other) for p in places]
        arrays += [lax.ppermute(a, "seq", other) for a in arrays]
    quarter = shard_rows // seq_count
    base = lax.axis_index("seq") * quarter
    places = [p - base for p in places]
    (table_grad,) = call(
        functools.partial(table_kernel, len(places)),
        [((quarter, width), F32)],
        [],
        [VMEM] * (2 * len(places)),
        10**9,
    )(*places, *arrays)
    in_total = jnp.concatenate([wg1[width:], wg2], axis=1)
    return layer_out, table_grad, in_total, wg1[:width]


def solution(mesh):
    placed = (
        P("emb", None),
        P("emb", "seq", None, None),
        P(("emb", "seq")),
        P(("emb", "seq"), None),
        P(),
        P(),
        P(("emb", "seq"), None),
    )
    return jax.shard_map(
        on_device,
        mesh=mesh,
        in_specs=placed,
        out_specs=(P(("emb", "seq"), None), P(("emb", "seq"), None), P(), P()),
        check_vma=False,
    )
```

time: 348 us -> 175 us (0.50)
  waiting for transfers between devices: 136 us -> 44.3 us
  matrix products: 70.9 us -> 0 us
  Pallas kernels: 0 us -> 50.9 us
  starting transfers between devices: 3.58 us -> 41.8 us
  other arithmetic: 43.8 us -> 7.99 us
  local copies, waits for them, and re-layouts: 38.2 us -> 14.8 us
  blocking collectives: 36.6 us -> 13.7 us
  between operations: 16 us -> 1.05 us
    psum x1 -> x0, waiting for transfers between devices: 119 us -> none  [on_device(): lax.psum((first_grad.astype(jnp.float32), second_grad.astype(jnp.float32)...]
    dot_general x12 -> x0, matrix products: 70.9 us -> none  [the longest x3 25.1 us: hstu_layer(): jnp.einsum('ihd,jhd->hij', queries, key_rows, preferred_element_type=jnp....]
    pallas_call x0 -> x4, Pallas kernels: none -> 50.9 us  [the longest x1 21 us: on_device(): call(first_kernel, [((tokens, width), BF), ((tokens, 3 * width), BF), ((t...]
    ppermute x0 -> x30, waiting for transfers between devices: none -> 38.2 us  [the longest x24 36.7 us: swap(): return lax.ppermute(x, AXES, [(d, partner(d)) for d in range(total)])]
    ppermute x0 -> x30, starting transfers between devices: none -> 34.6 us  [the longest x24 31.7 us: swap(): return lax.ppermute(x, AXES, [(d, partner(d)) for d in range(total)])]
    scatter-add x2 -> x0, other arithmetic: 24.1 us -> none  [the longest x1 15 us: on_device(): jax.ops.segment_sum(shared.reshape(-1, model_width), target, num_segments...]
    all_to_all x1 -> x0, blocking collectives: 17.4 us -> none  [on_device(): lax.all_to_all(slot_grad.reshape(emb_count, -1, model_width).astype(jnp.b...]
    add_any x2 -> x0, other arithmetic: 8.34 us -> none  [the longest x1 7.17 us: hstu_layer(): jax.nn.silu(jnp.dot(normed, in_weight, preferred_element_type=jnp.float32))]
  transfers between devices with their start and end apart: 3 -> 32, of which waited for: 3 -> 14; matrix products, arithmetic and copies ran while one was open for 9% -> 7% of each run, Pallas kernels for 0% -> 29%
where the time goes in v1:
time: 175 us
  Pallas kernels  50.9 us (29%)
  waiting for transfers between devices  44.3 us (25%)
  starting transfers between devices  41.8 us (24%)
  local copies, waits for them, and re-layouts  14.8 us (8%)
  blocking collectives  13.7 us (8%)
  other arithmetic  7.99 us (5%)
    ppermute x24, waiting for transfers between devices, swap(): return lax.ppermute(x, AXES, [(d, partner(d)) for d in range(total)])  36.7 us
    ppermute x24, starting transfers between devices, swap(): return lax.ppermute(x, AXES, [(d, partner(d)) for d in range(total)])  31.7 us
    pallas_call x1, Pallas kernels, on_device(): call(first_kernel, [((tokens, width), BF), ((tokens, 3 * width), BF), ((t...  21 us
    pallas_call x1, Pallas kernels, on_device(): call(second_kernel, [((slots, 3 * width), BF), ((slots, width), BF)], [((...  20.5 us
    all_to_all x1, blocking collectives, on_device(): lax.all_to_all(requests, 'emb', split_axis=0, concat_axis=0, tiled=True)  13.7 us
    all_to_all x1, waiting for transfers between devices, on_device(): lax.all_to_all(found, 'emb', split_axis=0, concat_axis=0, tiled=True)  6.13 us
    pallas_call x1, Pallas kernels, on_device(): call(functools.partial(table_kernel, len(places)), [((quarter, width), F3...  5.68 us
    gather x1, local copies, waits for them, and re-layouts, on_device(): found = item_table[asked]  5.39 us
  transfers between devices with their start and end apart: 32, of which 14 were waited for; matrix products, arithmetic and copies ran while one was open for 7% of the time, Pallas kernels for 29%

profile of v1, /device:TPU:0, one launch (start us, length us, event | category | flops | bytes accessed | tf_op | source)
XLA Modules:
  0.0 174.6 jit_solution(2144547539966506846)
XLA Ops:
  0.6 13.7 %all_to_all.22 = s32[8,1,64]{2,1,0:T(1,128)S(1)} all-to-all(s32[8,1,64]{2,1,0:T(1,128)} %bitcast.164), channel_id=1, replica_groups=mesh['emb'=8,'seq'=4] {'emb'}, dimensions={0} | all-to-all | bytes 4096 | tf_op jit(solution)/shard_map/all_to_all | solution.py:299
  14.4 5.4 %gather_fusion = bf16[512,512]{1,0:T(8,128)(2,1)} fusion(bf16[4096,512]{1,0:T(8,128)(2,1)} %param.7, s32[1024]{0:T(1024)S(1)} %pad_clamp_fusion), kind=kCustom, calls=%fused_computation | custom fusion | bytes 1050624 | tf_op jit(solution)/shard_map/gather | solution.py:300
  19.8 3.5 %all-to-all-start.1 = ((bf16[8,64,512]{2,1,0:T(8,128)(2,1)}), bf16[8,64,512]{2,1,0:T(8,128)(2,1)S(1)}, u32[]{:S(2)}, u32[]{:S(2)}) async-start(bf16[8,64,512]{2,1,0:T(8,128)(2,1)} %bitcast.4), calls=%async_computation.1 | async-start | bytes 1048576 | tf_op jit(solution)/shard_map/all_to_all | solution.py:301
  25.7 1.5 collective-permute-start
  27.8 1.5 collective-permute-done
  30.4 6.1 %all-to-all-done.1 = bf16[8,64,512]{2,1,0:T(8,128)(2,1)S(1)} async-done(((bf16[8,64,512]{2,1,0:T(8,128)(2,1)}), bf16[8,64,512]{2,1,0:T(8,128)(2,1)S(1)}, u32[]{:S(2)}, u32[]{:S(2)}) %all-to-all-start.1) | async-done | bytes 524320 | tf_op jit(solution)/shard_map/all_to_all | solution.py:301
  37.4 21.0 %shard_map.102 = (bf16[1024,512]{1,0:T(8,128)(2,1)}, bf16[1024,1536]{1,0:T(8,128)(2,1)}, bf16[1024,512]{1,0:T(8,128)(2,1)}, bf16[512,2048]{1,0:T(8,128)(2,1)}, b...) custom-call(s32[1,8]{1,0:T(1,128)} %len_ref.3, ...), custom_call_target="tpu_custom_call" | custom-call | flops 10000000000 | bytes 10000000 | tf_op jit(solution)/shard_map/pallas_call | solution.py:305
  59.6 20.5 %shard_map.103 = (bf16[512,1536]{1,0:T(8,128)(2,1)}, bf16[512,512]{1,0:T(8,128)(2,1)}) custom-call(s32[1,8]{1,0:T(1,128)} %len_ref.3, s32[1,1024]{1,0:T(1,128)} %bitcast.162, bf16[512,512]{1,0:T(8,128)(2,1)} %bitcast.155, bf16[1024,1536]{1,0:T(8,128)(2,1)} %get-tuple-element.15.vqk_ref, bf16[1024,512]{1,0:T(8,128)(2,1)} %get-tuple-element.16.datt_ref, ...), custom_call_target="tpu_custom_call" | custom-call | flops 10000000000 | bytes 10000000 | tf_op jit(solution)/shard_map/pallas_call | solution.py:320
  80.3 1.5 collective-permute-start.7
  81.9 3.7 %shard_map.105 = bf16[512,1536]{1,0:T(8,128)(2,1)} custom-call(bf16[512,512]{1,0:T(8,128)(2,1)} %get-tuple-element.22.nt_ref, bf16[512,1536]{1,0:T(8,128)(2,1)} %get-tuple-element.23.dpre_ref), custom_call_target="tpu_custom_call" | custom-call | flops 1000000000 | bytes 10000000 | tf_op jit(solution)/shard_map/pallas_call | solution.py:327
  85.6 2.2 %dynamic-slice_bitcast_fusion = bf16[256,1536]{1,0:T(8,128)(2,1)} fusion(bf16[2,256,1536]{2,1,0:T(8,128)(2,1)} %bitcast.138, s32[]{:T(128)S(6)} %select_n.97), kind=kLoop, calls=%fused_computation.13 | loop fusion | bytes 1572868 | tf_op jit(solution)/shard_map/jit(dynamic_index_in_dim)/squeeze | solution.py:264
  87.9 1.6 collective-permute-start.8
  90.0 3.7 %all-to-all-start.2 = ((bf16[8,64,512]{2,1,0:T(8,128)(2,1)}), bf16[8,64,512]{2,1,0:T(8,128)(2,1)S(1)}, u32[]{:S(2)}, u32[]{:S(2)}) async-start(bf16[8,64,512]{2,1,0:T(8,128)(2,1)} %bitcast.6), calls=%async_computation.2 | async-start | bytes 1048576 | tf_op jit(solution)/shard_map/all_to_all | solution.py:330
  93.8 3.6 %collective-permute-start.11 = (bf16[32,512]{1,0:T(8,128)(2,1)S(1)}, bf16[32,512]{1,0:T(8,128)(2,1)S(1)}, u32[]{:S(2)}, u32[]{:S(2)}) collective-permute-start(bf16[32,512]{1,0:T(8,128)(2,1)S(1)} %get-tuple-element.34), channel_id=1, source_target_pairs={{0,24},{1,25},{2,26},{3,27},{4,28},{5,29},{6,30},{7,31},{8,16},{9,... | collective-permute-start | bytes 98312 | tf_op jit(solution)/shard_map/ppermute | solution.py:234
  99.6 8.2 %collective-permute-done.11 = bf16[32,512]{1,0:T(8,128)(2,1)S(1)} collective-permute-done((bf16[32,512]{1,0:T(8,128)(2,1)S(1)}, bf16[32,512]{1,0:T(8,128)(2,1)S(1)}, u32[]{:S(2)}, u32[]{:S(2)}) %collective-permute-start.11) | collective-permute-done | bytes 32800 | tf_op jit(solution)/shard_map/ppermute | solution.py:234
  107.8 3.3 %collective-permute-done.10 = bf16[32,512]{1,0:T(8,128)(2,1)S(1)} collective-permute-done((bf16[32,512]{1,0:T(8,128)(2,1)S(1)}, bf16[32,512]{1,0:T(8,128)(2,1)S(1)}, u32[]{:S(2)}, u32[]{:S(2)}) %collective-permute-start.10) | collective-permute-done | bytes 32800 | tf_op jit(solution)/shard_map/ppermute | solution.py:234
  111.5 1.5 collective-permute-start.19
  113.9 1.8 %collective-permute-start.13 = (bf16[32,512]{1,0:T(8,128)(2,1)S(1)}, bf16[32,512]{1,0:T(8,128)(2,1)S(1)}, u32[]{:S(2)}, u32[]{:S(2)}) collective-permute-start(bf16[32,512]{1,0:T(8,128)(2,1)S(1)} %get-tuple-element.25), channel_id=1, source_target_pairs={{0,16},{1,17},{2,18},{3,19},{4,20},{5,21},{6,22},{7,23},{8,24},{9,... | collective-permute-start | bytes 98312 | tf_op jit(solution)/shard_map/ppermute | solution.py:234
  115.7 2.4 %collective-permute-start.14 = (bf16[32,512]{1,0:T(8,128)(2,1)S(1)}, bf16[32,512]{1,0:T(8,128)(2,1)S(1)}, u32[]{:S(2)}, u32[]{:S(2)}) collective-permute-start(bf16[32,512]{1,0:T(8,128)(2,1)S(1)} %get-tuple-element.25), channel_id=1, source_target_pairs={{0,24},{1,25},{2,26},{3,27},{4,28},{5,29},{6,30},{7,31},{8,16},{9,... | collective-permute-start | bytes 98312 | tf_op jit(solution)/shard_map/ppermute | solution.py:234
  122.6 8.0 %collective-permute-done.20 = bf16[64,1536]{1,0:T(8,128)(2,1)S(1)} collective-permute-done((bf16[64,1536]{1,0:T(8,128)(2,1)S(1)}, bf16[64,1536]{1,0:T(8,128)(2,1)S(1)}, u32[]{:S(2)}, u32[]{:S(2)}) %collective-permute-start.20) | collective-permute-done | bytes 196640 | tf_op jit(solution)/shard_map/ppermute | solution.py:234
  130.7 2.3 %collective-permute-start.23 = (bf16[16,1536]{1,0:T(8,128)(2,1)S(1)}, bf16[16,1536]{1,0:T(8,128)(2,1)S(1)}, u32[]{:S(2)}, u32[]{:S(2)}) collective-permute-start(bf16[16,1536]{1,0:T(8,128)(2,1)S(1)} %get-tuple-element.31), channel_id=1, source_target_pairs={{0,24},{1,25},{2,26},{3,27},{4,28},{5,29},{6,30},{7,31},{8,16},{9,... | collective-permute-start | bytes 147464 | tf_op jit(solution)/shard_map/ppermute | solution.py:234
  135.1 1.9 %collective-permute-done.23 = bf16[16,1536]{1,0:T(8,128)(2,1)S(1)} collective-permute-done((bf16[16,1536]{1,0:T(8,128)(2,1)S(1)}, bf16[16,1536]{1,0:T(8,128)(2,1)S(1)}, u32[]{:S(2)}, u32[]{:S(2)}) %collective-permute-start.23) | collective-permute-done | bytes 49184 | tf_op jit(solution)/shard_map/ppermute | solution.py:234
  139.0 1.3 collective-permute-start.24
  140.4 2.2 %collective-permute-start.25 = (bf16[16,1536]{1,0:T(8,128)(2,1)S(1)}, bf16[16,1536]{1,0:T(8,128)(2,1)S(1)}, u32[]{:S(2)}, u32[]{:S(2)}) collective-permute-start(bf16[16,1536]{1,0:T(8,128)(2,1)S(1)} %get-tuple-element.27), channel_id=1, source_target_pairs={{0,16},{1,17},{2,18},{3,19},{4,20},{5,21},{6,22},{7,23},{8,24},{9,... | collective-permute-start | bytes 147464 | tf_op jit(solution)/shard_map/ppermute | solution.py:234
  143.1 2.8 %collective-permute-start.26 = (bf16[16,1536]{1,0:T(8,128)(2,1)S(1)}, bf16[16,1536]{1,0:T(8,128)(2,1)S(1)}, u32[]{:S(2)}, u32[]{:S(2)}) collective-permute-start(bf16[16,1536]{1,0:T(8,128)(2,1)S(1)} %get-tuple-element.27), channel_id=1, source_target_pairs={{0,24},{1,25},{2,26},{3,27},{4,28},{5,29},{6,30},{7,31},{8,16},{9,... | collective-permute-start | bytes 147464 | tf_op jit(solution)/shard_map/ppermute | solution.py:234
  146.0 3.0 %collective-permute-done.26 = bf16[16,1536]{1,0:T(8,128)(2,1)S(1)} collective-permute-done((bf16[16,1536]{1,0:T(8,128)(2,1)S(1)}, bf16[16,1536]{1,0:T(8,128)(2,1)S(1)}, u32[]{:S(2)}, u32[]{:S(2)}) %collective-permute-start.26) | collective-permute-done | bytes 49184 | tf_op jit(solution)/shard_map/ppermute | solution.py:234
  149.0 2.0 %collective-permute-start.27 = (bf16[64,1536]{1,0:T(8,128)(2,1)S(1)}, bf16[64,1536]{1,0:T(8,128)(2,1)S(1)}, u32[]{:S(2)}, u32[]{:S(2)}) collective-permute-start(bf16[64,1536]{1,0:T(8,128)(2,1)S(1)} %bitcast.150), channel_id=1, source_target_pairs={{0,2},{1,5},{2,0},{3,7},{4,6},{5,1},{6,4},{7,3},{8,10},{9,13},{10,... | collective-permute-start | bytes 589832 | tf_op jit(solution)/shard_map/ppermute | solution.py:234
  151.1 3.6 %collective-permute-done.27 = bf16[64,1536]{1,0:T(8,128)(2,1)S(1)} collective-permute-done((bf16[64,1536]{1,0:T(8,128)(2,1)S(1)}, bf16[64,1536]{1,0:T(8,128)(2,1)S(1)}, u32[]{:S(2)}, u32[]{:S(2)}) %collective-permute-start.27) | collective-permute-done | bytes 196640 | tf_op jit(solution)/shard_map/ppermute | solution.py:234
  154.7 1.8 %collective-permute-start.28 = (bf16[128,1536]{1,0:T(8,128)(2,1)S(1)}, bf16[128,1536]{1,0:T(8,128)(2,1)S(1)}, u32[]{:S(2)}, u32[]{:S(2)}) collective-permute-start(bf16[128,1536]{1,0:T(8,128)(2,1)S(1)} %bitcast.140), channel_id=1, source_target_pairs={{0,4},{1,3},{2,6},{3,1},{4,0},{5,7},{6,2},{7,5},{8,12},{9,11},{10,... | collective-permute-start | bytes 1179656 | tf_op jit(solution)/shard_map/ppermute | solution.py:234
  157.4 5.1 %collective-permute-done.28 = bf16[128,1536]{1,0:T(8,128)(2,1)S(1)} collective-permute-done((bf16[128,1536]{1,0:T(8,128)(2,1)S(1)}, bf16[128,1536]{1,0:T(8,128)(2,1)S(1)}, u32[]{:S(2)}, u32[]{:S(2)}) %collective-permute-start.28) | collective-permute-done | bytes 393248 | tf_op jit(solution)/shard_map/ppermute | solution.py:234
  165.8 5.7 %shard_map.104 = f32[1024,512]{1,0:T(8,128)} custom-call(s32[1,512]{1,0:T(1,128)} %broadcast_subtract_fusion.3.refs_0_, s32[1,512]{1,0:T(1,128)} %broadcast_subtract_fusion.2.refs_1_, s32[1,512]{1,0:T(1,128)} %broadcast_subtract_fusion.1.refs_2_, s32[1,512]{1,0:T(1,128)} %broadcast_subtract_fusion.refs_3_, bf16[512,512]{1,0:T(8,128)(2,1)} %bitcast.137, ...), custom_call_target="tpu_custom_call" | custom-call | flops 1000000000 | bytes 10000000 | tf_op jit(solution)/shard_map/pallas_call | solution.py:341
  172.2 2.4 %pad_maximum_fusion = f32[512,2048]{1,0:T(8,128)} fusion(f32[512,1536]{1,0:T(8,128)S(1)} %bitcast_convert_fusion, f32[512,512]{1,0:T(8,128)S(1)} %get-tuple-element.29), kind=kLoop, calls=%fused_computation.1 | loop fusion | flops 1048576 | bytes 8388608 | tf_op jit(solution)/shard_map/concatenate | solution.py:348
  (111 shorter events, 24.7 us)
Async XLA Ops:
  19.8 16.8 %all-to-all-start.1 = ((bf16[8,64,512]{2,1,0:T(8,128)(2,1)}), bf16[8,64,512]{2,1,0:T(8,128)(2,1)S(1)}, u32[]{:S(2)}, u32[]{:S(2)}) async-start(bf16[8,64,512]{2,1,0:T(8,128)(2,1)} %bitcast.4), calls=%async_computation.1 | async-start | bytes 1048576 | tf_op jit(solution)/shard_map/all_to_all | solution.py:301
  25.7 3.6 %collective-permute-start = (s32[1,512]{1,0:T(1,128)S(1)}, s32[1,512]{1,0:T(1,128)S(1)}, u32[]{:S(2)}, u32[]{:S(2)}) collective-permute-start(s32[1,512]{1,0:T(1,128)S(1)} %reshape.146), channel_id=1, source_target_pairs={{0,2},{1,3},{2,0},{3,1},{4,6},{5,7},{6,4},{7,5},{8,10},{9,11},{10,... | collective-permute-start | bytes 6152 | tf_op jit(solution)/shard_map/ppermute | solution.py:336
  27.2 2.7 %collective-permute-start.1 = (s32[1,512]{1,0:T(1,128)S(1)}, s32[1,512]{1,0:T(1,128)S(1)}, u32[]{:S(2)}, u32[]{:S(2)}) collective-permute-start(s32[1,512]{1,0:T(1,128)S(1)} %reshape.146), channel_id=1, source_target_pairs={{0,1},{1,0},{2,3},{3,2},{4,5},{5,4},{6,7},{7,6},{8,9},{9,8},{10,11... | collective-permute-start | bytes 6152 | tf_op jit(solution)/shard_map/ppermute | solution.py:336
  29.8 59.6 %collective-permute-start.2 = (s32[1,512]{1,0:T(1,128)S(1)}, s32[1,512]{1,0:T(1,128)S(1)}, u32[]{:S(2)}, u32[]{:S(2)}) collective-permute-start(s32[1,512]{1,0:T(1,128)S(1)} %collective-permute-done), channel_id=1, source_target_pairs={{0,1},{1,0},{2,3},{3,2},{4,5},{5,4},{6,7},{7,6},{8,9},{9,8},{10,11... | collective-permute-start | bytes 6152 | tf_op jit(solution)/shard_map/ppermute | solution.py:336
  59.5 20.6 %collective-permute-start.6 = (bf16[512,512]{1,0:T(8,128)(2,1)S(1)}, bf16[512,512]{1,0:T(8,128)(2,1)S(1)}, u32[]{:S(2)}, u32[]{:S(2)}) collective-permute-start(bf16[512,512]{1,0:T(8,128)(2,1)S(1)} %dynamic-slice_bitcast_fusion.1), channel_id=1, source_target_pairs={{0,1},{1,0},{2,3},{3,2},{4,5},{5,4},{6,7},{7,6},{8,9},{9,8},{10,11... | collective-permute-start | bytes 1572872 | tf_op jit(solution)/shard_map/ppermute | solution.py:234
  80.3 7.4 %collective-permute-start.7 = (bf16[256,512]{1,0:T(8,128)(2,1)S(1)}, bf16[256,512]{1,0:T(8,128)(2,1)S(1)}, u32[]{:S(2)}, u32[]{:S(2)}) collective-permute-start(bf16[256,512]{1,0:T(8,128)(2,1)S(1)} %dynamic-slice_bitcast_fusion.3), channel_id=1, source_target_pairs={{0,4},{1,3},{2,6},{3,1},{4,0},{5,7},{6,2},{7,5},{8,12},{9,11},{10,... | collective-permute-start | bytes 786440 | tf_op jit(solution)/shard_map/ppermute | solution.py:234
  87.7 10.5 %collective-permute-start.18 = (bf16[256,1536]{1,0:T(8,128)(2,1)}, bf16[256,1536]{1,0:T(8,128)(2,1)}, u32[]{:S(2)}, u32[]{:S(2)}) collective-permute-start(bf16[256,1536]{1,0:T(8,128)(2,1)} %dynamic-slice_bitcast_fusion), channel_id=1, source_target_pairs={{0,1},{1,0},{2,3},{3,2},{4,5},{5,4},{6,7},{7,6},{8,9},{9,8},{10,11... | collective-permute-start | bytes 2359304 | tf_op jit(solution)/shard_map/ppermute | solution.py:234
  87.9 5.9 %collective-permute-start.8 = (bf16[128,512]{1,0:T(8,128)(2,1)S(1)}, bf16[128,512]{1,0:T(8,128)(2,1)S(1)}, u32[]{:S(2)}, u32[]{:S(2)}) collective-permute-start(bf16[128,512]{1,0:T(8,128)(2,1)S(1)} %dynamic-slice_bitcast_fusion.5), channel_id=1, source_target_pairs={{0,2},{1,5},{2,0},{3,7},{4,6},{5,1},{6,4},{7,3},{8,10},{9,13},{10,... | collective-permute-start | bytes 393224 | tf_op jit(solution)/shard_map/ppermute | solution.py:234
  90.0 23.0 %all-to-all-start.2 = ((bf16[8,64,512]{2,1,0:T(8,128)(2,1)}), bf16[8,64,512]{2,1,0:T(8,128)(2,1)S(1)}, u32[]{:S(2)}, u32[]{:S(2)}) async-start(bf16[8,64,512]{2,1,0:T(8,128)(2,1)} %bitcast.6), calls=%async_computation.2 | async-start | bytes 1048576 | tf_op jit(solution)/shard_map/all_to_all | solution.py:330
  93.8 14.0 %collective-permute-start.11 = (bf16[32,512]{1,0:T(8,128)(2,1)S(1)}, bf16[32,512]{1,0:T(8,128)(2,1)S(1)}, u32[]{:S(2)}, u32[]{:S(2)}) collective-permute-start(bf16[32,512]{1,0:T(8,128)(2,1)S(1)} %get-tuple-element.34), channel_id=1, source_target_pairs={{0,24},{1,25},{2,26},{3,27},{4,28},{5,29},{6,30},{7,31},{8,16},{9,... | collective-permute-start | bytes 98312 | tf_op jit(solution)/shard_map/ppermute | solution.py:234
  97.4 13.7 %collective-permute-start.10 = (bf16[32,512]{1,0:T(8,128)(2,1)S(1)}, bf16[32,512]{1,0:T(8,128)(2,1)S(1)}, u32[]{:S(2)}, u32[]{:S(2)}) collective-permute-start(bf16[32,512]{1,0:T(8,128)(2,1)S(1)} %get-tuple-element.35), channel_id=1, source_target_pairs={{0,16},{1,17},{2,18},{3,19},{4,20},{5,21},{6,22},{7,23},{8,24},{9,... | collective-permute-start | bytes 98312 | tf_op jit(solution)/shard_map/ppermute | solution.py:234
  97.4 13.7 %collective-permute-start.9 = (bf16[32,512]{1,0:T(8,128)(2,1)S(1)}, bf16[32,512]{1,0:T(8,128)(2,1)S(1)}, u32[]{:S(2)}, u32[]{:S(2)}) collective-permute-start(bf16[32,512]{1,0:T(8,128)(2,1)S(1)} %get-tuple-element.33), channel_id=1, source_target_pairs={{0,8},{1,9},{2,10},{3,11},{4,12},{5,13},{6,14},{7,15},{8,0},{9,1},... | collective-permute-start | bytes 98312 | tf_op jit(solution)/shard_map/ppermute | solution.py:234
  111.2 4.5 %collective-permute-start.12 = (bf16[32,512]{1,0:T(8,128)(2,1)S(1)}, bf16[32,512]{1,0:T(8,128)(2,1)S(1)}, u32[]{:S(2)}, u32[]{:S(2)}) collective-permute-start(bf16[32,512]{1,0:T(8,128)(2,1)S(1)} %get-tuple-element.25), channel_id=1, source_target_pairs={{0,8},{1,9},{2,10},{3,11},{4,12},{5,13},{6,14},{7,15},{8,0},{9,1},... | collective-permute-start | bytes 98312 | tf_op jit(solution)/shard_map/ppermute | solution.py:234
  111.5 7.8 %collective-permute-start.19 = (bf16[128,1536]{1,0:T(8,128)(2,1)S(1)}, bf16[128,1536]{1,0:T(8,128)(2,1)S(1)}, u32[]{:S(2)}, u32[]{:S(2)}) collective-permute-start(bf16[128,1536]{1,0:T(8,128)(2,1)S(1)} %dynamic-slice_bitcast_fusion.2), channel_id=1, source_target_pairs={{0,4},{1,3},{2,6},{3,1},{4,0},{5,7},{6,2},{7,5},{8,12},{9,11},{10,... | collective-permute-start | bytes 1179656 | tf_op jit(solution)/shard_map/ppermute | solution.py:234
  113.0 43.7 %collective-permute-start.3 = (bf16[512,512]{1,0:T(8,128)(2,1)S(1)}, bf16[512,512]{1,0:T(8,128)(2,1)S(1)}, u32[]{:S(2)}, u32[]{:S(2)}) collective-permute-start(bf16[512,512]{1,0:T(8,128)(2,1)S(1)} %bitcast.135), channel_id=1, source_target_pairs={{0,2},{1,3},{2,0},{3,1},{4,6},{5,7},{6,4},{7,5},{8,10},{9,11},{10,... | collective-permute-start | bytes 1572872 | tf_op jit(solution)/shard_map/ppermute | solution.py:337
  113.9 50.3 %collective-permute-start.4 = (bf16[512,512]{1,0:T(8,128)(2,1)S(1)}, bf16[512,512]{1,0:T(8,128)(2,1)S(1)}, u32[]{:S(2)}, u32[]{:S(2)}) collective-permute-start(bf16[512,512]{1,0:T(8,128)(2,1)S(1)} %bitcast.136), channel_id=1, source_target_pairs={{0,1},{1,0},{2,3},{3,2},{4,5},{5,4},{6,7},{7,6},{8,9},{9,8},{10,11... | collective-permute-start | bytes 1572872 | tf_op jit(solution)/shard_map/ppermute | solution.py:337
  113.9 5.1 %collective-permute-start.13 = (bf16[32,512]{1,0:T(8,128)(2,1)S(1)}, bf16[32,512]{1,0:T(8,128)(2,1)S(1)}, u32[]{:S(2)}, u32[]{:S(2)}) collective-permute-start(bf16[32,512]{1,0:T(8,128)(2,1)S(1)} %get-tuple-element.25), channel_id=1, source_target_pairs={{0,16},{1,17},{2,18},{3,19},{4,20},{5,21},{6,22},{7,23},{8,24},{9,... | collective-permute-start | bytes 98312 | tf_op jit(solution)/shard_map/ppermute | solution.py:234
  115.7 5.7 %collective-permute-start.14 = (bf16[32,512]{1,0:T(8,128)(2,1)S(1)}, bf16[32,512]{1,0:T(8,128)(2,1)S(1)}, u32[]{:S(2)}, u32[]{:S(2)}) collective-permute-start(bf16[32,512]{1,0:T(8,128)(2,1)S(1)} %get-tuple-element.25), channel_id=1, source_target_pairs={{0,24},{1,25},{2,26},{3,27},{4,28},{5,29},{6,30},{7,31},{8,16},{9,... | collective-permute-start | bytes 98312 | tf_op jit(solution)/shard_map/ppermute | solution.py:234
  119.5 11.1 %collective-permute-start.20 = (bf16[64,1536]{1,0:T(8,128)(2,1)S(1)}, bf16[64,1536]{1,0:T(8,128)(2,1)S(1)}, u32[]{:S(2)}, u32[]{:S(2)}) collective-permute-start(bf16[64,1536]{1,0:T(8,128)(2,1)S(1)} %dynamic-slice_bitcast_fusion.4), channel_id=1, source_target_pairs={{0,2},{1,5},{2,0},{3,7},{4,6},{5,1},{6,4},{7,3},{8,10},{9,13},{10,... | collective-permute-start | bytes 589832 | tf_op jit(solution)/shard_map/ppermute | solution.py:234
  121.4 12.5 %collective-permute-start.15 = (bf16[128,512]{1,0:T(8,128)(2,1)S(1)}, bf16[128,512]{1,0:T(8,128)(2,1)S(1)}, u32[]{:S(2)}, u32[]{:S(2)}) collective-permute-start(bf16[128,512]{1,0:T(8,128)(2,1)S(1)} %bitcast.158), channel_id=1, source_target_pairs={{0,2},{1,5},{2,0},{3,7},{4,6},{5,1},{6,4},{7,3},{8,10},{9,13},{10,... | collective-permute-start | bytes 393224 | tf_op jit(solution)/shard_map/ppermute | solution.py:234
  130.7 6.3 %collective-permute-start.23 = (bf16[16,1536]{1,0:T(8,128)(2,1)S(1)}, bf16[16,1536]{1,0:T(8,128)(2,1)S(1)}, u32[]{:S(2)}, u32[]{:S(2)}) collective-permute-start(bf16[16,1536]{1,0:T(8,128)(2,1)S(1)} %get-tuple-element.31), channel_id=1, source_target_pairs={{0,24},{1,25},{2,26},{3,27},{4,28},{5,29},{6,30},{7,31},{8,16},{9,... | collective-permute-start | bytes 147464 | tf_op jit(solution)/shard_map/ppermute | solution.py:234
  133.0 5.9 %collective-permute-start.22 = (bf16[16,1536]{1,0:T(8,128)(2,1)S(1)}, bf16[16,1536]{1,0:T(8,128)(2,1)S(1)}, u32[]{:S(2)}, u32[]{:S(2)}) collective-permute-start(bf16[16,1536]{1,0:T(8,128)(2,1)S(1)} %get-tuple-element.32), channel_id=1, source_target_pairs={{0,16},{1,17},{2,18},{3,19},{4,20},{5,21},{6,22},{7,23},{8,24},{9,... | collective-permute-start | bytes 147464 | tf_op jit(solution)/shard_map/ppermute | solution.py:234
  133.9 5.0 %collective-permute-start.21 = (bf16[16,1536]{1,0:T(8,128)(2,1)S(1)}, bf16[16,1536]{1,0:T(8,128)(2,1)S(1)}, u32[]{:S(2)}, u32[]{:S(2)}) collective-permute-start(bf16[16,1536]{1,0:T(8,128)(2,1)S(1)} %get-tuple-element.30), channel_id=1, source_target_pairs={{0,8},{1,9},{2,10},{3,11},{4,12},{5,13},{6,14},{7,15},{8,0},{9,1},... | collective-permute-start | bytes 147464 | tf_op jit(solution)/shard_map/ppermute | solution.py:234
  137.0 19.5 %collective-permute-start.16 = (bf16[256,512]{1,0:T(8,128)(2,1)S(1)}, bf16[256,512]{1,0:T(8,128)(2,1)S(1)}, u32[]{:S(2)}, u32[]{:S(2)}) collective-permute-start(bf16[256,512]{1,0:T(8,128)(2,1)S(1)} %bitcast.144), channel_id=1, source_target_pairs={{0,4},{1,3},{2,6},{3,1},{4,0},{5,7},{6,2},{7,5},{8,12},{9,11},{10,... | collective-permute-start | bytes 786440 | tf_op jit(solution)/shard_map/ppermute | solution.py:234
  139.0 4.2 %collective-permute-start.24 = (bf16[16,1536]{1,0:T(8,128)(2,1)S(1)}, bf16[16,1536]{1,0:T(8,128)(2,1)S(1)}, u32[]{:S(2)}, u32[]{:S(2)}) collective-permute-start(bf16[16,1536]{1,0:T(8,128)(2,1)S(1)} %get-tuple-element.27), channel_id=1, source_target_pairs={{0,8},{1,9},{2,10},{3,11},{4,12},{5,13},{6,14},{7,15},{8,0},{9,1},... | collective-permute-start | bytes 147464 | tf_op jit(solution)/shard_map/ppermute | solution.py:234
  140.4 5.6 %collective-permute-start.25 = (bf16[16,1536]{1,0:T(8,128)(2,1)S(1)}, bf16[16,1536]{1,0:T(8,128)(2,1)S(1)}, u32[]{:S(2)}, u32[]{:S(2)}) collective-permute-start(bf16[16,1536]{1,0:T(8,128)(2,1)S(1)} %get-tuple-element.27), channel_id=1, source_target_pairs={{0,16},{1,17},{2,18},{3,19},{4,20},{5,21},{6,22},{7,23},{8,24},{9,... | collective-permute-start | bytes 147464 | tf_op jit(solution)/shard_map/ppermute | solution.py:234
  143.1 5.9 %collective-permute-start.26 = (bf16[16,1536]{1,0:T(8,128)(2,1)S(1)}, bf16[16,1536]{1,0:T(8,128)(2,1)S(1)}, u32[]{:S(2)}, u32[]{:S(2)}) collective-permute-start(bf16[16,1536]{1,0:T(8,128)(2,1)S(1)} %get-tuple-element.27), channel_id=1, source_target_pairs={{0,24},{1,25},{2,26},{3,27},{4,28},{5,29},{6,30},{7,31},{8,16},{9,... | collective-permute-start | bytes 147464 | tf_op jit(solution)/shard_map/ppermute | solution.py:234
  149.0 5.7 %collective-permute-start.27 = (bf16[64,1536]{1,0:T(8,128)(2,1)S(1)}, bf16[64,1536]{1,0:T(8,128)(2,1)S(1)}, u32[]{:S(2)}, u32[]{:S(2)}) collective-permute-start(bf16[64,1536]{1,0:T(8,128)(2,1)S(1)} %bitcast.150), channel_id=1, source_target_pairs={{0,2},{1,5},{2,0},{3,7},{4,6},{5,1},{6,4},{7,3},{8,10},{9,13},{10,... | collective-permute-start | bytes 589832 | tf_op jit(solution)/shard_map/ppermute | solution.py:234
  154.7 7.8 %collective-permute-start.28 = (bf16[128,1536]{1,0:T(8,128)(2,1)S(1)}, bf16[128,1536]{1,0:T(8,128)(2,1)S(1)}, u32[]{:S(2)}, u32[]{:S(2)}) collective-permute-start(bf16[128,1536]{1,0:T(8,128)(2,1)S(1)} %bitcast.140), channel_id=1, source_target_pairs={{0,4},{1,3},{2,6},{3,1},{4,0},{5,7},{6,2},{7,5},{8,12},{9,11},{10,... | collective-permute-start | bytes 1179656 | tf_op jit(solution)/shard_map/ppermute | solution.py:234
  156.5 6.1 %collective-permute-start.17 = (bf16[512,512]{1,0:T(8,128)(2,1)S(1)}, bf16[512,512]{1,0:T(8,128)(2,1)S(1)}, u32[]{:S(2)}, u32[]{:S(2)}) collective-permute-start(bf16[512,512]{1,0:T(8,128)(2,1)S(1)} %bitcast.133), channel_id=1, source_target_pairs={{0,1},{1,0},{2,3},{3,2},{4,5},{5,4},{6,7},{7,6},{8,9},{9,8},{10,11... | collective-permute-start | bytes 1572872 | tf_op jit(solution)/shard_map/ppermute | solution.py:234
  156.7 7.4 %collective-permute-start.5 = (bf16[512,512]{1,0:T(8,128)(2,1)S(1)}, bf16[512,512]{1,0:T(8,128)(2,1)S(1)}, u32[]{:S(2)}, u32[]{:S(2)}) collective-permute-start(bf16[512,512]{1,0:T(8,128)(2,1)S(1)} %collective-permute-done.3.refs_5_), channel_id=1, source_target_pairs={{0,1},{1,0},{2,3},{3,2},{4,5},{5,4},{6,7},{7,6},{8,9},{9,8},{10,11... | collective-permute-start | bytes 1572872 | tf_op jit(solution)/shard_map/ppermute | solution.py:337
  162.6 9.1 %collective-permute-start.29 = (bf16[256,1536]{1,0:T(8,128)(2,1)S(1)}, bf16[256,1536]{1,0:T(8,128)(2,1)S(1)}, u32[]{:S(2)}, u32[]{:S(2)}) collective-permute-start(bf16[256,1536]{1,0:T(8,128)(2,1)S(1)} %bitcast.129), channel_id=1, source_target_pairs={{0,1},{1,0},{2,3},{3,2},{4,5},{5,4},{6,7},{7,6},{8,9},{9,8},{10,11... | collective-permute-start | bytes 2359304 | tf_op jit(solution)/shard_map/ppermute | solution.py:234
  (8 other events, 78.2 us)

commit v2 on v1

v2 whole, which is shorter than its diff:
```python
import functools

import jax
import jax.numpy as jnp
from jax import lax
from jax.experimental import pallas as pl
from jax.experimental.pallas import tpu as pltpu
from jax.sharding import PartitionSpec as P


HEADS = 4
MOST = 512
EPS = 1e-05
BLOCK = 256
GROUPS = ((0, 2), (2, 3), (3, 4))
VMEM = pl.BlockSpec(memory_space=pltpu.VMEM)
SMEM = pl.BlockSpec(memory_space=pltpu.SMEM)
BF = jnp.bfloat16
F32 = jnp.float32


AXES = ("e1", "e0", "s1", "s0")


def mm(a, b):
    return jnp.dot(a, b, preferred_element_type=F32)


def mm_t(a, b):
    return lax.dot_general(a, b, (((1,), (1,)), ((), ())), preferred_element_type=F32)


def tt_mm(a, b):
    return lax.dot_general(a, b, (((0,), (0,)), ((), ())), preferred_element_type=F32)


def center_rows(x):
    center = x - jnp.mean(x, axis=-1, keepdims=True)
    spread = jnp.mean(center * center, axis=-1, keepdims=True)
    inverse = lax.rsqrt(spread + EPS)
    return center * inverse, inverse


def center_back(grad, normed, inverse):
    along = jnp.mean(grad * normed, axis=-1, keepdims=True)
    return inverse * (grad - jnp.mean(grad, axis=-1, keepdims=True) - normed * along)


def history_ends(len_ref):
    ends, total = [], 0
    for k in range(len_ref.shape[1]):
        total = total + len_ref[0, k]
        ends.append(total)
    return ends


def history_start(ends, place):
    start = jnp.zeros_like(place)
    for end in ends:
        start = jnp.maximum(start, jnp.where(place >= end, end, 0))
    return start


def one_hot_rows(slot_row, slots):
    at = lax.broadcasted_iota(jnp.int32, (slots, slot_row.shape[1]), 0)
    return jnp.where(slot_row[...] == at, 1.0, 0.0).astype(BF)


def early_kernel(slot_row, wout_ref, og_ref, dgated_ref, res_ref):
    slots = res_ref.shape[0]
    dgated_ref[...] = mm_t(og_ref[...], wout_ref[...]).astype(BF)
    res_ref[...] = mm(one_hot_rows(slot_row, slots), og_ref[...])


def first_kernel(len_ref, slot_row, slot_col, rows_ref, win_ref, wout_ref, og_ref, dgated_ref, *refs):
    count = len(GROUPS)
    out_ref, wg_ref, nt_ref, dpre_ref = refs[:4]
    vqk, datt, dsil = (refs[4 + k * count : 4 + (k + 1) * count] for k in range(3))
    hid, gate, ev, att, gated, dgate, dsil_gate = refs[4 + 3 * count :]
    slots, width = rows_ref.shape
    tokens = og_ref.shape[0]
    head = width // HEADS
    half_scale = 0.5 * head**-0.5
    normed, _ = center_rows(rows_ref[...].astype(F32))
    normed = normed.astype(BF)
    nt_ref[...] = normed.T
    for j in range(4):
        cols = slice(j * width, (j + 1) * width)
        pre = mm(normed, win_ref[:, cols])
        sig = 0.5 + 0.5 * jnp.tanh(0.5 * pre)
        act = pre * sig
        hid[:, cols] = act.astype(BF)
        slope = (sig + act * (1.0 - sig)).astype(BF)
        if j == 0:
            dsil_gate[...] = slope
        else:
            for (h0, h1), ref in zip(GROUPS, dsil):
                wide = (h1 - h0) * head
                ref[:, (j - 1) * wide : j * wide] = slope[:, h0 * head : h1 * head]

    def spread(i, _):
        span = pl.ds(pl.multiple_of(i * BLOCK, BLOCK), BLOCK)
        lane = lax.broadcasted_iota(jnp.int32, (BLOCK, slots), 1)
        pick = jnp.where(slot_col[span, :] == lane, 1.0, 0.0).astype(BF)
        ev[span, :] = mm(pick, rows_ref[...]).astype(BF)
        gate[span, :] = mm(pick, hid[:, :width]).astype(BF)
        for j in range(3):
            part = mm(pick, hid[:, (j + 1) * width : (j + 2) * width]).astype(BF)
            for (h0, h1), ref in zip(GROUPS, vqk):
                wide = (h1 - h0) * head
                ref[span, j * wide : (j + 1) * wide] = part[:, h0 * head : h1 * head]
        return 0

    lax.fori_loop(0, tokens // BLOCK, spread, 0)
    ends = history_ends(len_ref)

    def rows_step(i, _):
        base = pl.multiple_of(i * BLOCK, BLOCK)
        span = pl.ds(base, BLOCK)
        start = history_start(ends, base + lax.broadcasted_iota(jnp.int32, (BLOCK, 1), 0))
        place = base + lax.broadcasted_iota(jnp.int32, (BLOCK, BLOCK), 0)
        att[...] = jnp.zeros_like(att)

        def keys_step(j, _):
            key_base = pl.multiple_of(j * BLOCK, BLOCK)
            keys = pl.ds(key_base, BLOCK)
            other = key_base + lax.broadcasted_iota(jnp.int32, (BLOCK, BLOCK), 1)
            allowed = (other >= start) & (other <= place)
            parts = []
            for (h0, h1), ref in zip(GROUPS, vqk):
                wide = (h1 - h0) * head
                for lo in range(0, wide, head):
                    q = ref[span, wide + lo : wide + lo + head]
                    k = ref[keys, 2 * wide + lo : 2 * wide + lo + head]
                    u = mm_t(q, k) * half_scale
                    w = jnp.where(allowed, u + u * jnp.tanh(u), 0.0).astype(BF)
                    parts.append(mm(w, ref[keys, lo : lo + head]))
            for h, part in enumerate(parts):
                att[:, h * head : (h + 1) * head] += part
            return 0

        lax.fori_loop(history_start(ends, base) // BLOCK, i + 1, keys_step, 0)
        normed_att, inverse = center_rows(att[...] * (1.0 / MOST))
        g = gate[span, :].astype(F32)
        gated_rows = (normed_att * g).astype(BF)
        gated[span, :] = gated_rows
        out_ref[span, :] = (mm(gated_rows, wout_ref[...]) + ev[span, :].astype(F32)).astype(BF)
        dgated = dgated_ref[span, :].astype(F32)
        dgate[span, :] = (dgated * normed_att).astype(BF)
        back = (center_back(dgated * g, normed_att, inverse) * (1.0 / MOST)).astype(BF)
        for (h0, h1), ref in zip(GROUPS, datt):
            ref[span, :] = back[:, h0 * head : h1 * head]
        return 0

    lax.fori_loop(0, tokens // BLOCK, rows_step, 0)
    wg_ref[:, :width] = tt_mm(gated[...], og_ref[...]).astype(BF)
    slot_sum = mm(one_hot_rows(slot_row, slots), dgate[...])
    dpre = (slot_sum * dsil_gate[...].astype(F32)).astype(BF)
    dpre_ref[...] = dpre
    wg_ref[:, width:] = mm(nt_ref[...], dpre).astype(BF)


def second_kernel(joined, heads, len_ref, core_ref, slot_row, vqk_ref, datt_ref, dsil_ref, nt_ref, *refs):
    before = refs[0] if joined else None
    refs = refs[1:] if joined else refs
    outs = 3 if joined else 2
    dpre_ref, sums = refs[0], refs[outs:]
    slots = dpre_ref.shape[0]
    tokens, wide = datt_ref.shape
    head = wide // heads
    half_scale = 0.5 * head**-0.5
    ends = history_ends(len_ref)
    for ref in sums:
        ref[...] = jnp.zeros_like(ref)

    def rows_step(i, _):
        base = pl.multiple_of(i * BLOCK, BLOCK)
        span = pl.ds(base, BLOCK)
        start = history_start(ends, base + lax.broadcasted_iota(jnp.int32, (1, BLOCK), 1))
        place = base + lax.broadcasted_iota(jnp.int32, (BLOCK, BLOCK), 1)

        def keys_step(j, _):
            key_base = pl.multiple_of(j * BLOCK, BLOCK)
            keys = pl.ds(key_base, BLOCK)
            other = key_base + lax.broadcasted_iota(jnp.int32, (BLOCK, BLOCK), 0)
            allowed = (other >= start) & (other <= place)
            parts = []
            for h in range(heads):
                lo = h * head
                q = vqk_ref[span, wide + lo : wide + lo + head]
                k = vqk_ref[keys, 2 * wide + lo : 2 * wide + lo + head]
                v = vqk_ref[keys, lo : lo + head]
                da = datt_ref[span, lo : lo + head]
                u = mm_t(k, q) * half_scale
                dw = mm_t(v, da)
                th = jnp.tanh(u)
                w = jnp.where(allowed, u + u * th, 0.0).astype(BF)
                slope = (half_scale + half_scale * th) * (1.0 + u - u * th)
                ds = jnp.where(allowed, dw * slope, 0.0).astype(BF)
                parts.append((mm(w, da), tt_mm(ds, k), mm(ds, q)))
            for h in range(heads):
                sums[3 * h][keys, :] += parts[h][0]
                sums[3 * h + 1][span, :] += parts[h][1]
                sums[3 * h + 2][keys, :] += parts[h][2]
            return 0

        lax.fori_loop(history_start(ends, base) // BLOCK, i + 1, keys_step, 0)
        return 0

    lax.fori_loop(0, tokens // BLOCK, rows_step, 0)
    put = one_hot_rows(slot_row, slots)
    for j in range(3):
        parts = [sums[3 * h + j][...].astype(BF) for h in range(heads)]
        cols = slice(j * wide, (j + 1) * wide)
        slot_sum = mm(put, jnp.concatenate(parts, axis=1) if heads > 1 else parts[0])
        dpre_ref[:, cols] = (slot_sum * dsil_ref[:, cols].astype(F32)).astype(BF)
    if not joined:
        refs[1][...] = mm(nt_ref[...], dpre_ref[...]).astype(BF)
        return
    half = nt_ref.shape[0] // 2
    offset = before.shape[1]
    for ref, place in ((refs[1], core_ref[0, 0]), (refs[2], 1 - core_ref[0, 0])):
        span = pl.ds(pl.multiple_of(place * half, half), half)
        ref[:, :offset] = before[span, :]
        ref[:, offset:] = mm(nt_ref[span, :], dpre_ref[...]).astype(BF)


def slot_kernel(rows_ref, res_ref, win_ref, gate_ref, *refs):
    grad_ref = refs[-1]
    width = rows_ref.shape[1]
    head = width // HEADS
    dn = mm_t(gate_ref[...], win_ref[:, :width])
    for (h0, h1), ref in zip(GROUPS, refs):
        wide = (h1 - h0) * head
        for j in range(3):
            first = (j + 1) * width + h0 * head
            dn = dn + mm_t(ref[:, j * wide : (j + 1) * wide], win_ref[:, first : first + wide])
    normed, inverse = center_rows(rows_ref[...].astype(F32))
    grad_ref[...] = (center_back(dn, normed, inverse) + res_ref[...]).astype(BF)


def assemble_kernel(core_ref, own1, got1, own2, got2, in_ref, out_ref):
    width = out_ref.shape[1]
    head = width // HEADS
    half = own1.shape[0]
    pieces = [(0, 0, out_ref, 0, width), (0, width, in_ref, 0, width)]
    at = [2 * width, 0]
    for i, (h0, h1) in enumerate(GROUPS):
        chain = 0 if i == 0 else 1
        for j in range(3):
            wide = (h1 - h0) * head
            pieces.append((chain, at[chain], in_ref, (j + 1) * width + h0 * head, wide))
            at[chain] += wide
    for sources, place in (((own1, own2), core_ref[0, 0]), ((got1, got2), 1 - core_ref[0, 0])):
        span = pl.ds(pl.multiple_of(place * half, half), half)
        for chain, source, ref, target, wide in pieces:
            ref[span, target : target + wide] = sources[chain][:, source : source + wide].astype(F32)


def table_kernel(count, *refs):
    places, rows, out = refs[:count], refs[count : 2 * count], refs[-1]
    height = min(BLOCK, out.shape[0])

    def step(i, _):
        base = pl.multiple_of(i * height, height)
        total = None
        for place, row in zip(places, rows):
            at = base + lax.broadcasted_iota(jnp.int32, (height, place.shape[1]), 0)
            put = jnp.where(place[...] == at, 1.0, 0.0).astype(BF)
            part = mm(put, row[...])
            total = part if total is None else total + part
        out[pl.ds(base, height), :] = total
        return 0

    lax.fori_loop(0, out.shape[0] // height, step, 0)


def call(kernel, outs, scratch, specs, flops, mib=24):
    return pl.pallas_call(
        kernel,
        out_shape=[jax.ShapeDtypeStruct(s, d) for s, d in outs],
        in_specs=specs,
        out_specs=[VMEM] * len(outs),
        scratch_shapes=[pltpu.VMEM(s, d) for s, d in scratch],
        compiler_params=pltpu.CompilerParams(vmem_limit_bytes=mib * 2**20),
        cost_estimate=pl.CostEstimate(flops=flops, bytes_accessed=10**7, transcendentals=0),
    )


def other_place(x, axis):
    size = lax.axis_size(axis)
    return lax.ppermute(x, axis, [(i, i ^ 1) for i in range(size)])


def exchange(x, axes):
    return lax.all_to_all(x, axes, split_axis=0, concat_axis=0, tiled=True)


def swap(x, partner):
    return lax.ppermute(x, AXES, [(d, partner(d)) for d in range(lax.axis_size(AXES))])


def weight_sum(keep, give):
    seq_bits = lax.axis_size(("s1", "s0")).bit_length() - 1
    all_bits = lax.axis_size(AXES).bit_length() - 1
    me = lax.axis_index(AXES)
    one, two = min(1, seq_bits), seq_bits
    line = [k for k in range(all_bits) if k not in (0, one, two)]
    by_core = lambda first, second: (lambda d: d ^ (1 << (second if d & 1 else first)))
    place = lambda first, second: (me >> jnp.where(me & 1 == 1, second, first)) & 1
    got = other_place(give, "s0")
    x = (keep.astype(F32) + got.astype(F32)).astype(BF)
    for first, second in ((two, one), (one, two)):
        halves = x.reshape(2, x.shape[0] // 2, x.shape[1])
        mine = lax.dynamic_index_in_dim(halves, place(first, second), 0, keepdims=False)
        give = lax.dynamic_index_in_dim(halves, 1 - place(first, second), 0, keepdims=False)
        got = swap(give, by_core(first, second))
        x = (mine.astype(F32) + got.astype(F32)).astype(BF)
    for first, second in zip(line, line[::-1]):
        got = swap(x, by_core(first, second))
        x = (x.astype(F32) + got.astype(F32)).astype(BF)
    for first, second in ((one, two), (two, one)):
        got = swap(x, by_core(first, second))
        upper = place(first, second) == 1
        x = jnp.concatenate([jnp.where(upper, got, x), jnp.where(upper, x, got)], axis=0)
    return x, other_place(x, "s0")


def on_device(item_table, fetch_rows, event_slot, lengths, in_weight, out_weight, out_grad):
    emb = ("e1", "e0")
    shard_rows, width = item_table.shape
    requests = fetch_rows.reshape(lax.axis_size(emb), -1)
    slots = requests.shape[0] * requests.shape[1]
    tokens = event_slot.shape[0]
    head = width // HEADS
    asked = exchange(requests, emb)
    found = item_table[asked]
    fetched = exchange(found, emb)
    rows = fetched.reshape(slots, width)
    slot_row, slot_col = event_slot.reshape(1, tokens), event_slot.reshape(tokens, 1)
    core = lax.axis_index("s0").reshape(1, 1)
    wides = [(h1 - h0) * head for h0, h1 in GROUPS]
    count = len(GROUPS)

    dgated, res = call(
        early_kernel, [((tokens, width), BF), ((slots, width), F32)], [], [VMEM] * 3, 10**9
    )(slot_row, out_weight, out_grad)
    outs = call(
        first_kernel,
        [((tokens, width), BF), ((width, 2 * width), BF), ((width, slots), BF), ((slots, width), BF)]
        + [((tokens, 3 * w), BF) for w in wides]
        + [((tokens, w), BF) for w in wides]
        + [((slots, 3 * w), BF) for w in wides],
        [
            ((slots, 4 * width), BF), ((tokens, width), BF), ((tokens, width), BF), ((BLOCK, width), F32),
            ((tokens, width), BF), ((tokens, width), BF), ((slots, width), BF),
        ],
        [SMEM] + [VMEM] * 7,
        10**10,
        32,
    )(lengths, slot_row, slot_col, rows, in_weight, out_weight, out_grad, dgated)
    layer_out, wg, nt, dpre_gate = outs[:4]
    vqk, datt, dsil = (outs[4 + k * count : 4 + (k + 1) * count] for k in range(3))

    def attention_back(i, before):
        heads = GROUPS[i][1] - GROUPS[i][0]
        grads = 3 * wides[i]
        joined = before is not None
        columns = grads + (before.shape[1] if joined else 0)
        return call(
            functools.partial(second_kernel, joined, heads),
            [((slots, grads), BF)]
            + ([((width // 2, columns), BF)] * 2 if joined else [((width, grads), BF)]),
            [((tokens, head), F32)] * (3 * heads),
            [SMEM] * 2 + [VMEM] * (5 + joined),
            10**9 * heads,
        )(lengths, core, slot_row, vqk[i], datt[i], dsil[i], nt, *([before] if joined else []))

    dpre_a, keep, give = attention_back(0, wg)
    own1, got1 = weight_sum(keep, give)
    dpre_b, wg_b = attention_back(1, None)
    dpre_c, keep, give = attention_back(2, wg_b)
    own2, got2 = weight_sum(keep, give)
    (slot_grad,) = call(slot_kernel, [((slots, width), BF)], [], [VMEM] * (4 + count), 10**9)(
        rows, res, in_weight, dpre_gate, dpre_a, dpre_b, dpre_c
    )

    returned = exchange(slot_grad.reshape(requests.shape + (width,)), emb)
    arrays, places = [returned.reshape(slots, width)], [asked.reshape(1, slots)]
    for axis in ("s1", "s0"):
        places += [other_place(p, axis) for p in places]
        arrays += [other_place(a, axis) for a in arrays]
    quarter = shard_rows // lax.axis_size(("s1", "s0"))
    base = lax.axis_index(("s1", "s0")) * quarter
    places = [p - base for p in places]
    (table_grad,) = call(
        functools.partial(table_kernel, len(places)),
        [((quarter, width), F32)],
        [],
        [VMEM] * (2 * len(places)),
        10**9,
    )(*places, *arrays)
    in_total, out_total = call(
        assemble_kernel,
        [((width, 4 * width), F32), ((width, width), F32)],
        [],
        [SMEM] + [VMEM] * 4,
        10**8,
    )(core, own1, got1, own2, got2)
    return layer_out, table_grad, in_total, out_total


def solution(mesh):
    emb, seq = mesh.shape["emb"], mesh.shape["seq"]
    fine = jax.sharding.Mesh(mesh.devices.reshape(emb // 2, 2, seq // 2, 2), AXES)
    placed = (
        P(("e1", "e0"), None),
        P(("e1", "e0"), ("s1", "s0"), None, None),
        P(AXES),
        P(AXES, None),
        P(),
        P(),
        P(AXES, None),
    )


    return jax.shard_map(
        on_device,
        mesh=fine,
        in_specs=placed,
        out_specs=(P(AXES, None), P(AXES, None), P(), P()),
        check_vma=False,
    )
```

time: 175 us -> 174 us (level)
  local copies, waits for them, and re-layouts: 14.8 us -> 22.4 us
  starting transfers between devices: 41.8 us -> 35.5 us
  waiting for transfers between devices: 44.3 us -> 41 us
  Pallas kernels: 50.9 us -> 54 us
  other arithmetic: 7.99 us -> 5.21 us
    unnamed x16 -> x72, local copies, waits for them, and re-layouts: 2.45 us -> 15.2 us
    ppermute x30 -> x22, starting transfers between devices: 34.6 us -> 28.5 us  [the longest x12 19.8 us: swap(): lax.ppermute(x, AXES, [(d, partner(d)) for d in range(lax.axis_size(AXES))])]
    ppermute x30 -> x22, waiting for transfers between devices: 38.2 us -> 33.5 us  [the longest x12 32 us: swap(): lax.ppermute(x, AXES, [(d, partner(d)) for d in range(lax.axis_size(AXES))])]
    pallas_call x3 -> x7, Pallas kernels: 45.3 us -> 49.8 us  [the longest x3 25.7 us: attention_back(): call(functools.partial(second_kernel, joined, heads), [((slots, grads), B...]
    squeeze x8 -> x4, local copies, waits for them, and re-layouts: 3.39 us -> 0.88 us  [weight_sum(): lax.dynamic_index_in_dim(halves, 1 - place(first, second), 0, keepdims=Fa...]
    sub x4, other arithmetic: 2.37 us -> 0.01 us  [on_device(): places = [p - base for p in places]]
    concatenate x1 -> x4, other arithmetic: 2.39 us -> 0.14 us  [weight_sum(): jnp.concatenate([jnp.where(upper, got, x), jnp.where(upper, x, got)], axi...]
  transfers between devices with their start and end apart: 32 -> 24, of which waited for: 14 -> 11; matrix products, arithmetic and copies ran while one was open for 7% -> 4% of each run, Pallas kernels for 29% -> 13%
where the time goes in v2:
time: 174 us; the launch traced here: 173 us
  Pallas kernels  54 us (31%)
  waiting for transfers between devices  41 us (24%)
  starting transfers between devices  35.5 us (20%)
  local copies, waits for them, and re-layouts  22.4 us (13%)
  blocking collectives  13.7 us (8%)
  other arithmetic  5.21 us (3%)
    ppermute x12, waiting for transfers between devices, swap(): lax.ppermute(x, AXES, [(d, partner(d)) for d in range(lax.axis_size(AXES))])  32 us
    pallas_call x3, Pallas kernels, attention_back(): call(functools.partial(second_kernel, joined, heads), [((slots, grads), B...  25.7 us
    ppermute x12, starting transfers between devices, swap(): lax.ppermute(x, AXES, [(d, partner(d)) for d in range(lax.axis_size(AXES))])  19.8 us
    pallas_call x1, Pallas kernels, on_device(): call(first_kernel, [((tokens, width), BF), ((width, 2 * width), BF), ((wi...  17.5 us
    unnamed x72, local copies, waits for them, and re-layouts  15.2 us
    all_to_all x1, blocking collectives, exchange(): return lax.all_to_all(x, axes, split_axis=0, concat_axis=0, tiled=True)  13.7 us
    ppermute x10, starting transfers between devices, other_place(): return lax.ppermute(x, axis, [(i, i ^ 1) for i in range(size)])  8.71 us
    all_to_all x2, waiting for transfers between devices, exchange(): return lax.all_to_all(x, axes, split_axis=0, concat_axis=0, tiled=True)  7.51 us
  transfers between devices with their start and end apart: 24, of which 11 were waited for; matrix products, arithmetic and copies ran while one was open for 4% of the time, Pallas kernels for 13%

profile of v2, /device:TPU:0, one launch (start us, length us, event | category | flops | bytes accessed | tf_op | source)
XLA Modules:
  0.0 172.8 jit_solution(9018645756836054514)
XLA Ops:
  0.6 13.7 %all_to_all.22 = s32[8,1,64]{2,1,0:T(1,128)S(1)} all-to-all(s32[8,1,64]{2,1,0:T(1,128)} %bitcast.55), channel_id=1, replica_groups=mesh['e1'=4,'e0'=2,'s1'=2,'s0'=2] {'e1','e0'}, dimensions={0} | all-to-all | bytes 4096 | tf_op jit(solution)/shard_map/all_to_all | solution.py:296
  14.4 5.4 %gather_fusion = bf16[512,512]{1,0:T(8,128)(2,1)} fusion(bf16[4096,512]{1,0:T(8,128)(2,1)} %param.7, s32[1024]{0:T(1024)S(1)} %pad_clamp_fusion), kind=kCustom, calls=%fused_computation | custom fusion | bytes 1050624 | tf_op jit(solution)/shard_map/gather | solution.py:337
  19.8 3.5 %all-to-all-start.1 = ((bf16[8,64,512]{2,1,0:T(8,128)(2,1)}), bf16[8,64,512]{2,1,0:T(8,128)(2,1)S(1)}, u32[]{:S(2)}, u32[]{:S(2)}) async-start(bf16[8,64,512]{2,1,0:T(8,128)(2,1)} %bitcast.4), calls=%async_computation.1 | async-start | bytes 1048576 | tf_op jit(solution)/shard_map/all_to_all | solution.py:296
  23.6 1.2 copy-done.13
  25.8 1.3 shard_map.102
  29.1 7.5 %all-to-all-done.1 = bf16[8,64,512]{2,1,0:T(8,128)(2,1)S(1)} async-done(((bf16[8,64,512]{2,1,0:T(8,128)(2,1)}), bf16[8,64,512]{2,1,0:T(8,128)(2,1)S(1)}, u32[]{:S(2)}, u32[]{:S(2)}) %all-to-all-start.1) | async-done | bytes 524320 | tf_op jit(solution)/shard_map/all_to_all | solution.py:296
  36.6 1.2 copy-done.14
  38.9 1.2 copy-done.25
  40.1 17.5 %shard_map.103 = (bf16[1024,512]{1,0:T(8,128)(2,1)}, bf16[512,1024]{1,0:T(8,128)(2,1)S(1)}, bf16[512,512]{1,0:T(8,128)(2,1)S(1)}, bf16[512,512]{1,0:T(8,128)(2,1...) custom-call(s32[1,8]{1,0:T(1,128)S(1)} %copy-done.17, ...), custom_call_target="tpu_custom_call" | custom-call | flops 10000000000 | bytes 10000000 | tf_op jit(solution)/shard_map/pallas_call | solution.py:348
  58.4 10.9 %shard_map.104 = (bf16[512,768]{1,0:T(8,128)(2,1)S(1)}, bf16[256,1792]{1,0:T(8,128)(2,1)S(1)}, bf16[256,1792]{1,0:T(8,128)(2,1)}) custom-call(s32[1,8]{1,0:T(1,128)S(1)} %copy-done.17, s32[1,1]{1,0:T(1,128)} %bitcast.6.core_ref, s32[1,1024]{1,0:T(1,128)S(1)} %bitcast.43, bf16[1024,768]{1,0:T(8,128)(2,1)S(1)} %get-tuple-element.33.vqk_ref, ...), custom_call_target="tpu_custom_call" | custom-call | flops 2000000000 | bytes 10000000 | tf_op jit(solution)/shard_map/pallas_call | solution.py:370
  74.3 6.9 %shard_map.105 = (bf16[512,384]{1,0:T(8,128)(2,1)S(1)}, bf16[512,384]{1,0:T(8,128)(2,1)S(1)}) custom-call(s32[1,8]{1,0:T(1,128)S(1)} %copy-done.17, s32[1,1]{1,0:T(1,128)} %bitcast.6.core_ref, s32[1,1024]{1,0:T(1,128)S(1)} %bitcast.44, bf16[1024,384]{1,0:T(8,128)(2,1)S(1)} %copy-done.23, bf16[1024,128]{1,0:T(8,128)(2,1)S(1)} %copy-done.33, ...), custom_call_target="tpu_custom_call" | custom-call | flops 1000000000 | bytes 10000000 | tf_op jit(solution)/shard_map/pallas_call | solution.py:370
  82.0 7.9 %shard_map.106 = (bf16[512,384]{1,0:T(8,128)(2,1)S(1)}, bf16[256,768]{1,0:T(8,128)(2,1)S(1)}, bf16[256,768]{1,0:T(8,128)(2,1)}) custom-call(s32[1,8]{1,0:T(1,128)S(1)} %copy-done.17, s32[1,1]{1,0:T(1,128)} %bitcast.6.core_ref, s32[1,1024]{1,0:T(1,128)S(1)} %bitcast.45, bf16[1024,384]{1,0:T(8,128)(2,1)S(1)} %copy-done.19, bf16[1024,128]{1,0:T(8,128)(2,1)S(1)} %copy-done.29, ...), custom_call_target="tpu_custom_call" | custom-call | flops 1000000000 | bytes 10000000 | tf_op jit(solution)/shard_map/pallas_call | solution.py:370
  90.4 1.4 add_convert_fusion
  93.6 1.5 collective-permute-start.7
  98.3 1.7 collective-permute-start.15
  99.9 2.5 %collective-permute-done.7 = bf16[128,1792]{1,0:T(8,128)(2,1)} collective-permute-done((bf16[128,1792]{1,0:T(8,128)(2,1)}, bf16[128,1792]{1,0:T(8,128)(2,1)}, u32[]{:S(2)}, u32[]{:S(2)}) %collective-permute-start.7) | collective-permute-done | bytes 458784 | tf_op jit(solution)/shard_map/ppermute | solution.py:300
  103.5 1.6 collective-permute-start.8
  106.0 3.6 %collective-permute-done.8 = bf16[64,1792]{1,0:T(8,128)(2,1)S(1)} collective-permute-done((bf16[64,1792]{1,0:T(8,128)(2,1)S(1)}, bf16[64,1792]{1,0:T(8,128)(2,1)S(1)}, u32[]{:S(2)}, u32[]{:S(2)}) %collective-permute-start.8) | collective-permute-done | bytes 229408 | tf_op jit(solution)/shard_map/ppermute | solution.py:300
  110.6 2.7 %shard_map.107 = bf16[512,512]{1,0:T(8,128)(2,1)} custom-call(bf16[512,512]{1,0:T(8,128)(2,1)S(1)} %bitcast.36, f32[512,512]{1,0:T(8,128)S(1)} %copy-done.2, bf16[512,2048]{1,0:T(8,128)(2,1)S(1)} %copy-done, bf16[512,512]{1,0:T(8,128)(2,1)S(1)} %copy-done.6, bf16[512,768]{1,0:T(8,128)(2,1)S(1)} %copy-done.4, bf16[512,384]{1,0:T(8,128)(2,1)S(1)} %copy-done.8, ...), custom_call_target="tpu_custom_call" | custom-call | flops 1000000000 | bytes 10000000 | tf_op jit(solution)/shard_map/pallas_call | solution.py:384
  113.3 3.5 %all-to-all-start.2 = ((bf16[8,64,512]{2,1,0:T(8,128)(2,1)}), bf16[8,64,512]{2,1,0:T(8,128)(2,1)S(1)}, u32[]{:S(2)}, u32[]{:S(2)}) async-start(bf16[8,64,512]{2,1,0:T(8,128)(2,1)} %bitcast.7), calls=%async_computation.2 | async-start | bytes 1048576 | tf_op jit(solution)/shard_map/all_to_all | solution.py:296
  116.8 2.0 %collective-permute-start.17 = (bf16[64,768]{1,0:T(8,128)(2,1)S(1)}, bf16[64,768]{1,0:T(8,128)(2,1)S(1)}, u32[]{:S(2)}, u32[]{:S(2)}) collective-permute-start(bf16[64,768]{1,0:T(8,128)(2,1)S(1)} %fusion.3), channel_id=1, source_target_pairs={{0,8},{1,17},{2,10},{3,19},{4,12},{5,21},{6,14},{7,23},{8,0},{9,25... | collective-permute-start | bytes 294920 | tf_op jit(solution)/shard_map/ppermute | solution.py:300
  118.9 2.4 %collective-permute-start.10 = (bf16[64,1792]{1,0:T(8,128)(2,1)S(1)}, bf16[64,1792]{1,0:T(8,128)(2,1)S(1)}, u32[]{:S(2)}, u32[]{:S(2)}) collective-permute-start(bf16[64,1792]{1,0:T(8,128)(2,1)S(1)} %add_convert_fusion.3), channel_id=1, source_target_pairs={{0,16},{1,9},{2,18},{3,11},{4,20},{5,13},{6,22},{7,15},{8,24},{9,1... | collective-permute-start | bytes 688136 | tf_op jit(solution)/shard_map/ppermute | solution.py:300
  121.4 7.9 %collective-permute-done.17 = bf16[64,768]{1,0:T(8,128)(2,1)S(1)} collective-permute-done((bf16[64,768]{1,0:T(8,128)(2,1)S(1)}, bf16[64,768]{1,0:T(8,128)(2,1)S(1)}, u32[]{:S(2)}, u32[]{:S(2)}) %collective-permute-start.17) | collective-permute-done | bytes 98336 | tf_op jit(solution)/shard_map/ppermute | solution.py:300
  129.3 4.2 %collective-permute-start.18 = (bf16[64,768]{1,0:T(8,128)(2,1)S(1)}, bf16[64,768]{1,0:T(8,128)(2,1)S(1)}, u32[]{:S(2)}, u32[]{:S(2)}) collective-permute-start(bf16[64,768]{1,0:T(8,128)(2,1)S(1)} %add_convert_fusion.5), channel_id=1, source_target_pairs={{0,16},{1,9},{2,18},{3,11},{4,20},{5,13},{6,22},{7,15},{8,24},{9,1... | collective-permute-start | bytes 294920 | tf_op jit(solution)/shard_map/ppermute | solution.py:300
  133.6 5.2 %collective-permute-done.10 = bf16[64,1792]{1,0:T(8,128)(2,1)S(1)} collective-permute-done((bf16[64,1792]{1,0:T(8,128)(2,1)S(1)}, bf16[64,1792]{1,0:T(8,128)(2,1)S(1)}, u32[]{:S(2)}, u32[]{:S(2)}) %collective-permute-start.10) | collective-permute-done | bytes 229408 | tf_op jit(solution)/shard_map/ppermute | solution.py:300
  141.0 6.3 %collective-permute-done.11 = bf16[64,1792]{1,0:T(8,128)(2,1)S(1)} collective-permute-done((bf16[64,1792]{1,0:T(8,128)(2,1)S(1)}, bf16[64,1792]{1,0:T(8,128)(2,1)S(1)}, u32[]{:S(2)}, u32[]{:S(2)}) %collective-permute-start.11) | collective-permute-done | bytes 229408 | tf_op jit(solution)/shard_map/ppermute | solution.py:300
  147.4 1.5 collective-permute-start.12
  151.0 5.0 %collective-permute-done.12 = bf16[128,1792]{1,0:T(8,128)(2,1)S(1)} collective-permute-done((bf16[128,1792]{1,0:T(8,128)(2,1)S(1)}, bf16[128,1792]{1,0:T(8,128)(2,1)S(1)}, u32[]{:S(2)}, u32[]{:S(2)}) %collective-permute-start.12) | collective-permute-done | bytes 458784 | tf_op jit(solution)/shard_map/ppermute | solution.py:300
  156.8 1.3 collective-permute-done.20
  158.1 5.7 %collective-permute-start.4 = (bf16[512,512]{1,0:T(8,128)(2,1)S(1)}, bf16[512,512]{1,0:T(8,128)(2,1)S(1)}, u32[]{:S(2)}, u32[]{:S(2)}) collective-permute-start(bf16[512,512]{1,0:T(8,128)(2,1)S(1)} %bitcast.38), channel_id=1, source_target_pairs={{0,1},{1,0},{2,3},{3,2},{4,5},{5,4},{6,7},{7,6},{8,9},{9,8},{10,11... | collective-permute-start | bytes 1572872 | tf_op jit(solution)/shard_map/ppermute | solution.py:292
  166.0 4.1 %shard_map.108 = f32[1024,512]{1,0:T(8,128)} custom-call(s32[1,512]{1,0:T(1,128)S(1)} %broadcast_subtract_fusion.3.refs_0_, s32[1,512]{1,0:T(1,128)S(1)} %broadcast_subtract_fusion.2.refs_1_, s32[1,512]{1,0:T(1,128)S(1)} %broadcast_subtract_fusion.1.refs_2_, s32[1,512]{1,0:T(1,128)S(1)} %broadcast_subtract_fusion.refs_3_, bf16[512,512]{1,0:T(8,128)(2,1)S(1)} %bitcast.39, ...), custom_call_target="tpu_custom_call" | custom-call | flops 1000000000 | bytes 10000000 | tf_op jit(solution)/shard_map/pallas_call | solution.py:396
  170.2 2.6 %shard_map.109 = (f32[512,2048]{1,0:T(8,128)}, f32[512,512]{1,0:T(8,128)}) custom-call(s32[1,1]{1,0:T(1,128)} %bitcast.6.core_ref, bf16[256,1792]{1,0:T(8,128)(2,1)S(1)} %pad_maximum_fusion.own1, bf16[256,1792]{1,0:T(8,128)(2,1)S(1)} %collective-permute-done.13.got1, bf16[256,768]{1,0:T(8,128)(2,1)S(1)} %pad_maximum_fusion.2.own2, ...), custom_call_target="tpu_custom_call" | custom-call | flops 100000000 | bytes 10000000 | tf_op jit(solution)/shard_map/pallas_call | solution.py:403
  (131 shorter events, 26.8 us)
Async XLA Ops:
  19.8 16.8 %all-to-all-start.1 = ((bf16[8,64,512]{2,1,0:T(8,128)(2,1)}), bf16[8,64,512]{2,1,0:T(8,128)(2,1)S(1)}, u32[]{:S(2)}, u32[]{:S(2)}) async-start(bf16[8,64,512]{2,1,0:T(8,128)(2,1)} %bitcast.4), calls=%async_computation.1 | async-start | bytes 1048576 | tf_op jit(solution)/shard_map/all_to_all | solution.py:296
  58.4 10.9 %copy-start.28 = (bf16[1024,128]{1,0:T(8,128)(2,1)}, bf16[1024,128]{1,0:T(8,128)(2,1)S(1)}, u32[]{:S(2)}) copy-start(bf16[1024,128]{1,0:T(8,128)(2,1)S(1)} %get-tuple-element.44.datt_ref) | copy-start | bytes 786436
  58.4 10.9 %copy-start.30 = (bf16[512,384]{1,0:T(8,128)(2,1)}, bf16[512,384]{1,0:T(8,128)(2,1)S(1)}, u32[]{:S(2)}) copy-start(bf16[512,384]{1,0:T(8,128)(2,1)S(1)} %get-tuple-element.41.dsil_ref) | copy-start | bytes 1179652
  58.4 10.9 %copy-start.32 = (bf16[1024,128]{1,0:T(8,128)(2,1)}, bf16[1024,128]{1,0:T(8,128)(2,1)S(1)}, u32[]{:S(2)}) copy-start(bf16[1024,128]{1,0:T(8,128)(2,1)S(1)} %get-tuple-element.40.datt_ref) | copy-start | bytes 786436
  70.2 20.2 %collective-permute-start.6 = (bf16[256,1792]{1,0:T(8,128)(2,1)}, bf16[256,1792]{1,0:T(8,128)(2,1)}, u32[]{:S(2)}, u32[]{:S(2)}) collective-permute-start(bf16[256,1792]{1,0:T(8,128)(2,1)} %get-tuple-element.49), channel_id=1, source_target_pairs={{0,1},{1,0},{2,3},{3,2},{4,5},{5,4},{6,7},{7,6},{8,9},{9,8},{10,11... | collective-permute-start | bytes 2752520 | tf_op jit(solution)/shard_map/ppermute | solution.py:292
  89.9 7.1 %collective-permute-start.14 = (bf16[256,768]{1,0:T(8,128)(2,1)}, bf16[256,768]{1,0:T(8,128)(2,1)}, u32[]{:S(2)}, u32[]{:S(2)}) collective-permute-start(bf16[256,768]{1,0:T(8,128)(2,1)} %get-tuple-element.51), channel_id=1, source_target_pairs={{0,1},{1,0},{2,3},{3,2},{4,5},{5,4},{6,7},{7,6},{8,9},{9,8},{10,11... | collective-permute-start | bytes 1179656 | tf_op jit(solution)/shard_map/ppermute | solution.py:292
  93.6 8.8 %collective-permute-start.7 = (bf16[128,1792]{1,0:T(8,128)(2,1)}, bf16[128,1792]{1,0:T(8,128)(2,1)}, u32[]{:S(2)}, u32[]{:S(2)}) collective-permute-start(bf16[128,1792]{1,0:T(8,128)(2,1)} %dynamic-slice_bitcast_fusion), channel_id=1, source_target_pairs={{0,4},{1,3},{2,6},{3,1},{4,0},{5,7},{6,2},{7,5},{8,12},{9,11},{10,... | collective-permute-start | bytes 1376264 | tf_op jit(solution)/shard_map/ppermute | solution.py:300
  96.4 67.5 %collective-permute-start.1 = (s32[1,512]{1,0:T(1,128)S(1)}, s32[1,512]{1,0:T(1,128)S(1)}, u32[]{:S(2)}, u32[]{:S(2)}) collective-permute-start(s32[1,512]{1,0:T(1,128)S(1)} %reshape.98), channel_id=1, source_target_pairs={{0,1},{1,0},{2,3},{3,2},{4,5},{5,4},{6,7},{7,6},{8,9},{9,8},{10,11... | collective-permute-start | bytes 6152 | tf_op jit(solution)/shard_map/ppermute | solution.py:292
  96.5 59.8 %collective-permute-start = (s32[1,512]{1,0:T(1,128)S(1)}, s32[1,512]{1,0:T(1,128)S(1)}, u32[]{:S(2)}, u32[]{:S(2)}) collective-permute-start(s32[1,512]{1,0:T(1,128)S(1)} %reshape.98), channel_id=1, source_target_pairs={{0,2},{2,0},{1,3},{3,1},{4,6},{6,4},{5,7},{7,5},{8,10},{10,8},{9,1... | collective-permute-start | bytes 6152 | tf_op jit(solution)/shard_map/ppermute | solution.py:292
  98.2 12.3 %copy-start.2 = (f32[512,512]{1,0:T(8,128)S(1)}, f32[512,512]{1,0:T(8,128)}, u32[]{:S(2)}) copy-start(f32[512,512]{1,0:T(8,128)} %copy-done.1) | copy-start | bytes 3145732
  98.2 12.3 %copy-start.4 = (bf16[512,768]{1,0:T(8,128)(2,1)S(1)}, bf16[512,768]{1,0:T(8,128)(2,1)}, u32[]{:S(2)}) copy-start(bf16[512,768]{1,0:T(8,128)(2,1)} %copy-done.3) | copy-start | bytes 2359300
  98.2 12.3 %copy-start.6 = (bf16[512,512]{1,0:T(8,128)(2,1)S(1)}, bf16[512,512]{1,0:T(8,128)(2,1)}, u32[]{:S(2)}) copy-start(bf16[512,512]{1,0:T(8,128)(2,1)} %copy-done.5) | copy-start | bytes 1572868
  98.2 12.3 %copy-start.8 = (bf16[512,384]{1,0:T(8,128)(2,1)S(1)}, bf16[512,384]{1,0:T(8,128)(2,1)}, u32[]{:S(2)}) copy-start(bf16[512,384]{1,0:T(8,128)(2,1)} %copy-done.7) | copy-start | bytes 1179652
  98.2 12.3 %copy-start.10 = (bf16[512,384]{1,0:T(8,128)(2,1)S(1)}, bf16[512,384]{1,0:T(8,128)(2,1)}, u32[]{:S(2)}) copy-start(bf16[512,384]{1,0:T(8,128)(2,1)} %copy-done.9) | copy-start | bytes 1179652
  98.3 6.9 %collective-permute-start.15 = (bf16[128,768]{1,0:T(8,128)(2,1)S(1)}, bf16[128,768]{1,0:T(8,128)(2,1)S(1)}, u32[]{:S(2)}, u32[]{:S(2)}) collective-permute-start(bf16[128,768]{1,0:T(8,128)(2,1)S(1)} %dynamic-slice_bitcast_fusion.2), channel_id=1, source_target_pairs={{0,4},{1,3},{2,6},{3,1},{4,0},{5,7},{6,2},{7,5},{8,12},{9,11},{10,... | collective-permute-start | bytes 589832 | tf_op jit(solution)/shard_map/ppermute | solution.py:300
  103.5 6.1 %collective-permute-start.8 = (bf16[64,1792]{1,0:T(8,128)(2,1)S(1)}, bf16[64,1792]{1,0:T(8,128)(2,1)S(1)}, u32[]{:S(2)}, u32[]{:S(2)}) collective-permute-start(bf16[64,1792]{1,0:T(8,128)(2,1)S(1)} %dynamic-slice_bitcast_fusion.1), channel_id=1, source_target_pairs={{0,2},{1,5},{2,0},{3,7},{4,6},{5,1},{6,4},{7,3},{8,10},{9,13},{10,... | collective-permute-start | bytes 688136 | tf_op jit(solution)/shard_map/ppermute | solution.py:300
  105.2 11.6 %collective-permute-start.16 = (bf16[64,768]{1,0:T(8,128)(2,1)S(1)}, bf16[64,768]{1,0:T(8,128)(2,1)S(1)}, u32[]{:S(2)}, u32[]{:S(2)}) collective-permute-start(bf16[64,768]{1,0:T(8,128)(2,1)S(1)} %dynamic-slice_bitcast_fusion.3), channel_id=1, source_target_pairs={{0,2},{1,5},{2,0},{3,7},{4,6},{5,1},{6,4},{7,3},{8,10},{9,13},{10,... | collective-permute-start | bytes 294920 | tf_op jit(solution)/shard_map/ppermute | solution.py:300
  109.7 9.2 %collective-permute-start.9 = (bf16[64,1792]{1,0:T(8,128)(2,1)S(1)}, bf16[64,1792]{1,0:T(8,128)(2,1)S(1)}, u32[]{:S(2)}, u32[]{:S(2)}) collective-permute-start(bf16[64,1792]{1,0:T(8,128)(2,1)S(1)} %fusion.1), channel_id=1, source_target_pairs={{0,8},{1,17},{2,10},{3,19},{4,12},{5,21},{6,14},{7,23},{8,0},{9,25... | collective-permute-start | bytes 688136 | tf_op jit(solution)/shard_map/ppermute | solution.py:300
  113.3 35.6 %all-to-all-start.2 = ((bf16[8,64,512]{2,1,0:T(8,128)(2,1)}), bf16[8,64,512]{2,1,0:T(8,128)(2,1)S(1)}, u32[]{:S(2)}, u32[]{:S(2)}) async-start(bf16[8,64,512]{2,1,0:T(8,128)(2,1)} %bitcast.7), calls=%async_computation.2 | async-start | bytes 1048576 | tf_op jit(solution)/shard_map/all_to_all | solution.py:296
  116.8 12.5 %collective-permute-start.17 = (bf16[64,768]{1,0:T(8,128)(2,1)S(1)}, bf16[64,768]{1,0:T(8,128)(2,1)S(1)}, u32[]{:S(2)}, u32[]{:S(2)}) collective-permute-start(bf16[64,768]{1,0:T(8,128)(2,1)S(1)} %fusion.3), channel_id=1, source_target_pairs={{0,8},{1,17},{2,10},{3,19},{4,12},{5,21},{6,14},{7,23},{8,0},{9,25... | collective-permute-start | bytes 294920 | tf_op jit(solution)/shard_map/ppermute | solution.py:300
  118.9 19.8 %collective-permute-start.10 = (bf16[64,1792]{1,0:T(8,128)(2,1)S(1)}, bf16[64,1792]{1,0:T(8,128)(2,1)S(1)}, u32[]{:S(2)}, u32[]{:S(2)}) collective-permute-start(bf16[64,1792]{1,0:T(8,128)(2,1)S(1)} %add_convert_fusion.3), channel_id=1, source_target_pairs={{0,16},{1,9},{2,18},{3,11},{4,20},{5,13},{6,22},{7,15},{8,24},{9,1... | collective-permute-start | bytes 688136 | tf_op jit(solution)/shard_map/ppermute | solution.py:300
  129.3 10.5 %collective-permute-start.18 = (bf16[64,768]{1,0:T(8,128)(2,1)S(1)}, bf16[64,768]{1,0:T(8,128)(2,1)S(1)}, u32[]{:S(2)}, u32[]{:S(2)}) collective-permute-start(bf16[64,768]{1,0:T(8,128)(2,1)S(1)} %add_convert_fusion.5), channel_id=1, source_target_pairs={{0,16},{1,9},{2,18},{3,11},{4,20},{5,13},{6,22},{7,15},{8,24},{9,1... | collective-permute-start | bytes 294920 | tf_op jit(solution)/shard_map/ppermute | solution.py:300
  138.8 8.5 %collective-permute-start.11 = (bf16[64,1792]{1,0:T(8,128)(2,1)S(1)}, bf16[64,1792]{1,0:T(8,128)(2,1)S(1)}, u32[]{:S(2)}, u32[]{:S(2)}) collective-permute-start(bf16[64,1792]{1,0:T(8,128)(2,1)S(1)} %add_convert_fusion.2), channel_id=1, source_target_pairs={{0,2},{1,5},{2,0},{3,7},{4,6},{5,1},{6,4},{7,3},{8,10},{9,13},{10,... | collective-permute-start | bytes 688136 | tf_op jit(solution)/shard_map/ppermute | solution.py:300
  139.8 9.9 %collective-permute-start.19 = (bf16[64,768]{1,0:T(8,128)(2,1)S(1)}, bf16[64,768]{1,0:T(8,128)(2,1)S(1)}, u32[]{:S(2)}, u32[]{:S(2)}) collective-permute-start(bf16[64,768]{1,0:T(8,128)(2,1)S(1)} %add_convert_fusion.4), channel_id=1, source_target_pairs={{0,2},{1,5},{2,0},{3,7},{4,6},{5,1},{6,4},{7,3},{8,10},{9,13},{10,... | collective-permute-start | bytes 294920 | tf_op jit(solution)/shard_map/ppermute | solution.py:300
  147.4 8.5 %collective-permute-start.12 = (bf16[128,1792]{1,0:T(8,128)(2,1)S(1)}, bf16[128,1792]{1,0:T(8,128)(2,1)S(1)}, u32[]{:S(2)}, u32[]{:S(2)}) collective-permute-start(bf16[128,1792]{1,0:T(8,128)(2,1)S(1)} %pad_maximum_fusion.1), channel_id=1, source_target_pairs={{0,4},{1,3},{2,6},{3,1},{4,0},{5,7},{6,2},{7,5},{8,12},{9,11},{10,... | collective-permute-start | bytes 1376264 | tf_op jit(solution)/shard_map/ppermute | solution.py:300
  148.9 14.9 %collective-permute-start.3 = (bf16[512,512]{1,0:T(8,128)(2,1)S(1)}, bf16[512,512]{1,0:T(8,128)(2,1)S(1)}, u32[]{:S(2)}, u32[]{:S(2)}) collective-permute-start(bf16[512,512]{1,0:T(8,128)(2,1)S(1)} %bitcast.37), channel_id=1, source_target_pairs={{0,2},{2,0},{1,3},{3,1},{4,6},{6,4},{5,7},{7,5},{8,10},{10,8},{9,1... | collective-permute-start | bytes 1572872 | tf_op jit(solution)/shard_map/ppermute | solution.py:292
  149.8 8.3 %collective-permute-start.20 = (bf16[128,768]{1,0:T(8,128)(2,1)S(1)}, bf16[128,768]{1,0:T(8,128)(2,1)S(1)}, u32[]{:S(2)}, u32[]{:S(2)}) collective-permute-start(bf16[128,768]{1,0:T(8,128)(2,1)S(1)} %pad_maximum_fusion.3), channel_id=1, source_target_pairs={{0,4},{1,3},{2,6},{3,1},{4,0},{5,7},{6,2},{7,5},{8,12},{9,11},{10,... | collective-permute-start | bytes 589832 | tf_op jit(solution)/shard_map/ppermute | solution.py:300
  156.2 14.0 %collective-permute-start.13 = (bf16[256,1792]{1,0:T(8,128)(2,1)S(1)}, bf16[256,1792]{1,0:T(8,128)(2,1)S(1)}, u32[]{:S(2)}, u32[]{:S(2)}) collective-permute-start(bf16[256,1792]{1,0:T(8,128)(2,1)S(1)} %pad_maximum_fusion.own1), channel_id=1, source_target_pairs={{0,1},{1,0},{2,3},{3,2},{4,5},{5,4},{6,7},{7,6},{8,9},{9,8},{10,11... | collective-permute-start | bytes 2752520 | tf_op jit(solution)/shard_map/ppermute | solution.py:292
  156.3 8.2 %collective-permute-start.2 = (s32[1,512]{1,0:T(1,128)S(1)}, s32[1,512]{1,0:T(1,128)S(1)}, u32[]{:S(2)}, u32[]{:S(2)}) collective-permute-start(s32[1,512]{1,0:T(1,128)S(1)} %collective-permute-done), channel_id=1, source_target_pairs={{0,1},{1,0},{2,3},{3,2},{4,5},{5,4},{6,7},{7,6},{8,9},{9,8},{10,11... | collective-permute-start | bytes 6152 | tf_op jit(solution)/shard_map/ppermute | solution.py:292
  158.1 7.2 %collective-permute-start.4 = (bf16[512,512]{1,0:T(8,128)(2,1)S(1)}, bf16[512,512]{1,0:T(8,128)(2,1)S(1)}, u32[]{:S(2)}, u32[]{:S(2)}) collective-permute-start(bf16[512,512]{1,0:T(8,128)(2,1)S(1)} %bitcast.38), channel_id=1, source_target_pairs={{0,1},{1,0},{2,3},{3,2},{4,5},{5,4},{6,7},{7,6},{8,9},{9,8},{10,11... | collective-permute-start | bytes 1572872 | tf_op jit(solution)/shard_map/ppermute | solution.py:292
  163.8 2.2 %collective-permute-start.5 = (bf16[512,512]{1,0:T(8,128)(2,1)S(1)}, bf16[512,512]{1,0:T(8,128)(2,1)S(1)}, u32[]{:S(2)}, u32[]{:S(2)}) collective-permute-start(bf16[512,512]{1,0:T(8,128)(2,1)S(1)} %collective-permute-done.3.refs_5_), channel_id=1, source_target_pairs={{0,1},{1,0},{2,3},{3,2},{4,5},{5,4},{6,7},{7,6},{8,9},{9,8},{10,11... | collective-permute-start | bytes 1572872 | tf_op jit(solution)/shard_map/ppermute | solution.py:292
  163.9 6.2 %collective-permute-start.21 = (bf16[256,768]{1,0:T(8,128)(2,1)S(1)}, bf16[256,768]{1,0:T(8,128)(2,1)S(1)}, u32[]{:S(2)}, u32[]{:S(2)}) collective-permute-start(bf16[256,768]{1,0:T(8,128)(2,1)S(1)} %pad_maximum_fusion.2.own2), channel_id=1, source_target_pairs={{0,1},{1,0},{2,3},{3,2},{4,5},{5,4},{6,7},{7,6},{8,9},{9,8},{10,11... | collective-permute-start | bytes 1179656 | tf_op jit(solution)/shard_map/ppermute | solution.py:292
  (28 other events, 128.3 us)

commit v3 on v2

--- a/solution.py
+++ b/solution.py
@@ -12,7 +12,8 @@
 MOST = 512
 EPS = 1e-05
 BLOCK = 256
-GROUPS = ((0, 2), (2, 3), (3, 4))
+MIB = 56
+GROUPS = ((0, HEADS),)
 VMEM = pl.BlockSpec(memory_space=pltpu.VMEM)
 SMEM = pl.BlockSpec(memory_space=pltpu.SMEM)
 BF = jnp.bfloat16
@@ -160,11 +161,9 @@
     wg_ref[:, width:] = mm(nt_ref[...], dpre).astype(BF)
 
 
-def second_kernel(joined, heads, len_ref, core_ref, slot_row, vqk_ref, datt_ref, dsil_ref, nt_ref, *refs):
-    before = refs[0] if joined else None
-    refs = refs[1:] if joined else refs
-    outs = 3 if joined else 2
-    dpre_ref, sums = refs[0], refs[outs:]
+def second_kernel(
+    heads, len_ref, core_ref, slot_row, vqk_ref, datt_ref, dsil_ref, nt_ref, dpre_ref, keep_ref, give_ref, *sums
+):
     slots = dpre_ref.shape[0]
     tokens, wide = datt_ref.shape
     head = wide // heads
@@ -214,15 +213,10 @@
         cols = slice(j * wide, (j + 1) * wide)
         slot_sum = mm(put, jnp.concatenate(parts, axis=1) if heads > 1 else parts[0])
         dpre_ref[:, cols] = (slot_sum * dsil_ref[:, cols].astype(F32)).astype(BF)
-    if not joined:
-        refs[1][...] = mm(nt_ref[...], dpre_ref[...]).astype(BF)
-        return
     half = nt_ref.shape[0] // 2
-    offset = before.shape[1]
-    for ref, place in ((refs[1], core_ref[0, 0]), (refs[2], 1 - core_ref[0, 0])):
+    for ref, place in ((keep_ref, core_ref[0, 0]), (give_ref, 1 - core_ref[0, 0])):
         span = pl.ds(pl.multiple_of(place * half, half), half)
-        ref[:, :offset] = before[span, :]
-        ref[:, offset:] = mm(nt_ref[span, :], dpre_ref[...]).astype(BF)
+        ref[...] = mm(nt_ref[span, :], dpre_ref[...]).astype(BF)
 
 
 def slot_kernel(rows_ref, res_ref, win_ref, gate_ref, *refs):
@@ -239,22 +233,14 @@
     grad_ref[...] = (center_back(dn, normed, inverse) + res_ref[...]).astype(BF)
 
 
-def assemble_kernel(core_ref, own1, got1, own2, got2, in_ref, out_ref):
+def assemble_kernel(core_ref, early, own, got, in_ref, out_ref):
     width = out_ref.shape[1]
-    head = width // HEADS
-    half = own1.shape[0]
-    pieces = [(0, 0, out_ref, 0, width), (0, width, in_ref, 0, width)]
-    at = [2 * width, 0]
-    for i, (h0, h1) in enumerate(GROUPS):
-        chain = 0 if i == 0 else 1
-        for j in range(3):
-            wide = (h1 - h0) * head
-            pieces.append((chain, at[chain], in_ref, (j + 1) * width + h0 * head, wide))
-            at[chain] += wide
-    for sources, place in (((own1, own2), core_ref[0, 0]), ((got1, got2), 1 - core_ref[0, 0])):
+    half = own.shape[0]
+    out_ref[...] = early[:, :width].astype(F32)
+    in_ref[:, :width] = early[:, width:].astype(F32)
+    for source, place in ((own, core_ref[0, 0]), (got, 1 - core_ref[0, 0])):
         span = pl.ds(pl.multiple_of(place * half, half), half)
-        for chain, source, ref, target, wide in pieces:
-            ref[span, target : target + wide] = sources[chain][:, source : source + wide].astype(F32)
+        in_ref[span, width:] = source[...].astype(F32)
 
 
 def table_kernel(count, *refs):
@@ -357,32 +343,28 @@
         ],
         [SMEM] + [VMEM] * 7,
         10**10,
-        32,
+        MIB,
     )(lengths, slot_row, slot_col, rows, in_weight, out_weight, out_grad, dgated)
     layer_out, wg, nt, dpre_gate = outs[:4]
     vqk, datt, dsil = (outs[4 + k * count : 4 + (k + 1) * count] for k in range(3))
 
-    def attention_back(i, before):
-        heads = GROUPS[i][1] - GROUPS[i][0]
-        grads = 3 * wides[i]
-        joined = before is not None
-        columns = grads + (before.shape[1] if joined else 0)
-        return call(
-            functools.partial(second_kernel, joined, heads),
-            [((slots, grads), BF)]
-            + ([((width // 2, columns), BF)] * 2 if joined else [((width, grads), BF)]),
-            [((tokens, head), F32)] * (3 * heads),
-            [SMEM] * 2 + [VMEM] * (5 + joined),
-            10**9 * heads,
-        )(lengths, core, slot_row, vqk[i], datt[i], dsil[i], nt, *([before] if joined else []))
-
-    dpre_a, keep, give = attention_back(0, wg)
-    own1, got1 = weight_sum(keep, give)
-    dpre_b, wg_b = attention_back(1, None)
-    dpre_c, keep, give = attention_back(2, wg_b)
-    own2, got2 = weight_sum(keep, give)
+    heads, grads = HEADS, 3 * width
+    dpre, keep, give = call(
+        functools.partial(second_kernel, heads),
+        [((slots, grads), BF)] + [((width // 2, grads), BF)] * 2,
+        [((tokens, head), F32)] * (3 * heads),
+        [SMEM] * 2 + [VMEM] * 5,
+        10**10,
+        MIB,
+    )(lengths, core, slot_row, vqk[0], datt[0], dsil[0], nt)
+    total = lax.axis_size(AXES)
+    early = exchange(wg.reshape(total, width // total, 2 * width), AXES)
+    early = jnp.sum(early.astype(F32), axis=0).astype(BF)
+    early = jnp.broadcast_to(early[None], (total,) + early.shape)
+    early = exchange(early, AXES).reshape(width, 2 * width)
+    own, got = weight_sum(keep, give)
     (slot_grad,) = call(slot_kernel, [((slots, width), BF)], [], [VMEM] * (4 + count), 10**9)(
-        rows, res, in_weight, dpre_gate, dpre_a, dpre_b, dpre_c
+        rows, res, in_weight, dpre_gate, dpre
     )
 
     returned = exchange(slot_grad.reshape(requests.shape + (width,)), emb)
@@ -404,9 +386,9 @@
         assemble_kernel,
         [((width, 4 * width), F32), ((width, width), F32)],
         [],
-        [SMEM] + [VMEM] * 4,
+        [SMEM] + [VMEM] * 3,
         10**8,
-    )(core, own1, got1, own2, got2)
+    )(core, early, own, got)
     return layer_out, table_grad, in_total, out_total
 
 

time: 174 us -> 194 us (1.11)
  waiting for transfers between devices: 41 us -> 76.8 us
  local copies, waits for them, and re-layouts: 22.4 us -> 13.1 us
  Pallas kernels: 54 us -> 51.3 us
  starting transfers between devices: 35.5 us -> 32.8 us
    ppermute x10 -> x8, waiting for transfers between devices: 1.53 us -> 26 us  [other_place(): return lax.ppermute(x, axis, [(i, i ^ 1) for i in range(size)])]
    unnamed x72 -> x22, local copies, waits for them, and re-layouts: 15.2 us -> 4.19 us
    all_to_all x2 -> x4, starting transfers between devices: 6.99 us -> 17.5 us  [exchange(): return lax.all_to_all(x, axes, split_axis=0, concat_axis=0, tiled=True)]
    all_to_all x2 -> x4, waiting for transfers between devices: 7.51 us -> 16.8 us  [exchange(): return lax.all_to_all(x, axes, split_axis=0, concat_axis=0, tiled=True)]
    ppermute x12 -> x6, starting transfers between devices: 19.8 us -> 12.3 us  [swap(): lax.ppermute(x, AXES, [(d, partner(d)) for d in range(lax.axis_size(AXES))])]
    ppermute x10 -> x8, starting transfers between devices: 8.71 us -> 2.98 us  [other_place(): return lax.ppermute(x, axis, [(i, i ^ 1) for i in range(size)])]
    pallas_call x3 -> x1, Pallas kernels: 25.7 us -> 20.1 us  [on_device(): call(functools.partial(second_kernel, heads), [((slots, grads), BF)] + [(...]
    pallas_call x1, Pallas kernels: 17.5 us -> 20.8 us  [on_device(): call(first_kernel, [((tokens, width), BF), ((width, 2 * width), BF), ((wi...]
  transfers between devices with their start and end apart: 24 -> 18, of which waited for: 11 -> 10; matrix products, arithmetic and copies ran while one was open for 4% -> 3% of each run, Pallas kernels for 13% -> 4%
where the time goes in v3:
time: 194 us; the launch traced here: 193 us
  waiting for transfers between devices  76.8 us (40%)
  Pallas kernels  51.3 us (26%)
  starting transfers between devices  32.8 us (17%)
  blocking collectives  13.7 us (7%)
  local copies, waits for them, and re-layouts  13.1 us (7%)
  other arithmetic  4.8 us (2%)
    ppermute x6, waiting for transfers between devices, swap(): lax.ppermute(x, AXES, [(d, partner(d)) for d in range(lax.axis_size(AXES))])  34 us
    ppermute x8, waiting for transfers between devices, other_place(): return lax.ppermute(x, axis, [(i, i ^ 1) for i in range(size)])  26 us
    pallas_call x1, Pallas kernels, on_device(): call(first_kernel, [((tokens, width), BF), ((width, 2 * width), BF), ((wi...  20.8 us
    pallas_call x1, Pallas kernels, on_device(): call(functools.partial(second_kernel, heads), [((slots, grads), BF)] + [(...  20.1 us
    all_to_all x4, starting transfers between devices, exchange(): return lax.all_to_all(x, axes, split_axis=0, concat_axis=0, tiled=True)  17.5 us
    all_to_all x4, waiting for transfers between devices, exchange(): return lax.all_to_all(x, axes, split_axis=0, concat_axis=0, tiled=True)  16.8 us
    all_to_all x1, blocking collectives, exchange(): return lax.all_to_all(x, axes, split_axis=0, concat_axis=0, tiled=True)  13.7 us
    ppermute x6, starting transfers between devices, swap(): lax.ppermute(x, AXES, [(d, partner(d)) for d in range(lax.axis_size(AXES))])  12.3 us
  transfers between devices with their start and end apart: 18, of which 10 were waited for; matrix products, arithmetic and copies ran while one was open for 3% of the time, Pallas kernels for 4%

profile of v3, /device:TPU:0, one launch (start us, length us, event | category | flops | bytes accessed | tf_op | source)
XLA Modules:
  0.0 193.4 jit_solution(10844409849465977418)
XLA Ops:
  0.6 13.7 %all_to_all.32 = s32[8,1,64]{2,1,0:T(1,128)S(1)} all-to-all(s32[8,1,64]{2,1,0:T(1,128)} %bitcast.41), channel_id=1, replica_groups=mesh['e1'=4,'e0'=2,'s1'=2,'s0'=2] {'e1','e0'}, dimensions={0} | all-to-all | bytes 4096 | tf_op jit(solution)/shard_map/all_to_all | solution.py:282
  14.4 5.4 %gather_fusion = bf16[512,512]{1,0:T(8,128)(2,1)} fusion(bf16[4096,512]{1,0:T(8,128)(2,1)} %param.7, s32[1024]{0:T(1024)S(1)} %pad_clamp_fusion), kind=kCustom, calls=%fused_computation | custom fusion | bytes 1050624 | tf_op jit(solution)/shard_map/gather | solution.py:323
  19.8 3.6 %all-to-all-start.1 = ((bf16[8,64,512]{2,1,0:T(8,128)(2,1)}), bf16[8,64,512]{2,1,0:T(8,128)(2,1)S(1)}, u32[]{:S(2)}, u32[]{:S(2)}) async-start(bf16[8,64,512]{2,1,0:T(8,128)(2,1)} %bitcast.4), calls=%async_computation.1 | async-start | bytes 1048576 | tf_op jit(solution)/shard_map/all_to_all | solution.py:282
  23.5 1.0 copy.12.slot_col
  24.5 1.3 shard_map.102
  27.8 8.9 %all-to-all-done.1 = bf16[8,64,512]{2,1,0:T(8,128)(2,1)S(1)} async-done(((bf16[8,64,512]{2,1,0:T(8,128)(2,1)}), bf16[8,64,512]{2,1,0:T(8,128)(2,1)S(1)}, u32[]{:S(2)}, u32[]{:S(2)}) %all-to-all-start.1) | async-done | bytes 524320 | tf_op jit(solution)/shard_map/all_to_all | solution.py:282
  37.5 20.8 %shard_map.103 = (bf16[1024,512]{1,0:T(8,128)(2,1)}, bf16[512,1024]{1,0:T(8,128)(2,1)}, bf16[512,512]{1,0:T(8,128)(2,1)}, bf16[512,512]{1,0:T(8,128)(2,1)}, bf16...) custom-call(s32[1,8]{1,0:T(1,128)} %len_ref.3, s32[1,1024]{1,0:T(1,128)} %bitcast.31, ...), custom_call_target="tpu_custom_call" | custom-call | flops 10000000000 | bytes 10000000 | tf_op jit(solution)/shard_map/pallas_call | solution.py:334
  58.4 20.1 %shard_map.104 = (bf16[512,1536]{1,0:T(8,128)(2,1)}, bf16[256,1536]{1,0:T(8,128)(2,1)}, bf16[256,1536]{1,0:T(8,128)(2,1)}) custom-call(s32[1,8]{1,0:T(1,128)} %len_ref.3, s32[1,1]{1,0:T(1,128)} %bitcast.6.core_ref, s32[1,1024]{1,0:T(1,128)} %bitcast.32, bf16[1024,1536]{1,0:T(8,128)(2,1)} %get-tuple-element.22.vqk_ref, ...), custom_call_target="tpu_custom_call" | custom-call | flops 10000000000 | bytes 10000000 | tf_op jit(solution)/shard_map/pallas_call | solution.py:352
  78.5 2.5 %collective-permute-done.6 = bf16[256,1536]{1,0:T(8,128)(2,1)S(1)} collective-permute-done((bf16[256,1536]{1,0:T(8,128)(2,1)}, bf16[256,1536]{1,0:T(8,128)(2,1)S(1)}, u32[]{:S(2)}, u32[]{:S(2)}) %collective-permute-start.6) | collective-permute-done | bytes 786464 | tf_op jit(solution)/shard_map/ppermute | solution.py:278
  81.0 1.3 add_convert_fusion
  82.4 1.5 collective-permute-start.7
  83.9 6.3 %collective-permute-done.7 = bf16[128,1536]{1,0:T(8,128)(2,1)S(1)} collective-permute-done((bf16[128,1536]{1,0:T(8,128)(2,1)S(1)}, bf16[128,1536]{1,0:T(8,128)(2,1)S(1)}, u32[]{:S(2)}, u32[]{:S(2)}) %collective-permute-start.7) | collective-permute-done | bytes 393248 | tf_op jit(solution)/shard_map/ppermute | solution.py:286
  91.0 1.5 collective-permute-start.8
  92.5 3.7 %all-to-all-start.3 = ((bf16[32,16,1024]{2,1,0:T(8,128)(2,1)}), bf16[32,16,1024]{2,1,0:T(8,128)(2,1)}, u32[]{:S(2)}, u32[]{:S(2)}) async-start(bf16[32,16,1024]{2,1,0:T(8,128)(2,1)} %bitcast.39), calls=%async_computation.3 | async-start | bytes 2097152 | tf_op jit(solution)/shard_map/all_to_all | solution.py:282
  98.9 18.8 %collective-permute-done.9 = bf16[64,1536]{1,0:T(8,128)(2,1)S(1)} collective-permute-done((bf16[64,1536]{1,0:T(8,128)(2,1)S(1)}, bf16[64,1536]{1,0:T(8,128)(2,1)S(1)}, u32[]{:S(2)}, u32[]{:S(2)}) %collective-permute-start.9) | collective-permute-done | bytes 196640 | tf_op jit(solution)/shard_map/ppermute | solution.py:286
  117.7 4.7 %collective-permute-start.10 = (bf16[64,1536]{1,0:T(8,128)(2,1)S(1)}, bf16[64,1536]{1,0:T(8,128)(2,1)S(1)}, u32[]{:S(2)}, u32[]{:S(2)}) collective-permute-start(bf16[64,1536]{1,0:T(8,128)(2,1)S(1)} %add_convert_fusion.2), channel_id=1, source_target_pairs={{0,16},{1,9},{2,18},{3,11},{4,20},{5,13},{6,22},{7,15},{8,24},{9,1... | collective-permute-start | bytes 589832 | tf_op jit(solution)/shard_map/ppermute | solution.py:286
  122.4 8.2 %collective-permute-done.10 = bf16[64,1536]{1,0:T(8,128)(2,1)S(1)} collective-permute-done((bf16[64,1536]{1,0:T(8,128)(2,1)S(1)}, bf16[64,1536]{1,0:T(8,128)(2,1)S(1)}, u32[]{:S(2)}, u32[]{:S(2)}) %collective-permute-start.10) | collective-permute-done | bytes 196640 | tf_op jit(solution)/shard_map/ppermute | solution.py:286
  130.6 1.6 collective-permute-start.11
  132.2 1.4 copy-done.3
  133.6 2.3 %shard_map.105 = bf16[512,512]{1,0:T(8,128)(2,1)} custom-call(bf16[512,512]{1,0:T(8,128)(2,1)S(1)} %bitcast.27, f32[512,512]{1,0:T(8,128)S(1)} %copy-done.5, bf16[512,2048]{1,0:T(8,128)(2,1)S(1)} %copy-done, bf16[512,512]{1,0:T(8,128)(2,1)S(1)} %copy-done.6, bf16[512,1536]{1,0:T(8,128)(2,1)S(1)} %copy-done.3), custom_call_target="tpu_custom_call" | custom-call | flops 1000000000 | bytes 10000000 | tf_op jit(solution)/shard_map/pallas_call | solution.py:366
  135.9 3.5 %all-to-all-start.2 = ((bf16[8,64,512]{2,1,0:T(8,128)(2,1)}), bf16[8,64,512]{2,1,0:T(8,128)(2,1)S(1)}, u32[]{:S(2)}, u32[]{:S(2)}) async-start(bf16[8,64,512]{2,1,0:T(8,128)(2,1)} %bitcast.7), calls=%async_computation.2 | async-start | bytes 1048576 | tf_op jit(solution)/shard_map/all_to_all | solution.py:282
  139.5 2.1 %collective-permute-start.12 = (bf16[128,1536]{1,0:T(8,128)(2,1)S(1)}, bf16[128,1536]{1,0:T(8,128)(2,1)S(1)}, u32[]{:S(2)}, u32[]{:S(2)}) collective-permute-start(bf16[128,1536]{1,0:T(8,128)(2,1)S(1)} %pad_maximum_fusion.1), channel_id=1, source_target_pairs={{0,4},{1,3},{2,6},{3,1},{4,0},{5,7},{6,2},{7,5},{8,12},{9,11},{10,... | collective-permute-start | bytes 1179656 | tf_op jit(solution)/shard_map/ppermute | solution.py:286
  141.6 1.4 reduce_sum.12
  143.0 7.9 %all-to-all-done.2 = bf16[8,64,512]{2,1,0:T(8,128)(2,1)S(1)} async-done(((bf16[8,64,512]{2,1,0:T(8,128)(2,1)}), bf16[8,64,512]{2,1,0:T(8,128)(2,1)S(1)}, u32[]{:S(2)}, u32[]{:S(2)}) %all-to-all-start.2) | async-done | bytes 524320 | tf_op jit(solution)/shard_map/all_to_all | solution.py:282
  150.9 1.1 broadcast_in_dim.2
  152.0 6.7 %all-to-all-start.4 = ((bf16[32,16,1024]{2,1,0:T(8,128)(2,1)}), bf16[32,16,1024]{2,1,0:T(8,128)(2,1)S(1)}, u32[]{:S(2)}, u32[]{:S(2)}) async-start(bf16[32,16,1024]{2,1,0:T(8,128)(2,1)} %broadcast_in_dim.2), calls=%async_computation.4 | async-start | bytes 2097152 | tf_op jit(solution)/shard_map/all_to_all | solution.py:282
  159.9 1.8 collective-permute-start
  162.5 1.0 collective-permute-done
  164.0 20.7 %collective-permute-done.3.refs_5_ = bf16[512,512]{1,0:T(8,128)(2,1)S(1)} collective-permute-done((bf16[512,512]{1,0:T(8,128)(2,1)S(1)}, bf16[512,512]{1,0:T(8,128)(2,1)S(1)}, u32[]{:S(2)}, u32[]{:S(2)}) %collective-permute-start.3) | collective-permute-done | bytes 524320 | tf_op jit(solution)/shard_map/ppermute | solution.py:278
  184.9 1.7 collective-permute-done.5.refs_7_
  186.7 4.1 %shard_map.106 = f32[1024,512]{1,0:T(8,128)} custom-call(s32[1,512]{1,0:T(1,128)S(1)} %broadcast_subtract_fusion.3.refs_0_, s32[1,512]{1,0:T(1,128)S(1)} %broadcast_subtract_fusion.2.refs_1_, s32[1,512]{1,0:T(1,128)S(1)} %broadcast_subtract_fusion.1.refs_2_, s32[1,512]{1,0:T(1,128)S(1)} %broadcast_subtract_fusion.refs_3_, bf16[512,512]{1,0:T(8,128)(2,1)S(1)} %bitcast.30, ...), custom_call_target="tpu_custom_call" | custom-call | flops 1000000000 | bytes 10000000 | tf_op jit(solution)/shard_map/pallas_call | solution.py:378
  190.8 2.6 %shard_map.107 = (f32[512,2048]{1,0:T(8,128)}, f32[512,512]{1,0:T(8,128)}) custom-call(s32[1,1]{1,0:T(1,128)} %bitcast.6.core_ref, bf16[512,1024]{1,0:T(8,128)(2,1)S(1)} %bitcast.25, bf16[256,1536]{1,0:T(8,128)(2,1)S(1)} %pad_maximum_fusion.own, bf16[256,1536]{1,0:T(8,128)(2,1)S(1)} %collective-permute-done.13.got), custom_call_target="tpu_custom_call" | custom-call | flops 100000000 | bytes 10000000 | tf_op jit(solution)/shard_map/pallas_call | solution.py:385
  (58 shorter events, 9.2 us)
Async XLA Ops:
  14.4 9.0 %copy-start.7 = (s32[1024]{0:T(1024)S(1)}, s32[1024]{0:T(1024)}, u32[]{:S(2)}) copy-start(s32[1024]{0:T(1024)} %param.9) | copy-start | bytes 12292
  19.8 4.7 %copy-start.8 = (bf16[1024,512]{1,0:T(8,128)(2,1)S(1)}, bf16[1024,512]{1,0:T(8,128)(2,1)}, u32[]{:S(2)}) copy-start(bf16[1024,512]{1,0:T(8,128)(2,1)} %og_ref.3) | copy-start | bytes 3145732
  19.8 4.7 %copy-start.9 = (bf16[512,512]{1,0:T(8,128)(2,1)S(1)}, bf16[512,512]{1,0:T(8,128)(2,1)}, u32[]{:S(2)}) copy-start(bf16[512,512]{1,0:T(8,128)(2,1)} %wout_ref.3) | copy-start | bytes 1572868
  19.8 16.9 %all-to-all-start.1 = ((bf16[8,64,512]{2,1,0:T(8,128)(2,1)}), bf16[8,64,512]{2,1,0:T(8,128)(2,1)S(1)}, u32[]{:S(2)}, u32[]{:S(2)}) async-start(bf16[8,64,512]{2,1,0:T(8,128)(2,1)} %bitcast.4), calls=%async_computation.1 | async-start | bytes 1048576 | tf_op jit(solution)/shard_map/all_to_all | solution.py:282
  25.8 1.0 copy-start.4
  26.8 1.0 copy-start.10
  36.7 0.8 copy-start.1
  78.5 2.5 %collective-permute-start.6 = (bf16[256,1536]{1,0:T(8,128)(2,1)}, bf16[256,1536]{1,0:T(8,128)(2,1)S(1)}, u32[]{:S(2)}, u32[]{:S(2)}) collective-permute-start(bf16[256,1536]{1,0:T(8,128)(2,1)} %get-tuple-element.29), channel_id=1, source_target_pairs={{0,1},{1,0},{2,3},{3,2},{4,5},{5,4},{6,7},{7,6},{8,9},{9,8},{10,11... | collective-permute-start | bytes 2359304 | tf_op jit(solution)/shard_map/ppermute | solution.py:278
  82.4 7.8 %collective-permute-start.7 = (bf16[128,1536]{1,0:T(8,128)(2,1)S(1)}, bf16[128,1536]{1,0:T(8,128)(2,1)S(1)}, u32[]{:S(2)}, u32[]{:S(2)}) collective-permute-start(bf16[128,1536]{1,0:T(8,128)(2,1)S(1)} %dynamic-slice_bitcast_fusion), channel_id=1, source_target_pairs={{0,4},{1,3},{2,6},{3,1},{4,0},{5,7},{6,2},{7,5},{8,12},{9,11},{10,... | collective-permute-start | bytes 1179656 | tf_op jit(solution)/shard_map/ppermute | solution.py:286
  90.3 41.9 %copy-start.6 = (bf16[512,512]{1,0:T(8,128)(2,1)S(1)}, bf16[512,512]{1,0:T(8,128)(2,1)}, u32[]{:S(2)}) copy-start(bf16[512,512]{1,0:T(8,128)(2,1)} %get-tuple-element.21.gate_ref) | copy-start | bytes 1572868
  91.0 6.0 %collective-permute-start.8 = (bf16[64,1536]{1,0:T(8,128)(2,1)}, bf16[64,1536]{1,0:T(8,128)(2,1)}, u32[]{:S(2)}, u32[]{:S(2)}) collective-permute-start(bf16[64,1536]{1,0:T(8,128)(2,1)} %dynamic-slice_bitcast_fusion.1), channel_id=1, source_target_pairs={{0,2},{1,5},{2,0},{3,7},{4,6},{5,1},{6,4},{7,3},{8,10},{9,13},{10,... | collective-permute-start | bytes 589832 | tf_op jit(solution)/shard_map/ppermute | solution.py:286
  92.5 39.7 %copy-start = (bf16[512,2048]{1,0:T(8,128)(2,1)S(1)}, bf16[512,2048]{1,0:T(8,128)(2,1)}, u32[]{:S(2)}) copy-start(bf16[512,2048]{1,0:T(8,128)(2,1)} %win_ref.3) | copy-start | bytes 6291460
  92.5 39.7 %copy-start.2 = (bf16[8,64,512]{2,1,0:T(8,128)(2,1)S(1)}, bf16[8,64,512]{2,1,0:T(8,128)(2,1)}, u32[]{:S(2)}) copy-start(bf16[8,64,512]{2,1,0:T(8,128)(2,1)} %copy-done.1) | copy-start | bytes 1572868
  92.5 43.4 %all-to-all-start.3 = ((bf16[32,16,1024]{2,1,0:T(8,128)(2,1)}), bf16[32,16,1024]{2,1,0:T(8,128)(2,1)}, u32[]{:S(2)}, u32[]{:S(2)}) async-start(bf16[32,16,1024]{2,1,0:T(8,128)(2,1)} %bitcast.39), calls=%async_computation.3 | async-start | bytes 2097152 | tf_op jit(solution)/shard_map/all_to_all | solution.py:282
  96.3 35.9 %copy-start.5 = (f32[512,512]{1,0:T(8,128)S(1)}, f32[512,512]{1,0:T(8,128)}, u32[]{:S(2)}) copy-start(f32[512,512]{1,0:T(8,128)} %copy-done.4) | copy-start | bytes 3145732
  98.0 19.7 %collective-permute-start.9 = (bf16[64,1536]{1,0:T(8,128)(2,1)S(1)}, bf16[64,1536]{1,0:T(8,128)(2,1)S(1)}, u32[]{:S(2)}, u32[]{:S(2)}) collective-permute-start(bf16[64,1536]{1,0:T(8,128)(2,1)S(1)} %fusion.1), channel_id=1, source_target_pairs={{0,8},{1,17},{2,10},{3,19},{4,12},{5,21},{6,14},{7,23},{8,0},{9,25... | collective-permute-start | bytes 589832 | tf_op jit(solution)/shard_map/ppermute | solution.py:286
  117.7 12.9 %collective-permute-start.10 = (bf16[64,1536]{1,0:T(8,128)(2,1)S(1)}, bf16[64,1536]{1,0:T(8,128)(2,1)S(1)}, u32[]{:S(2)}, u32[]{:S(2)}) collective-permute-start(bf16[64,1536]{1,0:T(8,128)(2,1)S(1)} %add_convert_fusion.2), channel_id=1, source_target_pairs={{0,16},{1,9},{2,18},{3,11},{4,20},{5,13},{6,22},{7,15},{8,24},{9,1... | collective-permute-start | bytes 589832 | tf_op jit(solution)/shard_map/ppermute | solution.py:286
  130.6 8.8 %collective-permute-start.11 = (bf16[64,1536]{1,0:T(8,128)(2,1)S(1)}, bf16[64,1536]{1,0:T(8,128)(2,1)S(1)}, u32[]{:S(2)}, u32[]{:S(2)}) collective-permute-start(bf16[64,1536]{1,0:T(8,128)(2,1)S(1)} %add_convert_fusion.1), channel_id=1, source_target_pairs={{0,2},{1,5},{2,0},{3,7},{4,6},{5,1},{6,4},{7,3},{8,10},{9,13},{10,... | collective-permute-start | bytes 589832 | tf_op jit(solution)/shard_map/ppermute | solution.py:286
  132.2 1.4 copy-start.3
  135.9 15.0 %all-to-all-start.2 = ((bf16[8,64,512]{2,1,0:T(8,128)(2,1)}), bf16[8,64,512]{2,1,0:T(8,128)(2,1)S(1)}, u32[]{:S(2)}, u32[]{:S(2)}) async-start(bf16[8,64,512]{2,1,0:T(8,128)(2,1)} %bitcast.7), calls=%async_computation.2 | async-start | bytes 1048576 | tf_op jit(solution)/shard_map/all_to_all | solution.py:282
  139.5 22.4 %collective-permute-start.12 = (bf16[128,1536]{1,0:T(8,128)(2,1)S(1)}, bf16[128,1536]{1,0:T(8,128)(2,1)S(1)}, u32[]{:S(2)}, u32[]{:S(2)}) collective-permute-start(bf16[128,1536]{1,0:T(8,128)(2,1)S(1)} %pad_maximum_fusion.1), channel_id=1, source_target_pairs={{0,4},{1,3},{2,6},{3,1},{4,0},{5,7},{6,2},{7,5},{8,12},{9,11},{10,... | collective-permute-start | bytes 1179656 | tf_op jit(solution)/shard_map/ppermute | solution.py:286
  152.0 38.8 %all-to-all-start.4 = ((bf16[32,16,1024]{2,1,0:T(8,128)(2,1)}), bf16[32,16,1024]{2,1,0:T(8,128)(2,1)S(1)}, u32[]{:S(2)}, u32[]{:S(2)}) async-start(bf16[32,16,1024]{2,1,0:T(8,128)(2,1)} %broadcast_in_dim.2), calls=%async_computation.4 | async-start | bytes 2097152 | tf_op jit(solution)/shard_map/all_to_all | solution.py:282
  159.9 3.6 %collective-permute-start = (s32[1,512]{1,0:T(1,128)S(1)}, s32[1,512]{1,0:T(1,128)S(1)}, u32[]{:S(2)}, u32[]{:S(2)}) collective-permute-start(s32[1,512]{1,0:T(1,128)S(1)} %reshape.95), channel_id=1, source_target_pairs={{0,2},{2,0},{1,3},{3,1},{4,6},{6,4},{5,7},{7,5},{8,10},{10,8},{9,1... | collective-permute-start | bytes 6152 | tf_op jit(solution)/shard_map/ppermute | solution.py:278
  161.7 23.2 %collective-permute-start.1 = (s32[1,512]{1,0:T(1,128)S(1)}, s32[1,512]{1,0:T(1,128)S(1)}, u32[]{:S(2)}, u32[]{:S(2)}) collective-permute-start(s32[1,512]{1,0:T(1,128)S(1)} %reshape.95), channel_id=1, source_target_pairs={{0,1},{1,0},{2,3},{3,2},{4,5},{5,4},{6,7},{7,6},{8,9},{9,8},{10,11... | collective-permute-start | bytes 6152 | tf_op jit(solution)/shard_map/ppermute | solution.py:278
  161.7 23.0 %collective-permute-start.3 = (bf16[512,512]{1,0:T(8,128)(2,1)S(1)}, bf16[512,512]{1,0:T(8,128)(2,1)S(1)}, u32[]{:S(2)}, u32[]{:S(2)}) collective-permute-start(bf16[512,512]{1,0:T(8,128)(2,1)S(1)} %bitcast.28), channel_id=1, source_target_pairs={{0,2},{2,0},{1,3},{3,1},{4,6},{6,4},{5,7},{7,5},{8,10},{10,8},{9,1... | collective-permute-start | bytes 1572872 | tf_op jit(solution)/shard_map/ppermute | solution.py:278
  162.2 28.6 %collective-permute-start.13 = (bf16[256,1536]{1,0:T(8,128)(2,1)S(1)}, bf16[256,1536]{1,0:T(8,128)(2,1)S(1)}, u32[]{:S(2)}, u32[]{:S(2)}) collective-permute-start(bf16[256,1536]{1,0:T(8,128)(2,1)S(1)} %pad_maximum_fusion.own), channel_id=1, source_target_pairs={{0,1},{1,0},{2,3},{3,2},{4,5},{5,4},{6,7},{7,6},{8,9},{9,8},{10,11... | collective-permute-start | bytes 2359304 | tf_op jit(solution)/shard_map/ppermute | solution.py:278
  163.5 21.4 %collective-permute-start.2 = (s32[1,512]{1,0:T(1,128)S(1)}, s32[1,512]{1,0:T(1,128)S(1)}, u32[]{:S(2)}, u32[]{:S(2)}) collective-permute-start(s32[1,512]{1,0:T(1,128)S(1)} %collective-permute-done), channel_id=1, source_target_pairs={{0,1},{1,0},{2,3},{3,2},{4,5},{5,4},{6,7},{7,6},{8,9},{9,8},{10,11... | collective-permute-start | bytes 6152 | tf_op jit(solution)/shard_map/ppermute | solution.py:278
  163.5 21.4 %collective-permute-start.4 = (bf16[512,512]{1,0:T(8,128)(2,1)S(1)}, bf16[512,512]{1,0:T(8,128)(2,1)S(1)}, u32[]{:S(2)}, u32[]{:S(2)}) collective-permute-start(bf16[512,512]{1,0:T(8,128)(2,1)S(1)} %bitcast.29), channel_id=1, source_target_pairs={{0,1},{1,0},{2,3},{3,2},{4,5},{5,4},{6,7},{7,6},{8,9},{9,8},{10,11... | collective-permute-start | bytes 1572872 | tf_op jit(solution)/shard_map/ppermute | solution.py:278
  184.7 1.9 collective-permute-start.5

commit v4 on v3

--- a/solution.py
+++ b/solution.py
@@ -73,7 +73,13 @@
     res_ref[...] = mm(one_hot_rows(slot_row, slots), og_ref[...])
 
 
-def first_kernel(len_ref, slot_row, slot_col, rows_ref, win_ref, wout_ref, og_ref, dgated_ref, *refs):
+def blocks(ref, order, cols, value):
+    rows = value.shape[0] // len(order)
+    for i, block in enumerate(order):
+        ref[i * rows : (i + 1) * rows, cols] = value[block * rows : (block + 1) * rows, :]
+
+
+def first_kernel(order, len_ref, slot_row, slot_col, rows_ref, win_ref, wout_ref, og_ref, dgated_ref, *refs):
     count = len(GROUPS)
     out_ref, wg_ref, nt_ref, dpre_ref = refs[:4]
     vqk, datt, dsil = (refs[4 + k * count : 4 + (k + 1) * count] for k in range(3))
@@ -154,11 +160,11 @@
         return 0
 
     lax.fori_loop(0, tokens // BLOCK, rows_step, 0)
-    wg_ref[:, :width] = tt_mm(gated[...], og_ref[...]).astype(BF)
+    blocks(wg_ref, order, slice(0, width), tt_mm(gated[...], og_ref[...]).astype(BF))
     slot_sum = mm(one_hot_rows(slot_row, slots), dgate[...])
     dpre = (slot_sum * dsil_gate[...].astype(F32)).astype(BF)
     dpre_ref[...] = dpre
-    wg_ref[:, width:] = mm(nt_ref[...], dpre).astype(BF)
+    blocks(wg_ref, order, slice(width, 2 * width), mm(nt_ref[...], dpre).astype(BF))
 
 
 def second_kernel(
@@ -233,14 +239,13 @@
     grad_ref[...] = (center_back(dn, normed, inverse) + res_ref[...]).astype(BF)
 
 
-def assemble_kernel(core_ref, early, own, got, in_ref, out_ref):
+def assemble_kernel(core_ref, own, got, in_ref, out_ref):
     width = out_ref.shape[1]
     half = own.shape[0]
-    out_ref[...] = early[:, :width].astype(F32)
-    in_ref[:, :width] = early[:, width:].astype(F32)
     for source, place in ((own, core_ref[0, 0]), (got, 1 - core_ref[0, 0])):
         span = pl.ds(pl.multiple_of(place * half, half), half)
-        in_ref[span, width:] = source[...].astype(F32)
+        out_ref[span, :] = source[:, :width].astype(F32)
+        in_ref[span, :] = source[:, width:].astype(F32)
 
 
 def table_kernel(count, *refs):
@@ -261,7 +266,7 @@
     lax.fori_loop(0, out.shape[0] // height, step, 0)
 
 
-def call(kernel, outs, scratch, specs, flops, mib=24):
+def call(kernel, outs, scratch, specs, flops, mib=MIB):
     return pl.pallas_call(
         kernel,
         out_shape=[jax.ShapeDtypeStruct(s, d) for s, d in outs],
@@ -286,29 +291,44 @@
     return lax.ppermute(x, AXES, [(d, partner(d)) for d in range(lax.axis_size(AXES))])
 
 
-def weight_sum(keep, give):
-    seq_bits = lax.axis_size(("s1", "s0")).bit_length() - 1
-    all_bits = lax.axis_size(AXES).bit_length() - 1
+def block_order():
+    line = lax.axis_size("e1")
+    order = []
+    for d in range(lax.axis_size(AXES)):
+        core, near, far = d & 1, (d >> 1) & 1, (d >> 2) & 1
+        first, second = (near, far) if core else (far, near)
+        order.append(((core * 2 + first) * 2 + second) * line + (d >> 3))
+    return order
+
+
+def weight_sum(early, keep, give):
+    total, line = lax.axis_size(AXES), lax.axis_size("e1")
     me = lax.axis_index(AXES)
-    one, two = min(1, seq_bits), seq_bits
-    line = [k for k in range(all_bits) if k not in (0, one, two)]
+    early = exchange(early.reshape(total, early.shape[0] // total, early.shape[1]), AXES)
+    early = jnp.sum(early.astype(F32), axis=0).astype(BF)
+    early = exchange(jnp.broadcast_to(early[None], (line,) + early.shape), ("e1",))
+    early = early.reshape(-1, early.shape[-1])
+
     by_core = lambda first, second: (lambda d: d ^ (1 << (second if d & 1 else first)))
-    place = lambda first, second: (me >> jnp.where(me & 1 == 1, second, first)) & 1
+    upper = lambda first, second: (me >> jnp.where(me & 1 == 1, second, first)) & 1
     got = other_place(give, "s0")
     x = (keep.astype(F32) + got.astype(F32)).astype(BF)
-    for first, second in ((two, one), (one, two)):
+    for first, second in ((2, 1), (1, 2)):
         halves = x.reshape(2, x.shape[0] // 2, x.shape[1])
-        mine = lax.dynamic_index_in_dim(halves, place(first, second), 0, keepdims=False)
-        give = lax.dynamic_index_in_dim(halves, 1 - place(first, second), 0, keepdims=False)
+        place = upper(first, second)
+        mine = lax.dynamic_index_in_dim(halves, place, 0, keepdims=False)
+        give = lax.dynamic_index_in_dim(halves, 1 - place, 0, keepdims=False)
         got = swap(give, by_core(first, second))
         x = (mine.astype(F32) + got.astype(F32)).astype(BF)
-    for first, second in zip(line, line[::-1]):
+    bits = range(3, total.bit_length() - 1)
+    for first, second in zip(bits, bits[::-1]):
         got = swap(x, by_core(first, second))
         x = (x.astype(F32) + got.astype(F32)).astype(BF)
-    for first, second in ((one, two), (two, one)):
+    x = jnp.concatenate([early, x], axis=1)
+    for first, second in ((1, 2), (2, 1)):
         got = swap(x, by_core(first, second))
-        upper = place(first, second) == 1
-        x = jnp.concatenate([jnp.where(upper, got, x), jnp.where(upper, x, got)], axis=0)
+        place = upper(first, second) == 1
+        x = jnp.concatenate([jnp.where(place, got, x), jnp.where(place, x, got)], axis=0)
     return x, other_place(x, "s0")
 
 
@@ -331,8 +351,8 @@
     dgated, res = call(
         early_kernel, [((tokens, width), BF), ((slots, width), F32)], [], [VMEM] * 3, 10**9
     )(slot_row, out_weight, out_grad)
-    outs = call(
-        first_kernel,
+    first = call(
+        functools.partial(first_kernel, block_order()),
         [((tokens, width), BF), ((width, 2 * width), BF), ((width, slots), BF), ((slots, width), BF)]
         + [((tokens, 3 * w), BF) for w in wides]
         + [((tokens, w), BF) for w in wides]
@@ -343,8 +363,8 @@
         ],
         [SMEM] + [VMEM] * 7,
         10**10,
-        MIB,
-    )(lengths, slot_row, slot_col, rows, in_weight, out_weight, out_grad, dgated)
+    )
+    outs = first(lengths, slot_row, slot_col, rows, in_weight, out_weight, out_grad, dgated)
     layer_out, wg, nt, dpre_gate = outs[:4]
     vqk, datt, dsil = (outs[4 + k * count : 4 + (k + 1) * count] for k in range(3))
 
@@ -355,14 +375,8 @@
         [((tokens, head), F32)] * (3 * heads),
         [SMEM] * 2 + [VMEM] * 5,
         10**10,
-        MIB,
     )(lengths, core, slot_row, vqk[0], datt[0], dsil[0], nt)
-    total = lax.axis_size(AXES)
-    early = exchange(wg.reshape(total, width // total, 2 * width), AXES)
-    early = jnp.sum(early.astype(F32), axis=0).astype(BF)
-    early = jnp.broadcast_to(early[None], (total,) + early.shape)
-    early = exchange(early, AXES).reshape(width, 2 * width)
-    own, got = weight_sum(keep, give)
+    own, got = weight_sum(wg, keep, give)
     (slot_grad,) = call(slot_kernel, [((slots, width), BF)], [], [VMEM] * (4 + count), 10**9)(
         rows, res, in_weight, dpre_gate, dpre
     )
@@ -386,9 +400,9 @@
         assemble_kernel,
         [((width, 4 * width), F32), ((width, width), F32)],
         [],
-        [SMEM] + [VMEM] * 3,
+        [SMEM] + [VMEM] * 2,
         10**8,
-    )(core, early, own, got)
+    )(core, own, got)
     return layer_out, table_grad, in_total, out_total
 
 

time: 194 us -> 191 us (0.985)
  Pallas kernels: 51.3 us -> 59.6 us
  starting transfers between devices: 32.8 us -> 25.5 us
  waiting for transfers between devices: 76.8 us -> 74.3 us
    all_to_all x4, waiting for transfers between devices: 16.8 us -> 33.4 us  [exchange(): return lax.all_to_all(x, axes, split_axis=0, concat_axis=0, tiled=True)]
    ppermute x8, waiting for transfers between devices: 26 us -> 12.9 us  [other_place(): return lax.ppermute(x, axis, [(i, i ^ 1) for i in range(size)])]
    ppermute x6, waiting for transfers between devices: 34 us -> 28 us  [swap(): lax.ppermute(x, AXES, [(d, partner(d)) for d in range(lax.axis_size(AXES))])]
    all_to_all x4, starting transfers between devices: 17.5 us -> 13.3 us  [exchange(): return lax.all_to_all(x, axes, split_axis=0, concat_axis=0, tiled=True)]
    ppermute x6, starting transfers between devices: 12.3 us -> 8.98 us  [swap(): lax.ppermute(x, AXES, [(d, partner(d)) for d in range(lax.axis_size(AXES))])]
    pallas_call x1, Pallas kernels: 2.34 us -> 5.01 us  [on_device(): call(slot_kernel, [((slots, width), BF)], [], [VMEM] * (4 + count), 10 ** 9)]
    pallas_call x1, Pallas kernels: 1.28 us -> 3.68 us  [on_device(): call(early_kernel, [((tokens, width), BF), ((slots, width), F32)], [], [V...]
    sub x4, other arithmetic: 0.01 us -> 2.36 us  [on_device(): places = [p - base for p in places]]
  transfers between devices with their start and end apart: 18 -> 18, of which waited for: 10 -> 12; matrix products, arithmetic and copies ran while one was open for 3% -> 3% of each run, Pallas kernels for 4% -> 8%
where the time goes in v4:
time: 191 us; the launch traced here: 190 us
  waiting for transfers between devices  74.3 us (39%)
  Pallas kernels  59.6 us (31%)
  starting transfers between devices  25.5 us (13%)
  blocking collectives  13.7 us (7%)
  local copies, waits for them, and re-layouts  11.3 us (6%)
  other arithmetic  5.23 us (3%)
    all_to_all x4, waiting for transfers between devices, exchange(): return lax.all_to_all(x, axes, split_axis=0, concat_axis=0, tiled=True)  33.4 us
    ppermute x6, waiting for transfers between devices, swap(): lax.ppermute(x, AXES, [(d, partner(d)) for d in range(lax.axis_size(AXES))])  28 us
    pallas_call x1, Pallas kernels, on_device(): first(lengths, slot_row, slot_col, rows, in_weight, out_weight, out_grad,...  20.8 us
    pallas_call x1, Pallas kernels, on_device(): call(functools.partial(second_kernel, heads), [((slots, grads), BF)] + [(...  20.1 us
    all_to_all x1, blocking collectives, exchange(): return lax.all_to_all(x, axes, split_axis=0, concat_axis=0, tiled=True)  13.7 us
    all_to_all x4, starting transfers between devices, exchange(): return lax.all_to_all(x, axes, split_axis=0, concat_axis=0, tiled=True)  13.3 us
    ppermute x8, waiting for transfers between devices, other_place(): return lax.ppermute(x, axis, [(i, i ^ 1) for i in range(size)])  12.9 us
    ppermute x6, starting transfers between devices, swap(): lax.ppermute(x, AXES, [(d, partner(d)) for d in range(lax.axis_size(AXES))])  8.98 us
  transfers between devices with their start and end apart: 18, of which 12 were waited for; matrix products, arithmetic and copies ran while one was open for 3% of the time, Pallas kernels for 8%

profile of v4, /device:TPU:0, one launch (start us, length us, event | category | flops | bytes accessed | tf_op | source)
XLA Modules:
  0.0 190.4 jit_solution(5595612675619905085)
XLA Ops:
  0.6 13.7 %all_to_all.32 = s32[8,1,64]{2,1,0:T(1,128)S(1)} all-to-all(s32[8,1,64]{2,1,0:T(1,128)} %bitcast.42), channel_id=1, replica_groups=mesh['e1'=4,'e0'=2,'s1'=2,'s0'=2] {'e1','e0'}, dimensions={0} | all-to-all | bytes 4096 | tf_op jit(solution)/shard_map/all_to_all | solution.py:287
  14.4 5.4 %gather_fusion = bf16[512,512]{1,0:T(8,128)(2,1)} fusion(bf16[4096,512]{1,0:T(8,128)(2,1)} %param.7, s32[1024]{0:T(1024)S(1)} %pad_clamp_fusion), kind=kCustom, calls=%fused_computation | custom fusion | bytes 1050624 | tf_op jit(solution)/shard_map/gather | solution.py:343
  19.8 3.5 %all-to-all-start.1 = ((bf16[8,64,512]{2,1,0:T(8,128)(2,1)}), bf16[8,64,512]{2,1,0:T(8,128)(2,1)S(1)}, u32[]{:S(2)}, u32[]{:S(2)}) async-start(bf16[8,64,512]{2,1,0:T(8,128)(2,1)} %bitcast.4), calls=%async_computation.1 | async-start | bytes 1048576 | tf_op jit(solution)/shard_map/all_to_all | solution.py:287
  23.3 1.0 copy.12.slot_col
  24.4 3.7 %shard_map.102 = (bf16[1024,512]{1,0:T(8,128)(2,1)}, f32[512,512]{1,0:T(8,128)}) custom-call(s32[1,1024]{1,0:T(1,128)} %bitcast.38, bf16[512,512]{1,0:T(8,128)(2,1)} %wout_ref.3, bf16[1024,512]{1,0:T(8,128)(2,1)} %og_ref.3), custom_call_target="tpu_custom_call" | custom-call | flops 1000000000 | bytes 10000000 | tf_op jit(solution)/shard_map/pallas_call | solution.py:351
  28.1 8.5 %all-to-all-done.1 = bf16[8,64,512]{2,1,0:T(8,128)(2,1)S(1)} async-done(((bf16[8,64,512]{2,1,0:T(8,128)(2,1)}), bf16[8,64,512]{2,1,0:T(8,128)(2,1)S(1)}, u32[]{:S(2)}, u32[]{:S(2)}) %all-to-all-start.1) | async-done | bytes 524320 | tf_op jit(solution)/shard_map/all_to_all | solution.py:287
  36.6 0.8 copy-done.1
  37.4 20.8 %shard_map.103 = (bf16[1024,512]{1,0:T(8,128)(2,1)}, bf16[512,1024]{1,0:T(8,128)(2,1)}, bf16[512,512]{1,0:T(8,128)(2,1)}, bf16[512,512]{1,0:T(8,128)(2,1)}, bf16...) custom-call(s32[1,8]{1,0:T(1,128)} %len_ref.3, s32[1,1024]{1,0:T(1,128)} %bitcast.39, ...), custom_call_target="tpu_custom_call" | custom-call | flops 10000000000 | bytes 10000000 | tf_op jit(solution)/shard_map/pallas_call | solution.py:367
  58.2 20.1 %shard_map.104 = (bf16[512,1536]{1,0:T(8,128)(2,1)}, bf16[256,1536]{1,0:T(8,128)(2,1)}, bf16[256,1536]{1,0:T(8,128)(2,1)}) custom-call(s32[1,8]{1,0:T(1,128)} %len_ref.3, s32[1,1]{1,0:T(1,128)} %bitcast.6.core_ref, s32[1,1024]{1,0:T(1,128)} %bitcast.40, bf16[1024,1536]{1,0:T(8,128)(2,1)} %get-tuple-element.22.vqk_ref, ...), custom_call_target="tpu_custom_call" | custom-call | flops 10000000000 | bytes 10000000 | tf_op jit(solution)/shard_map/pallas_call | solution.py:372
  78.3 2.5 %collective-permute-done.6 = bf16[256,1536]{1,0:T(8,128)(2,1)S(1)} collective-permute-done((bf16[256,1536]{1,0:T(8,128)(2,1)}, bf16[256,1536]{1,0:T(8,128)(2,1)S(1)}, u32[]{:S(2)}, u32[]{:S(2)}) %collective-permute-start.6) | collective-permute-done | bytes 786464 | tf_op jit(solution)/shard_map/ppermute | solution.py:283
  80.8 1.3 add_convert_fusion
  82.2 1.5 collective-permute-start.7
  83.7 2.8 %all-to-all-start.3 = ((bf16[32,16,1024]{2,1,0:T(8,128)(2,1)}), bf16[32,16,1024]{2,1,0:T(8,128)(2,1)S(1)}, u32[]{:S(2)}, u32[]{:S(2)}) async-start(bf16[32,16,1024]{2,1,0:T(8,128)(2,1)} %bitcast.9), calls=%async_computation.3 | async-start | bytes 2097152 | tf_op jit(solution)/shard_map/all_to_all | solution.py:287
  86.5 7.3 %collective-permute-done.7 = bf16[128,1536]{1,0:T(8,128)(2,1)S(1)} collective-permute-done((bf16[128,1536]{1,0:T(8,128)(2,1)S(1)}, bf16[128,1536]{1,0:T(8,128)(2,1)S(1)}, u32[]{:S(2)}, u32[]{:S(2)}) %collective-permute-start.7) | collective-permute-done | bytes 393248 | tf_op jit(solution)/shard_map/ppermute | solution.py:291
  94.1 7.5 %collective-permute-done.8 = bf16[64,1536]{1,0:T(8,128)(2,1)S(1)} collective-permute-done((bf16[64,1536]{1,0:T(8,128)(2,1)S(1)}, bf16[64,1536]{1,0:T(8,128)(2,1)S(1)}, u32[]{:S(2)}, u32[]{:S(2)}) %collective-permute-start.8) | collective-permute-done | bytes 196640 | tf_op jit(solution)/shard_map/ppermute | solution.py:291
  101.6 7.1 %collective-permute-done.9 = bf16[64,1536]{1,0:T(8,128)(2,1)S(1)} collective-permute-done((bf16[64,1536]{1,0:T(8,128)(2,1)S(1)}, bf16[64,1536]{1,0:T(8,128)(2,1)S(1)}, u32[]{:S(2)}, u32[]{:S(2)}) %collective-permute-start.9) | collective-permute-done | bytes 196640 | tf_op jit(solution)/shard_map/ppermute | solution.py:291
  108.8 4.2 %collective-permute-start.10 = (bf16[64,1536]{1,0:T(8,128)(2,1)S(1)}, bf16[64,1536]{1,0:T(8,128)(2,1)S(1)}, u32[]{:S(2)}, u32[]{:S(2)}) collective-permute-start(bf16[64,1536]{1,0:T(8,128)(2,1)S(1)} %add_convert_fusion.2), channel_id=1, source_target_pairs={{0,16},{1,9},{2,18},{3,11},{4,20},{5,13},{6,22},{7,15},{8,24},{9,1... | collective-permute-start | bytes 589832 | tf_op jit(solution)/shard_map/ppermute | solution.py:291
  113.0 4.6 %all-to-all-done.3 = bf16[32,16,1024]{2,1,0:T(8,128)(2,1)S(1)} async-done(((bf16[32,16,1024]{2,1,0:T(8,128)(2,1)}), bf16[32,16,1024]{2,1,0:T(8,128)(2,1)S(1)}, u32[]{:S(2)}, u32[]{:S(2)}) %all-to-all-start.3) | async-done | bytes 1048608 | tf_op jit(solution)/shard_map/all_to_all | solution.py:287
  118.4 3.5 %all-to-all-start.4 = ((bf16[4,16,1024]{2,1,0:T(8,128)(2,1)}), bf16[4,16,1024]{2,1,0:T(8,128)(2,1)S(1)}, u32[]{:S(2)}, u32[]{:S(2)}) async-start(bf16[4,16,1024]{2,1,0:T(8,128)(2,1)} %broadcast_in_dim.2), calls=%async_computation.4 | async-start | bytes 262144 | tf_op jit(solution)/shard_map/all_to_all | solution.py:287
  121.9 5.6 %all-to-all-done.4 = bf16[4,16,1024]{2,1,0:T(8,128)(2,1)S(1)} async-done(((bf16[4,16,1024]{2,1,0:T(8,128)(2,1)}), bf16[4,16,1024]{2,1,0:T(8,128)(2,1)S(1)}, u32[]{:S(2)}, u32[]{:S(2)}) %all-to-all-start.4) | async-done | bytes 131104 | tf_op jit(solution)/shard_map/all_to_all | solution.py:287
  127.6 1.5 collective-permute-start.11
  129.2 5.6 %collective-permute-done.11 = bf16[64,2560]{1,0:T(8,128)(2,1)S(1)} collective-permute-done((bf16[64,2560]{1,0:T(8,128)(2,1)S(1)}, bf16[64,2560]{1,0:T(8,128)(2,1)S(1)}, u32[]{:S(2)}, u32[]{:S(2)}) %collective-permute-start.11) | collective-permute-done | bytes 327712 | tf_op jit(solution)/shard_map/ppermute | solution.py:291
  134.9 1.5 collective-permute-start.12
  136.5 5.0 %shard_map.105 = bf16[512,512]{1,0:T(8,128)(2,1)} custom-call(bf16[512,512]{1,0:T(8,128)(2,1)} %bitcast.28, f32[512,512]{1,0:T(8,128)} %get-tuple-element.20.res_ref, bf16[512,2048]{1,0:T(8,128)(2,1)} %win_ref.3, bf16[512,512]{1,0:T(8,128)(2,1)} %get-tuple-element.21.gate_ref, bf16[512,1536]{1,0:T(8,128)(2,1)} %get-tuple-element.26.refs_0_), custom_call_target="tpu_custom_call" | custom-call | flops 1000000000 | bytes 10000000 | tf_op jit(solution)/shard_map/pallas_call | solution.py:380
  141.5 3.5 %all-to-all-start.2 = ((bf16[8,64,512]{2,1,0:T(8,128)(2,1)}), bf16[8,64,512]{2,1,0:T(8,128)(2,1)S(1)}, u32[]{:S(2)}, u32[]{:S(2)}) async-start(bf16[8,64,512]{2,1,0:T(8,128)(2,1)} %bitcast.29), calls=%async_computation.2 | async-start | bytes 1048576 | tf_op jit(solution)/shard_map/all_to_all | solution.py:287
  146.3 14.7 %all-to-all-done.2 = bf16[8,64,512]{2,1,0:T(8,128)(2,1)S(1)} async-done(((bf16[8,64,512]{2,1,0:T(8,128)(2,1)}), bf16[8,64,512]{2,1,0:T(8,128)(2,1)S(1)}, u32[]{:S(2)}, u32[]{:S(2)}) %all-to-all-start.2) | async-done | bytes 524320 | tf_op jit(solution)/shard_map/all_to_all | solution.py:287
  162.7 1.7 collective-permute-start
  165.1 10.0 %collective-permute-done.3.refs_5_ = bf16[512,512]{1,0:T(8,128)(2,1)} collective-permute-done((bf16[512,512]{1,0:T(8,128)(2,1)S(1)}, bf16[512,512]{1,0:T(8,128)(2,1)}, u32[]{:S(2)}, u32[]{:S(2)}) %collective-permute-start.3) | collective-permute-done | bytes 524320 | tf_op jit(solution)/shard_map/ppermute | solution.py:283
  178.6 0.8 copy-done.5
  179.4 5.7 %shard_map.106 = f32[1024,512]{1,0:T(8,128)} custom-call(s32[1,512]{1,0:T(1,128)} %broadcast_subtract_fusion.3.refs_0_, s32[1,512]{1,0:T(1,128)} %broadcast_subtract_fusion.2.refs_1_, s32[1,512]{1,0:T(1,128)} %broadcast_subtract_fusion.1.refs_2_, s32[1,512]{1,0:T(1,128)} %broadcast_subtract_fusion.refs_3_, bf16[512,512]{1,0:T(8,128)(2,1)} %bitcast.32, ...), custom_call_target="tpu_custom_call" | custom-call | flops 1000000000 | bytes 10000000 | tf_op jit(solution)/shard_map/pallas_call | solution.py:392
  185.1 1.1 copy-done.3
  186.1 4.3 %shard_map.107 = (f32[512,2048]{1,0:T(8,128)}, f32[512,512]{1,0:T(8,128)}) custom-call(s32[1,1]{1,0:T(1,128)} %bitcast.6.core_ref, bf16[256,2560]{1,0:T(8,128)(2,1)} %copy-done, bf16[256,2560]{1,0:T(8,128)(2,1)} %copy-done.3), custom_call_target="tpu_custom_call" | custom-call | flops 100000000 | bytes 10000000 | tf_op jit(solution)/shard_map/pallas_call | solution.py:399
  (51 shorter events, 8.8 us)
Async XLA Ops:
  14.4 8.9 %copy-start.6 = (s32[1024]{0:T(1024)S(1)}, s32[1024]{0:T(1024)}, u32[]{:S(2)}) copy-start(s32[1024]{0:T(1024)} %param.9) | copy-start | bytes 12292
  19.8 16.8 %all-to-all-start.1 = ((bf16[8,64,512]{2,1,0:T(8,128)(2,1)}), bf16[8,64,512]{2,1,0:T(8,128)(2,1)S(1)}, u32[]{:S(2)}, u32[]{:S(2)}) async-start(bf16[8,64,512]{2,1,0:T(8,128)(2,1)} %bitcast.4), calls=%async_computation.1 | async-start | bytes 1048576 | tf_op jit(solution)/shard_map/all_to_all | solution.py:287
  36.6 0.8 copy-start.1
  78.3 2.5 %collective-permute-start.6 = (bf16[256,1536]{1,0:T(8,128)(2,1)}, bf16[256,1536]{1,0:T(8,128)(2,1)S(1)}, u32[]{:S(2)}, u32[]{:S(2)}) collective-permute-start(bf16[256,1536]{1,0:T(8,128)(2,1)} %get-tuple-element.29), channel_id=1, source_target_pairs={{0,1},{1,0},{2,3},{3,2},{4,5},{5,4},{6,7},{7,6},{8,9},{9,8},{10,11... | collective-permute-start | bytes 2359304 | tf_op jit(solution)/shard_map/ppermute | solution.py:283
  82.2 11.6 %collective-permute-start.7 = (bf16[128,1536]{1,0:T(8,128)(2,1)S(1)}, bf16[128,1536]{1,0:T(8,128)(2,1)S(1)}, u32[]{:S(2)}, u32[]{:S(2)}) collective-permute-start(bf16[128,1536]{1,0:T(8,128)(2,1)S(1)} %dynamic-slice_bitcast_fusion), channel_id=1, source_target_pairs={{0,4},{1,3},{2,6},{3,1},{4,0},{5,7},{6,2},{7,5},{8,12},{9,11},{10,... | collective-permute-start | bytes 1179656 | tf_op jit(solution)/shard_map/ppermute | solution.py:291
  83.7 33.8 %all-to-all-start.3 = ((bf16[32,16,1024]{2,1,0:T(8,128)(2,1)}), bf16[32,16,1024]{2,1,0:T(8,128)(2,1)S(1)}, u32[]{:S(2)}, u32[]{:S(2)}) async-start(bf16[32,16,1024]{2,1,0:T(8,128)(2,1)} %bitcast.9), calls=%async_computation.3 | async-start | bytes 2097152 | tf_op jit(solution)/shard_map/all_to_all | solution.py:287
  94.0 7.5 %collective-permute-start.8 = (bf16[64,1536]{1,0:T(8,128)(2,1)S(1)}, bf16[64,1536]{1,0:T(8,128)(2,1)S(1)}, u32[]{:S(2)}, u32[]{:S(2)}) collective-permute-start(bf16[64,1536]{1,0:T(8,128)(2,1)S(1)} %dynamic-slice_bitcast_fusion.1), channel_id=1, source_target_pairs={{0,2},{1,5},{2,0},{3,7},{4,6},{5,1},{6,4},{7,3},{8,10},{9,13},{10,... | collective-permute-start | bytes 589832 | tf_op jit(solution)/shard_map/ppermute | solution.py:291
  101.6 7.1 %collective-permute-start.9 = (bf16[64,1536]{1,0:T(8,128)(2,1)S(1)}, bf16[64,1536]{1,0:T(8,128)(2,1)S(1)}, u32[]{:S(2)}, u32[]{:S(2)}) collective-permute-start(bf16[64,1536]{1,0:T(8,128)(2,1)S(1)} %fusion.1), channel_id=1, source_target_pairs={{0,8},{1,17},{2,10},{3,19},{4,12},{5,21},{6,14},{7,23},{8,0},{9,25... | collective-permute-start | bytes 589832 | tf_op jit(solution)/shard_map/ppermute | solution.py:291
  108.8 13.1 %collective-permute-start.10 = (bf16[64,1536]{1,0:T(8,128)(2,1)S(1)}, bf16[64,1536]{1,0:T(8,128)(2,1)S(1)}, u32[]{:S(2)}, u32[]{:S(2)}) collective-permute-start(bf16[64,1536]{1,0:T(8,128)(2,1)S(1)} %add_convert_fusion.2), channel_id=1, source_target_pairs={{0,16},{1,9},{2,18},{3,11},{4,20},{5,13},{6,22},{7,15},{8,24},{9,1... | collective-permute-start | bytes 589832 | tf_op jit(solution)/shard_map/ppermute | solution.py:291
  118.4 9.2 %all-to-all-start.4 = ((bf16[4,16,1024]{2,1,0:T(8,128)(2,1)}), bf16[4,16,1024]{2,1,0:T(8,128)(2,1)S(1)}, u32[]{:S(2)}, u32[]{:S(2)}) async-start(bf16[4,16,1024]{2,1,0:T(8,128)(2,1)} %broadcast_in_dim.2), calls=%async_computation.4 | async-start | bytes 262144 | tf_op jit(solution)/shard_map/all_to_all | solution.py:287
  127.6 7.1 %collective-permute-start.11 = (bf16[64,2560]{1,0:T(8,128)(2,1)S(1)}, bf16[64,2560]{1,0:T(8,128)(2,1)S(1)}, u32[]{:S(2)}, u32[]{:S(2)}) collective-permute-start(bf16[64,2560]{1,0:T(8,128)(2,1)S(1)} %pad_maximum_fusion.2), channel_id=1, source_target_pairs={{0,2},{1,5},{2,0},{3,7},{4,6},{5,1},{6,4},{7,3},{8,10},{9,13},{10,... | collective-permute-start | bytes 983048 | tf_op jit(solution)/shard_map/ppermute | solution.py:291
  134.9 10.7 %collective-permute-start.12 = (bf16[128,2560]{1,0:T(8,128)(2,1)S(1)}, bf16[128,2560]{1,0:T(8,128)(2,1)S(1)}, u32[]{:S(2)}, u32[]{:S(2)}) collective-permute-start(bf16[128,2560]{1,0:T(8,128)(2,1)S(1)} %pad_maximum_fusion.1), channel_id=1, source_target_pairs={{0,4},{1,3},{2,6},{3,1},{4,0},{5,7},{6,2},{7,5},{8,12},{9,11},{10,... | collective-permute-start | bytes 1966088 | tf_op jit(solution)/shard_map/ppermute | solution.py:291
  141.5 19.5 %all-to-all-start.2 = ((bf16[8,64,512]{2,1,0:T(8,128)(2,1)}), bf16[8,64,512]{2,1,0:T(8,128)(2,1)S(1)}, u32[]{:S(2)}, u32[]{:S(2)}) async-start(bf16[8,64,512]{2,1,0:T(8,128)(2,1)} %bitcast.29), calls=%async_computation.2 | async-start | bytes 1048576 | tf_op jit(solution)/shard_map/all_to_all | solution.py:287
  145.9 39.2 %copy-start = (bf16[256,2560]{1,0:T(8,128)(2,1)}, bf16[256,2560]{1,0:T(8,128)(2,1)S(1)}, u32[]{:S(2)}) copy-start(bf16[256,2560]{1,0:T(8,128)(2,1)S(1)} %pad_maximum_fusion.own) | copy-start | bytes 3932164
  145.9 39.2 %collective-permute-start.13 = (bf16[256,2560]{1,0:T(8,128)(2,1)S(1)}, bf16[256,2560]{1,0:T(8,128)(2,1)S(1)}, u32[]{:S(2)}, u32[]{:S(2)}) collective-permute-start(bf16[256,2560]{1,0:T(8,128)(2,1)S(1)} %pad_maximum_fusion.own), channel_id=1, source_target_pairs={{0,1},{1,0},{2,3},{3,2},{4,5},{5,4},{6,7},{7,6},{8,9},{9,8},{10,11... | collective-permute-start | bytes 3932168 | tf_op jit(solution)/shard_map/ppermute | solution.py:283
  161.0 16.8 %copy-start.2 = (bf16[8,64,512]{2,1,0:T(8,128)(2,1)}, bf16[8,64,512]{2,1,0:T(8,128)(2,1)S(1)}, u32[]{:S(2)}) copy-start(bf16[8,64,512]{2,1,0:T(8,128)(2,1)S(1)} %all-to-all-done.2) | copy-start | bytes 1572868
  161.0 14.1 %collective-permute-start.3 = (bf16[512,512]{1,0:T(8,128)(2,1)S(1)}, bf16[512,512]{1,0:T(8,128)(2,1)}, u32[]{:S(2)}, u32[]{:S(2)}) collective-permute-start(bf16[512,512]{1,0:T(8,128)(2,1)S(1)} %bitcast.30), channel_id=1, source_target_pairs={{0,2},{2,0},{1,3},{3,1},{4,6},{6,4},{5,7},{7,5},{8,10},{10,8},{9,1... | collective-permute-start | bytes 1572872 | tf_op jit(solution)/shard_map/ppermute | solution.py:283
  162.6 13.5 %collective-permute-start.1 = (s32[1,512]{1,0:T(1,128)S(1)}, s32[1,512]{1,0:T(1,128)S(1)}, u32[]{:S(2)}, u32[]{:S(2)}) collective-permute-start(s32[1,512]{1,0:T(1,128)S(1)} %reshape.95), channel_id=1, source_target_pairs={{0,1},{1,0},{2,3},{3,2},{4,5},{5,4},{6,7},{7,6},{8,9},{9,8},{10,11... | collective-permute-start | bytes 6152 | tf_op jit(solution)/shard_map/ppermute | solution.py:283
  162.7 12.4 %collective-permute-start = (s32[1,512]{1,0:T(1,128)S(1)}, s32[1,512]{1,0:T(1,128)S(1)}, u32[]{:S(2)}, u32[]{:S(2)}) collective-permute-start(s32[1,512]{1,0:T(1,128)S(1)} %reshape.95), channel_id=1, source_target_pairs={{0,2},{2,0},{1,3},{3,1},{4,6},{6,4},{5,7},{7,5},{8,10},{10,8},{9,1... | collective-permute-start | bytes 6152 | tf_op jit(solution)/shard_map/ppermute | solution.py:283
  164.9 12.8 %collective-permute-start.4 = (bf16[512,512]{1,0:T(8,128)(2,1)S(1)}, bf16[512,512]{1,0:T(8,128)(2,1)S(1)}, u32[]{:S(2)}, u32[]{:S(2)}) collective-permute-start(bf16[512,512]{1,0:T(8,128)(2,1)S(1)} %bitcast.31), channel_id=1, source_target_pairs={{0,1},{1,0},{2,3},{3,2},{4,5},{5,4},{6,7},{7,6},{8,9},{9,8},{10,11... | collective-permute-start | bytes 1572872 | tf_op jit(solution)/shard_map/ppermute | solution.py:283
  175.1 2.7 %collective-permute-start.5 = (bf16[512,512]{1,0:T(8,128)(2,1)}, bf16[512,512]{1,0:T(8,128)(2,1)S(1)}, u32[]{:S(2)}, u32[]{:S(2)}) collective-permute-start(bf16[512,512]{1,0:T(8,128)(2,1)} %collective-permute-done.3.refs_5_), channel_id=1, source_target_pairs={{0,1},{1,0},{2,3},{3,2},{4,5},{5,4},{6,7},{7,6},{8,9},{9,8},{10,11... | collective-permute-start | bytes 1572872 | tf_op jit(solution)/shard_map/ppermute | solution.py:283
  175.7 1.5 collective-permute-start.2
  177.8 0.8 copy-start.4
  178.6 0.8 copy-start.5
  185.1 1.1 copy-start.3

commit v5 on v4

--- a/solution.py
+++ b/solution.py
@@ -21,6 +21,7 @@
 
 
 AXES = ("e1", "e0", "s1", "s0")
+PLANE = AXES[1:]
 
 
 def mm(a, b):
@@ -188,7 +189,8 @@
             key_base = pl.multiple_of(j * BLOCK, BLOCK)
             keys = pl.ds(key_base, BLOCK)
             other = key_base + lax.broadcasted_iota(jnp.int32, (BLOCK, BLOCK), 0)
-            allowed = (other >= start) & (other <= place)
+            allowed = jnp.where((other >= start) & (other <= place), 1.0, 0.0).astype(BF)
+            one, half = jnp.asarray(1.0, BF), jnp.asarray(half_scale, BF)
             parts = []
             for h in range(heads):
                 lo = h * head
@@ -196,12 +198,12 @@
                 k = vqk_ref[keys, 2 * wide + lo : 2 * wide + lo + head]
                 v = vqk_ref[keys, lo : lo + head]
                 da = datt_ref[span, lo : lo + head]
-                u = mm_t(k, q) * half_scale
-                dw = mm_t(v, da)
+                u = (mm_t(k, q) * half_scale).astype(BF)
+                dw = mm_t(v, da).astype(BF) * allowed
                 th = jnp.tanh(u)
-                w = jnp.where(allowed, u + u * th, 0.0).astype(BF)
-                slope = (half_scale + half_scale * th) * (1.0 + u - u * th)
-                ds = jnp.where(allowed, dw * slope, 0.0).astype(BF)
+                uth = u * th
+                w = (u + uth) * allowed
+                ds = dw * ((half + half * th) * (one + (u - uth)))
                 parts.append((mm(w, da), tt_mm(ds, k), mm(ds, q)))
             for h in range(heads):
                 sums[3 * h][keys, :] += parts[h][0]
@@ -239,13 +241,11 @@
     grad_ref[...] = (center_back(dn, normed, inverse) + res_ref[...]).astype(BF)
 
 
-def assemble_kernel(core_ref, own, got, in_ref, out_ref):
+def lay_kernel(place_ref, source, *refs):
+    in_ref, out_ref = refs[-2:]
     width = out_ref.shape[1]
-    half = own.shape[0]
-    for source, place in ((own, core_ref[0, 0]), (got, 1 - core_ref[0, 0])):
-        span = pl.ds(pl.multiple_of(place * half, half), half)
-        out_ref[span, :] = source[:, :width].astype(F32)
-        in_ref[span, :] = source[:, width:].astype(F32)
+    out_ref[...] = source[:, :width].astype(F32)
+    in_ref[...] = source[:, width:].astype(F32)
 
 
 def table_kernel(count, *refs):
@@ -278,6 +278,55 @@
     )
 
 
+def call_first(order, tokens, slots, width):
+    wides = [(h1 - h0) * width // HEADS for h0, h1 in GROUPS]
+    return call(
+        functools.partial(first_kernel, order),
+        [((tokens, width), BF), ((width, 2 * width), BF), ((width, slots), BF), ((slots, width), BF)]
+        + [((tokens, 3 * w), BF) for w in wides]
+        + [((tokens, w), BF) for w in wides]
+        + [((slots, 3 * w), BF) for w in wides],
+        [
+            ((slots, 4 * width), BF), ((tokens, width), BF), ((tokens, width), BF), ((BLOCK, width), F32),
+            ((tokens, width), BF), ((tokens, width), BF), ((slots, width), BF),
+        ],
+        [SMEM] + [VMEM] * 7,
+        10**10,
+    )
+
+
+def call_attention(tokens, slots, width):
+    head, grads = width // HEADS, 3 * width
+    return call(
+        functools.partial(second_kernel, HEADS),
+        [((slots, grads), BF)] + [((width // 2, grads), BF)] * 2,
+        [((tokens, head), F32)] * (3 * HEADS),
+        [SMEM] * 2 + [VMEM] * 5,
+        10**10,
+    )
+
+
+def lay(place, source, width, *into):
+    half, steps = source.shape[0], 4
+    rows = half // steps
+    block = lambda columns: pl.BlockSpec((rows, columns), lambda i, place_ref: (place_ref[0] * steps + i, 0))
+    shapes = [(2 * half, source.shape[1] - width), (2 * half, width)]
+    return pl.pallas_call(
+        lay_kernel,
+        out_shape=[jax.ShapeDtypeStruct(s, F32) for s in shapes],
+        grid_spec=pltpu.PrefetchScalarGridSpec(
+            num_scalar_prefetch=1,
+            grid=(steps,),
+            in_specs=[pl.BlockSpec((rows, source.shape[1]), lambda i, place_ref: (i, 0))]
+            + [pl.BlockSpec(memory_space=pl.ANY)] * len(into),
+            out_specs=[block(shape[1]) for shape in shapes],
+        ),
+        input_output_aliases={2 + i: i for i in range(len(into))},
+        compiler_params=pltpu.CompilerParams(vmem_limit_bytes=16 * 2**20),
+        cost_estimate=pl.CostEstimate(flops=10**8, bytes_accessed=4 * 10**6, transcendentals=0),
+    )(place, source, *into)
+
+
 def other_place(x, axis):
     size = lax.axis_size(axis)
     return lax.ppermute(x, axis, [(i, i ^ 1) for i in range(size)])
@@ -292,23 +341,19 @@
 
 
 def block_order():
-    line = lax.axis_size("e1")
     order = []
-    for d in range(lax.axis_size(AXES)):
-        core, near, far = d & 1, (d >> 1) & 1, (d >> 2) & 1
+    for d in range(lax.axis_size(PLANE)):
+        core, near, far = d & 1, (d >> 1) & 1, d >> 2
         first, second = (near, far) if core else (far, near)
-        order.append(((core * 2 + first) * 2 + second) * line + (d >> 3))
+        order.append((core * 2 + first) * 2 + second)
     return order
 
 
 def weight_sum(early, keep, give):
-    total, line = lax.axis_size(AXES), lax.axis_size("e1")
+    total, plane = lax.axis_size(AXES), lax.axis_size(PLANE)
     me = lax.axis_index(AXES)
-    early = exchange(early.reshape(total, early.shape[0] // total, early.shape[1]), AXES)
+    early = exchange(early.reshape(plane, early.shape[0] // plane, early.shape[1]), PLANE)
     early = jnp.sum(early.astype(F32), axis=0).astype(BF)
-    early = exchange(jnp.broadcast_to(early[None], (line,) + early.shape), ("e1",))
-    early = early.reshape(-1, early.shape[-1])
-
     by_core = lambda first, second: (lambda d: d ^ (1 << (second if d & 1 else first)))
     upper = lambda first, second: (me >> jnp.where(me & 1 == 1, second, first)) & 1
     got = other_place(give, "s0")
@@ -320,11 +365,11 @@
         give = lax.dynamic_index_in_dim(halves, 1 - place, 0, keepdims=False)
         got = swap(give, by_core(first, second))
         x = (mine.astype(F32) + got.astype(F32)).astype(BF)
+    x = jnp.concatenate([early, x], axis=1)
     bits = range(3, total.bit_length() - 1)
     for first, second in zip(bits, bits[::-1]):
         got = swap(x, by_core(first, second))
         x = (x.astype(F32) + got.astype(F32)).astype(BF)
-    x = jnp.concatenate([early, x], axis=1)
     for first, second in ((1, 2), (2, 1)):
         got = swap(x, by_core(first, second))
         place = upper(first, second) == 1
@@ -338,44 +383,25 @@
     requests = fetch_rows.reshape(lax.axis_size(emb), -1)
     slots = requests.shape[0] * requests.shape[1]
     tokens = event_slot.shape[0]
-    head = width // HEADS
     asked = exchange(requests, emb)
     found = item_table[asked]
     fetched = exchange(found, emb)
     rows = fetched.reshape(slots, width)
     slot_row, slot_col = event_slot.reshape(1, tokens), event_slot.reshape(tokens, 1)
     core = lax.axis_index("s0").reshape(1, 1)
-    wides = [(h1 - h0) * head for h0, h1 in GROUPS]
     count = len(GROUPS)
 
     dgated, res = call(
         early_kernel, [((tokens, width), BF), ((slots, width), F32)], [], [VMEM] * 3, 10**9
     )(slot_row, out_weight, out_grad)
-    first = call(
-        functools.partial(first_kernel, block_order()),
-        [((tokens, width), BF), ((width, 2 * width), BF), ((width, slots), BF), ((slots, width), BF)]
-        + [((tokens, 3 * w), BF) for w in wides]
-        + [((tokens, w), BF) for w in wides]
-        + [((slots, 3 * w), BF) for w in wides],
-        [
-            ((slots, 4 * width), BF), ((tokens, width), BF), ((tokens, width), BF), ((BLOCK, width), F32),
-            ((tokens, width), BF), ((tokens, width), BF), ((slots, width), BF),
-        ],
-        [SMEM] + [VMEM] * 7,
-        10**10,
-    )
+    first = call_first(block_order(), tokens, slots, width)
     outs = first(lengths, slot_row, slot_col, rows, in_weight, out_weight, out_grad, dgated)
     layer_out, wg, nt, dpre_gate = outs[:4]
     vqk, datt, dsil = (outs[4 + k * count : 4 + (k + 1) * count] for k in range(3))
 
-    heads, grads = HEADS, 3 * width
-    dpre, keep, give = call(
-        functools.partial(second_kernel, heads),
-        [((slots, grads), BF)] + [((width // 2, grads), BF)] * 2,
-        [((tokens, head), F32)] * (3 * heads),
-        [SMEM] * 2 + [VMEM] * 5,
-        10**10,
-    )(lengths, core, slot_row, vqk[0], datt[0], dsil[0], nt)
+    dpre, keep, give = call_attention(tokens, slots, width)(
+        lengths, core, slot_row, vqk[0], datt[0], dsil[0], nt
+    )
     own, got = weight_sum(wg, keep, give)
     (slot_grad,) = call(slot_kernel, [((slots, width), BF)], [], [VMEM] * (4 + count), 10**9)(
         rows, res, in_weight, dpre_gate, dpre
@@ -395,14 +421,11 @@
         [],
         [VMEM] * (2 * len(places)),
         10**9,
+        24,
     )(*places, *arrays)
-    in_total, out_total = call(
-        assemble_kernel,
-        [((width, 4 * width), F32), ((width, width), F32)],
-        [],
-        [SMEM] + [VMEM] * 2,
-        10**8,
-    )(core, own, got)
+    place = core.reshape(1)
+    laid = lay(place, own, width)
+    in_total, out_total = lay(1 - place, got, width, *laid)
     return layer_out, table_grad, in_total, out_total
 
 

time: 191 us -> 174 us (0.911)
  starting transfers between devices: 25.5 us -> 19.8 us
  local copies, waits for them, and re-layouts: 11.3 us -> 7.92 us
  Pallas kernels: 59.6 us -> 56.6 us
  other arithmetic: 5.23 us -> 2.91 us
  waiting for transfers between devices: 74.3 us -> 72 us
    ppermute x6, waiting for transfers between devices: 28 us -> 35.6 us  [swap(): lax.ppermute(x, AXES, [(d, partner(d)) for d in range(lax.axis_size(AXES))])]
    all_to_all x4 -> x3, waiting for transfers between devices: 33.4 us -> 26.5 us  [exchange(): return lax.all_to_all(x, axes, split_axis=0, concat_axis=0, tiled=True)]
    ppermute x8, waiting for transfers between devices: 12.9 us -> 9.9 us  [other_place(): return lax.ppermute(x, axis, [(i, i ^ 1) for i in range(size)])]
    ppermute x6, starting transfers between devices: 8.98 us -> 6.27 us  [swap(): lax.ppermute(x, AXES, [(d, partner(d)) for d in range(lax.axis_size(AXES))])]
    unnamed x14 -> x4, local copies, waits for them, and re-layouts: 3.45 us -> 0.79 us
    all_to_all x4 -> x3, starting transfers between devices: 13.3 us -> 10.7 us  [exchange(): return lax.all_to_all(x, axes, split_axis=0, concat_axis=0, tiled=True)]
    pallas_call x2 -> x3, Pallas kernels: 24.4 us -> 21.9 us  [the longest x1 18 us: on_device(): call_attention(tokens, slots, width)]
    sub x4, other arithmetic: 2.36 us -> 0.01 us  [on_device(): places = [p - base for p in places]]
  transfers between devices with their start and end apart: 18 -> 17, of which waited for: 12 -> 12; matrix products, arithmetic and copies ran while one was open for 3% -> 2% of each run, Pallas kernels for 8% -> 9%
where the time goes in v5:
time: 174 us
  waiting for transfers between devices  72 us (41%)
  Pallas kernels  56.6 us (33%)
  starting transfers between devices  19.8 us (11%)
  blocking collectives  13.7 us (8%)
  local copies, waits for them, and re-layouts  7.92 us (5%)
  other arithmetic  2.91 us (2%)
    ppermute x6, waiting for transfers between devices, swap(): lax.ppermute(x, AXES, [(d, partner(d)) for d in range(lax.axis_size(AXES))])  35.6 us
    all_to_all x3, waiting for transfers between devices, exchange(): return lax.all_to_all(x, axes, split_axis=0, concat_axis=0, tiled=True)  26.5 us
    pallas_call x1, Pallas kernels, on_device(): first(lengths, slot_row, slot_col, rows, in_weight, out_weight, out_grad,...  20.8 us
    pallas_call x1, Pallas kernels, on_device(): call_attention(tokens, slots, width)  18 us
    all_to_all x1, blocking collectives, exchange(): return lax.all_to_all(x, axes, split_axis=0, concat_axis=0, tiled=True)  13.7 us
    all_to_all x3, starting transfers between devices, exchange(): return lax.all_to_all(x, axes, split_axis=0, concat_axis=0, tiled=True)  10.7 us
    ppermute x8, waiting for transfers between devices, other_place(): return lax.ppermute(x, axis, [(i, i ^ 1) for i in range(size)])  9.9 us
    ppermute x6, starting transfers between devices, swap(): lax.ppermute(x, AXES, [(d, partner(d)) for d in range(lax.axis_size(AXES))])  6.27 us
  transfers between devices with their start and end apart: 17, of which 12 were waited for; matrix products, arithmetic and copies ran while one was open for 2% of the time, Pallas kernels for 9%

profile of v5, /device:TPU:0, one launch (start us, length us, event | category | flops | bytes accessed | tf_op | source)
XLA Modules:
  0.0 173.8 jit_solution(15836637926790109238)
XLA Ops:
  0.6 13.7 %all_to_all.27 = s32[8,1,64]{2,1,0:T(1,128)S(1)} all-to-all(s32[8,1,64]{2,1,0:T(1,128)} %bitcast.40), channel_id=1, replica_groups=mesh['e1'=4,'e0'=2,'s1'=2,'s0'=2] {'e1','e0'}, dimensions={0} | all-to-all | bytes 4096 | tf_op jit(solution)/shard_map/all_to_all | solution.py:336
  14.4 5.4 %gather_fusion = bf16[512,512]{1,0:T(8,128)(2,1)} fusion(bf16[4096,512]{1,0:T(8,128)(2,1)} %param.7, s32[1024]{0:T(1024)S(1)} %pad_clamp_fusion), kind=kCustom, calls=%fused_computation | custom fusion | bytes 1050624 | tf_op jit(solution)/shard_map/gather | solution.py:387
  19.8 3.5 %all-to-all-start.1 = ((bf16[8,64,512]{2,1,0:T(8,128)(2,1)}), bf16[8,64,512]{2,1,0:T(8,128)(2,1)S(1)}, u32[]{:S(2)}, u32[]{:S(2)}) async-start(bf16[8,64,512]{2,1,0:T(8,128)(2,1)} %bitcast.4), calls=%async_computation.1 | async-start | bytes 1048576 | tf_op jit(solution)/shard_map/all_to_all | solution.py:336
  23.3 1.0 copy.14.slot_col
  24.4 3.7 %shard_map.102 = (bf16[1024,512]{1,0:T(8,128)(2,1)}, f32[512,512]{1,0:T(8,128)}) custom-call(s32[1,1024]{1,0:T(1,128)} %bitcast.36, bf16[512,512]{1,0:T(8,128)(2,1)} %wout_ref.3, bf16[1024,512]{1,0:T(8,128)(2,1)} %og_ref.3), custom_call_target="tpu_custom_call" | custom-call | flops 1000000000 | bytes 10000000 | tf_op jit(solution)/shard_map/pallas_call | solution.py:394
  28.0 8.6 %all-to-all-done.1 = bf16[8,64,512]{2,1,0:T(8,128)(2,1)S(1)} async-done(((bf16[8,64,512]{2,1,0:T(8,128)(2,1)}), bf16[8,64,512]{2,1,0:T(8,128)(2,1)S(1)}, u32[]{:S(2)}, u32[]{:S(2)}) %all-to-all-start.1) | async-done | bytes 524320 | tf_op jit(solution)/shard_map/all_to_all | solution.py:336
  36.6 0.8 copy-done
  37.4 20.8 %shard_map.103 = (bf16[1024,512]{1,0:T(8,128)(2,1)}, bf16[512,1024]{1,0:T(8,128)(2,1)}, bf16[512,512]{1,0:T(8,128)(2,1)}, bf16[512,512]{1,0:T(8,128)(2,1)}, bf16...) custom-call(s32[1,8]{1,0:T(1,128)} %len_ref.3, s32[1,1024]{1,0:T(1,128)} %bitcast.37, ...), custom_call_target="tpu_custom_call" | custom-call | flops 10000000000 | bytes 10000000 | tf_op jit(solution)/shard_map/pallas_call | solution.py:398
  58.2 18.0 %shard_map.104 = (bf16[512,1536]{1,0:T(8,128)(2,1)}, bf16[256,1536]{1,0:T(8,128)(2,1)}, bf16[256,1536]{1,0:T(8,128)(2,1)}) custom-call(s32[1,8]{1,0:T(1,128)} %len_ref.3, s32[1,1]{1,0:T(1,128)} %bitcast.6.core_ref, s32[1,1024]{1,0:T(1,128)} %bitcast.38, bf16[1024,1536]{1,0:T(8,128)(2,1)} %get-tuple-element.24.vqk_ref, ...), custom_call_target="tpu_custom_call" | custom-call | flops 10000000000 | bytes 10000000 | tf_op jit(solution)/shard_map/pallas_call | solution.py:402
  76.2 2.5 %collective-permute-done.6 = bf16[256,1536]{1,0:T(8,128)(2,1)S(1)} collective-permute-done((bf16[256,1536]{1,0:T(8,128)(2,1)}, bf16[256,1536]{1,0:T(8,128)(2,1)S(1)}, u32[]{:S(2)}, u32[]{:S(2)}) %collective-permute-start.6) | collective-permute-done | bytes 786464 | tf_op jit(solution)/shard_map/ppermute | solution.py:332
  78.7 1.3 add_convert_fusion
  80.1 1.5 collective-permute-start.7
  81.6 3.7 %all-to-all-start.3 = ((bf16[8,64,1024]{2,1,0:T(8,128)(2,1)}), bf16[8,64,1024]{2,1,0:T(8,128)(2,1)S(1)}, u32[]{:S(2)}, u32[]{:S(2)}) async-start(bf16[8,64,1024]{2,1,0:T(8,128)(2,1)} %bitcast.10), calls=%async_computation.3 | async-start | bytes 2097152 | tf_op jit(solution)/shard_map/all_to_all | solution.py:336
  85.4 2.6 %collective-permute-done.7 = bf16[128,1536]{1,0:T(8,128)(2,1)S(1)} collective-permute-done((bf16[128,1536]{1,0:T(8,128)(2,1)S(1)}, bf16[128,1536]{1,0:T(8,128)(2,1)S(1)}, u32[]{:S(2)}, u32[]{:S(2)}) %collective-permute-start.7) | collective-permute-done | bytes 393248 | tf_op jit(solution)/shard_map/ppermute | solution.py:340
  88.0 1.6 collective-permute-start.8
  89.6 10.5 %all-to-all-done.3 = bf16[8,64,1024]{2,1,0:T(8,128)(2,1)S(1)} async-done(((bf16[8,64,1024]{2,1,0:T(8,128)(2,1)}), bf16[8,64,1024]{2,1,0:T(8,128)(2,1)S(1)}, u32[]{:S(2)}, u32[]{:S(2)}) %all-to-all-start.3) | async-done | bytes 1048608 | tf_op jit(solution)/shard_map/all_to_all | solution.py:336
  100.3 1.3 collective-permute-done.8
  101.8 10.5 %collective-permute-done.9 = bf16[64,2560]{1,0:T(8,128)(2,1)S(1)} collective-permute-done((bf16[64,2560]{1,0:T(8,128)(2,1)S(1)}, bf16[64,2560]{1,0:T(8,128)(2,1)S(1)}, u32[]{:S(2)}, u32[]{:S(2)}) %collective-permute-start.9) | collective-permute-done | bytes 327712 | tf_op jit(solution)/shard_map/ppermute | solution.py:340
  112.5 10.9 %collective-permute-done.10 = bf16[64,2560]{1,0:T(8,128)(2,1)S(1)} collective-permute-done((bf16[64,2560]{1,0:T(8,128)(2,1)S(1)}, bf16[64,2560]{1,0:T(8,128)(2,1)S(1)}, u32[]{:S(2)}, u32[]{:S(2)}) %collective-permute-start.10) | collective-permute-done | bytes 327712 | tf_op jit(solution)/shard_map/ppermute | solution.py:340
  123.6 7.9 %collective-permute-done.11 = bf16[64,2560]{1,0:T(8,128)(2,1)S(1)} collective-permute-done((bf16[64,2560]{1,0:T(8,128)(2,1)S(1)}, bf16[64,2560]{1,0:T(8,128)(2,1)S(1)}, u32[]{:S(2)}, u32[]{:S(2)}) %collective-permute-start.11) | collective-permute-done | bytes 327712 | tf_op jit(solution)/shard_map/ppermute | solution.py:340
  131.6 2.9 %collective-permute-start.12 = (bf16[128,2560]{1,0:T(8,128)(2,1)S(1)}, bf16[128,2560]{1,0:T(8,128)(2,1)S(1)}, u32[]{:S(2)}, u32[]{:S(2)}) collective-permute-start(bf16[128,2560]{1,0:T(8,128)(2,1)S(1)} %pad_maximum_fusion.1), channel_id=1, source_target_pairs={{0,4},{1,3},{2,6},{3,1},{4,0},{5,7},{6,2},{7,5},{8,12},{9,11},{10,... | collective-permute-start | bytes 1966088 | tf_op jit(solution)/shard_map/ppermute | solution.py:340
  134.5 5.0 %shard_map.105 = bf16[512,512]{1,0:T(8,128)(2,1)} custom-call(bf16[512,512]{1,0:T(8,128)(2,1)} %bitcast.31, f32[512,512]{1,0:T(8,128)} %get-tuple-element.22.res_ref, bf16[512,2048]{1,0:T(8,128)(2,1)} %win_ref.3, bf16[512,512]{1,0:T(8,128)(2,1)} %get-tuple-element.23.gate_ref, bf16[512,1536]{1,0:T(8,128)(2,1)} %get-tuple-element.28.refs_0_), custom_call_target="tpu_custom_call" | custom-call | flops 1000000000 | bytes 10000000 | tf_op jit(solution)/shard_map/pallas_call | solution.py:406
  139.5 3.5 %all-to-all-start.2 = ((bf16[8,64,512]{2,1,0:T(8,128)(2,1)}), bf16[8,64,512]{2,1,0:T(8,128)(2,1)S(1)}, u32[]{:S(2)}, u32[]{:S(2)}) async-start(bf16[8,64,512]{2,1,0:T(8,128)(2,1)} %bitcast.32), calls=%async_computation.2 | async-start | bytes 1048576 | tf_op jit(solution)/shard_map/all_to_all | solution.py:336
  143.0 2.4 %collective-permute-done.12 = bf16[128,2560]{1,0:T(8,128)(2,1)S(1)} collective-permute-done((bf16[128,2560]{1,0:T(8,128)(2,1)S(1)}, bf16[128,2560]{1,0:T(8,128)(2,1)S(1)}, u32[]{:S(2)}, u32[]{:S(2)}) %collective-permute-start.12) | collective-permute-done | bytes 655392 | tf_op jit(solution)/shard_map/ppermute | solution.py:340
  145.8 7.4 %all-to-all-done.2 = bf16[8,64,512]{2,1,0:T(8,128)(2,1)S(1)} async-done(((bf16[8,64,512]{2,1,0:T(8,128)(2,1)}), bf16[8,64,512]{2,1,0:T(8,128)(2,1)S(1)}, u32[]{:S(2)}, u32[]{:S(2)}) %all-to-all-start.2) | async-done | bytes 524320 | tf_op jit(solution)/shard_map/all_to_all | solution.py:336
  153.7 0.7 reduce.4
  154.5 2.1 %collective-permute-start = (s32[1,512]{1,0:T(1,128)S(1)}, s32[1,512]{1,0:T(1,128)S(1)}, u32[]{:S(2)}, u32[]{:S(2)}) collective-permute-start(s32[1,512]{1,0:T(1,128)S(1)} %reshape.91), channel_id=1, source_target_pairs={{0,2},{2,0},{1,3},{3,1},{4,6},{6,4},{5,7},{7,5},{8,10},{10,8},{9,1... | collective-permute-start | bytes 6152 | tf_op jit(solution)/shard_map/ppermute | solution.py:332
  156.7 5.8 %collective-permute-done.3.refs_5_ = bf16[512,512]{1,0:T(8,128)(2,1)} collective-permute-done((bf16[512,512]{1,0:T(8,128)(2,1)S(1)}, bf16[512,512]{1,0:T(8,128)(2,1)}, u32[]{:S(2)}, u32[]{:S(2)}) %collective-permute-start.3) | collective-permute-done | bytes 524320 | tf_op jit(solution)/shard_map/ppermute | solution.py:332
  163.0 1.6 collective-permute-done.2
  164.6 5.2 %shard_map.106 = f32[1024,512]{1,0:T(8,128)} custom-call(s32[1,512]{1,0:T(1,128)S(1)} %broadcast_subtract_fusion.3.refs_0_, s32[1,512]{1,0:T(1,128)S(1)} %broadcast_subtract_fusion.2.refs_1_, s32[1,512]{1,0:T(1,128)S(1)} %broadcast_subtract_fusion.1.refs_2_, s32[1,512]{1,0:T(1,128)S(1)} %broadcast_subtract_fusion.refs_3_, bf16[512,512]{1,0:T(8,128)(2,1)S(1)} %bitcast.27, ...), custom_call_target="tpu_custom_call" | custom-call | flops 1000000000 | bytes 10000000 | tf_op jit(solution)/shard_map/pallas_call | solution.py:418
  169.8 1.9 %shard_map.107 = (f32[512,2048]{1,0:T(8,128)}, f32[512,512]{1,0:T(8,128)}) custom-call(s32[1]{0:T(128)} %bitcast.9.place_ref, bf16[256,2560]{1,0:T(8,128)(2,1)S(1)} %pad_maximum_fusion.source), custom_call_target="tpu_custom_call" | custom-call | flops 100000000 | bytes 4000000 | tf_op jit(solution)/shard_map/pallas_call | solution.py:314
  171.8 2.0 %shard_map.108 = (f32[512,2048]{1,0:T(8,128)}, f32[512,512]{1,0:T(8,128)}) custom-call(s32[1]{0:T(128)S(6)} %sub.32.place_ref, bf16[256,2560]{1,0:T(8,128)(2,1)S(1)} %collective-permute-done.13.source, f32[512,2048]{1,0:T(8,128)} %get-tuple-element.32.refs_0_, f32[512,512]{1,0:T(8,128)} %get-tuple-element.33.refs_1_), custom_call_target="tpu_custom_call", output_to_operand_aliasing={{0}: (2, {}), {1}: (3, {})} | custom-call | flops 100000000 | bytes 4000000 | tf_op jit(solution)/shard_map/pallas_call | solution.py:314
  (39 shorter events, 2.7 us)
Async XLA Ops:
  14.4 8.9 %copy-start.1 = (s32[1024]{0:T(1024)S(1)}, s32[1024]{0:T(1024)}, u32[]{:S(2)}) copy-start(s32[1024]{0:T(1024)} %param.9) | copy-start | bytes 12292
  19.8 16.8 %all-to-all-start.1 = ((bf16[8,64,512]{2,1,0:T(8,128)(2,1)}), bf16[8,64,512]{2,1,0:T(8,128)(2,1)S(1)}, u32[]{:S(2)}, u32[]{:S(2)}) async-start(bf16[8,64,512]{2,1,0:T(8,128)(2,1)} %bitcast.4), calls=%async_computation.1 | async-start | bytes 1048576 | tf_op jit(solution)/shard_map/all_to_all | solution.py:336
  36.6 0.8 copy-start
  76.2 2.5 %collective-permute-start.6 = (bf16[256,1536]{1,0:T(8,128)(2,1)}, bf16[256,1536]{1,0:T(8,128)(2,1)S(1)}, u32[]{:S(2)}, u32[]{:S(2)}) collective-permute-start(bf16[256,1536]{1,0:T(8,128)(2,1)} %get-tuple-element.31), channel_id=1, source_target_pairs={{0,1},{1,0},{2,3},{3,2},{4,5},{5,4},{6,7},{7,6},{8,9},{9,8},{10,11... | collective-permute-start | bytes 2359304 | tf_op jit(solution)/shard_map/ppermute | solution.py:332
  80.1 7.8 %collective-permute-start.7 = (bf16[128,1536]{1,0:T(8,128)(2,1)S(1)}, bf16[128,1536]{1,0:T(8,128)(2,1)S(1)}, u32[]{:S(2)}, u32[]{:S(2)}) collective-permute-start(bf16[128,1536]{1,0:T(8,128)(2,1)S(1)} %dynamic-slice_bitcast_fusion), channel_id=1, source_target_pairs={{0,4},{1,3},{2,6},{3,1},{4,0},{5,7},{6,2},{7,5},{8,12},{9,11},{10,... | collective-permute-start | bytes 1179656 | tf_op jit(solution)/shard_map/ppermute | solution.py:340
  81.6 18.5 %all-to-all-start.3 = ((bf16[8,64,1024]{2,1,0:T(8,128)(2,1)}), bf16[8,64,1024]{2,1,0:T(8,128)(2,1)S(1)}, u32[]{:S(2)}, u32[]{:S(2)}) async-start(bf16[8,64,1024]{2,1,0:T(8,128)(2,1)} %bitcast.10), calls=%async_computation.3 | async-start | bytes 2097152 | tf_op jit(solution)/shard_map/all_to_all | solution.py:336
  88.0 13.6 %collective-permute-start.8 = (bf16[64,1536]{1,0:T(8,128)(2,1)S(1)}, bf16[64,1536]{1,0:T(8,128)(2,1)S(1)}, u32[]{:S(2)}, u32[]{:S(2)}) collective-permute-start(bf16[64,1536]{1,0:T(8,128)(2,1)S(1)} %dynamic-slice_bitcast_fusion.1), channel_id=1, source_target_pairs={{0,2},{1,5},{2,0},{3,7},{4,6},{5,1},{6,4},{7,3},{8,10},{9,13},{10,... | collective-permute-start | bytes 589832 | tf_op jit(solution)/shard_map/ppermute | solution.py:340
  101.7 10.7 %collective-permute-start.9 = (bf16[64,2560]{1,0:T(8,128)(2,1)S(1)}, bf16[64,2560]{1,0:T(8,128)(2,1)S(1)}, u32[]{:S(2)}, u32[]{:S(2)}) collective-permute-start(bf16[64,2560]{1,0:T(8,128)(2,1)S(1)} %pad_maximum_fusion.2), channel_id=1, source_target_pairs={{0,8},{1,17},{2,10},{3,19},{4,12},{5,21},{6,14},{7,23},{8,0},{9,25... | collective-permute-start | bytes 983048 | tf_op jit(solution)/shard_map/ppermute | solution.py:340
  112.4 11.0 %collective-permute-start.10 = (bf16[64,2560]{1,0:T(8,128)(2,1)S(1)}, bf16[64,2560]{1,0:T(8,128)(2,1)S(1)}, u32[]{:S(2)}, u32[]{:S(2)}) collective-permute-start(bf16[64,2560]{1,0:T(8,128)(2,1)S(1)} %add_convert_fusion.2), channel_id=1, source_target_pairs={{0,16},{1,9},{2,18},{3,11},{4,20},{5,13},{6,22},{7,15},{8,24},{9,1... | collective-permute-start | bytes 983048 | tf_op jit(solution)/shard_map/ppermute | solution.py:340
  123.5 8.0 %collective-permute-start.11 = (bf16[64,2560]{1,0:T(8,128)(2,1)S(1)}, bf16[64,2560]{1,0:T(8,128)(2,1)S(1)}, u32[]{:S(2)}, u32[]{:S(2)}) collective-permute-start(bf16[64,2560]{1,0:T(8,128)(2,1)S(1)} %add_convert_fusion.1), channel_id=1, source_target_pairs={{0,2},{1,5},{2,0},{3,7},{4,6},{5,1},{6,4},{7,3},{8,10},{9,13},{10,... | collective-permute-start | bytes 983048 | tf_op jit(solution)/shard_map/ppermute | solution.py:340
  131.6 13.8 %collective-permute-start.12 = (bf16[128,2560]{1,0:T(8,128)(2,1)S(1)}, bf16[128,2560]{1,0:T(8,128)(2,1)S(1)}, u32[]{:S(2)}, u32[]{:S(2)}) collective-permute-start(bf16[128,2560]{1,0:T(8,128)(2,1)S(1)} %pad_maximum_fusion.1), channel_id=1, source_target_pairs={{0,4},{1,3},{2,6},{3,1},{4,0},{5,7},{6,2},{7,5},{8,12},{9,11},{10,... | collective-permute-start | bytes 1966088 | tf_op jit(solution)/shard_map/ppermute | solution.py:340
  139.5 13.7 %all-to-all-start.2 = ((bf16[8,64,512]{2,1,0:T(8,128)(2,1)}), bf16[8,64,512]{2,1,0:T(8,128)(2,1)S(1)}, u32[]{:S(2)}, u32[]{:S(2)}) async-start(bf16[8,64,512]{2,1,0:T(8,128)(2,1)} %bitcast.32), calls=%async_computation.2 | async-start | bytes 1048576 | tf_op jit(solution)/shard_map/all_to_all | solution.py:336
  145.7 26.1 %collective-permute-start.13 = (bf16[256,2560]{1,0:T(8,128)(2,1)S(1)}, bf16[256,2560]{1,0:T(8,128)(2,1)S(1)}, u32[]{:S(2)}, u32[]{:S(2)}) collective-permute-start(bf16[256,2560]{1,0:T(8,128)(2,1)S(1)} %pad_maximum_fusion.source), channel_id=1, source_target_pairs={{0,1},{1,0},{2,3},{3,2},{4,5},{5,4},{6,7},{7,6},{8,9},{9,8},{10,11... | collective-permute-start | bytes 3932168 | tf_op jit(solution)/shard_map/ppermute | solution.py:332
  153.2 9.3 %collective-permute-start.3 = (bf16[512,512]{1,0:T(8,128)(2,1)S(1)}, bf16[512,512]{1,0:T(8,128)(2,1)}, u32[]{:S(2)}, u32[]{:S(2)}) collective-permute-start(bf16[512,512]{1,0:T(8,128)(2,1)S(1)} %bitcast.25), channel_id=1, source_target_pairs={{0,2},{2,0},{1,3},{3,1},{4,6},{6,4},{5,7},{7,5},{8,10},{10,8},{9,1... | collective-permute-start | bytes 1572872 | tf_op jit(solution)/shard_map/ppermute | solution.py:332
  154.5 8.6 %collective-permute-start.1 = (s32[1,512]{1,0:T(1,128)S(1)}, s32[1,512]{1,0:T(1,128)S(1)}, u32[]{:S(2)}, u32[]{:S(2)}) collective-permute-start(s32[1,512]{1,0:T(1,128)S(1)} %reshape.91), channel_id=1, source_target_pairs={{0,1},{1,0},{2,3},{3,2},{4,5},{5,4},{6,7},{7,6},{8,9},{9,8},{10,11... | collective-permute-start | bytes 6152 | tf_op jit(solution)/shard_map/ppermute | solution.py:332
  154.5 8.0 %collective-permute-start = (s32[1,512]{1,0:T(1,128)S(1)}, s32[1,512]{1,0:T(1,128)S(1)}, u32[]{:S(2)}, u32[]{:S(2)}) collective-permute-start(s32[1,512]{1,0:T(1,128)S(1)} %reshape.91), channel_id=1, source_target_pairs={{0,2},{2,0},{1,3},{3,1},{4,6},{6,4},{5,7},{7,5},{8,10},{10,8},{9,1... | collective-permute-start | bytes 6152 | tf_op jit(solution)/shard_map/ppermute | solution.py:332
  156.6 8.1 %collective-permute-start.4 = (bf16[512,512]{1,0:T(8,128)(2,1)S(1)}, bf16[512,512]{1,0:T(8,128)(2,1)S(1)}, u32[]{:S(2)}, u32[]{:S(2)}) collective-permute-start(bf16[512,512]{1,0:T(8,128)(2,1)S(1)} %bitcast.26), channel_id=1, source_target_pairs={{0,1},{1,0},{2,3},{3,2},{4,5},{5,4},{6,7},{7,6},{8,9},{9,8},{10,11... | collective-permute-start | bytes 1572872 | tf_op jit(solution)/shard_map/ppermute | solution.py:332
  162.5 2.1 %collective-permute-start.5 = (bf16[512,512]{1,0:T(8,128)(2,1)}, bf16[512,512]{1,0:T(8,128)(2,1)S(1)}, u32[]{:S(2)}, u32[]{:S(2)}) collective-permute-start(bf16[512,512]{1,0:T(8,128)(2,1)} %collective-permute-done.3.refs_5_), channel_id=1, source_target_pairs={{0,1},{1,0},{2,3},{3,2},{4,5},{5,4},{6,7},{7,6},{8,9},{9,8},{10,11... | collective-permute-start | bytes 1572872 | tf_op jit(solution)/shard_map/ppermute | solution.py:332
  162.5 2.1 %collective-permute-start.2 = (s32[1,512]{1,0:T(1,128)S(1)}, s32[1,512]{1,0:T(1,128)S(1)}, u32[]{:S(2)}, u32[]{:S(2)}) collective-permute-start(s32[1,512]{1,0:T(1,128)S(1)} %collective-permute-done), channel_id=1, source_target_pairs={{0,1},{1,0},{2,3},{3,2},{4,5},{5,4},{6,7},{7,6},{8,9},{9,8},{10,11... | collective-permute-start | bytes 6152 | tf_op jit(solution)/shard_map/ppermute | solution.py:332

commit v6 on v5

--- a/solution.py
+++ b/solution.py
@@ -16,6 +16,7 @@
 GROUPS = ((0, HEADS),)
 VMEM = pl.BlockSpec(memory_space=pltpu.VMEM)
 SMEM = pl.BlockSpec(memory_space=pltpu.SMEM)
+ANY = pl.BlockSpec(memory_space=pl.ANY)
 BF = jnp.bfloat16
 F32 = jnp.float32
 
@@ -80,11 +81,17 @@
         ref[i * rows : (i + 1) * rows, cols] = value[block * rows : (block + 1) * rows, :]
 
 
-def first_kernel(order, len_ref, slot_row, slot_col, rows_ref, win_ref, wout_ref, og_ref, dgated_ref, *refs):
-    count = len(GROUPS)
-    out_ref, wg_ref, nt_ref, dpre_ref = refs[:4]
-    vqk, datt, dsil = (refs[4 + k * count : 4 + (k + 1) * count] for k in range(3))
-    hid, gate, ev, att, gated, dgate, dsil_gate = refs[4 + 3 * count :]
+def first_kernel(order, len_ref, slot_row, slot_col, rows_ref, *refs):
+    sources, targets = refs[:4], refs[4:11]
+    held, kept = refs[11:15], refs[15:22]
+    hid, gate, ev, att, gated, dgate, dsil_gate, sems = refs[22:]
+    loads = [pltpu.make_async_copy(sources[i], held[i], sems.at[i]) for i in range(4)]
+    stores = [pltpu.make_async_copy(kept[i], targets[i], sems.at[4 + i]) for i in range(7)]
+    win_ref, wout_ref, og_ref, dgated_ref = held
+    out_ref, wg_ref, nt_ref, dpre_ref, vqk, datt, dsil = kept
+    vqk, datt, dsil = (vqk,), (datt,), (dsil,)
+    for load in loads:
+        load.start()
     slots, width = rows_ref.shape
     tokens = og_ref.shape[0]
     head = width // HEADS
@@ -92,6 +99,8 @@
     normed, _ = center_rows(rows_ref[...].astype(F32))
     normed = normed.astype(BF)
     nt_ref[...] = normed.T
+    stores[2].start()
+    loads[0].wait()
     for j in range(4):
         cols = slice(j * width, (j + 1) * width)
         pre = mm(normed, win_ref[:, cols])
@@ -106,6 +115,8 @@
                 wide = (h1 - h0) * head
                 ref[:, (j - 1) * wide : j * wide] = slope[:, h0 * head : h1 * head]
 
+    stores[6].start()
+
     def spread(i, _):
         span = pl.ds(pl.multiple_of(i * BLOCK, BLOCK), BLOCK)
         lane = lax.broadcasted_iota(jnp.int32, (BLOCK, slots), 1)
@@ -120,6 +131,9 @@
         return 0
 
     lax.fori_loop(0, tokens // BLOCK, spread, 0)
+    stores[4].start()
+    for load in loads[1:]:
+        load.wait()
     ends = history_ends(len_ref)
 
     def rows_step(i, _):
@@ -161,20 +175,49 @@
         return 0
 
     lax.fori_loop(0, tokens // BLOCK, rows_step, 0)
+    stores[0].start()
+    stores[5].start()
     blocks(wg_ref, order, slice(0, width), tt_mm(gated[...], og_ref[...]).astype(BF))
     slot_sum = mm(one_hot_rows(slot_row, slots), dgate[...])
     dpre = (slot_sum * dsil_gate[...].astype(F32)).astype(BF)
     dpre_ref[...] = dpre
+    stores[3].start()
     blocks(wg_ref, order, slice(width, 2 * width), mm(nt_ref[...], dpre).astype(BF))
-
-
-def second_kernel(
-    heads, len_ref, core_ref, slot_row, vqk_ref, datt_ref, dsil_ref, nt_ref, dpre_ref, keep_ref, give_ref, *sums
-):
-    slots = dpre_ref.shape[0]
-    tokens, wide = datt_ref.shape
+    stores[1].start()
+    for store in stores:
+        store.wait()
+
+
+def second_kernel(len_ref, core_ref, slot_row, *refs):
+    sources, targets = refs[:4], refs[4:7]
+    vqk_ref, datt_ref, dsil_ref, nt_ref, dpre_ref, keep_ref, give_ref, kt = refs[7:15]
+    sums, sems = refs[15:-1], refs[-1]
+    heads, tokens = HEADS, datt_ref.shape[0]
+    slots, wide = dpre_ref.shape[0], datt_ref.shape[1]
     head = wide // heads
     half_scale = 0.5 * head**-0.5
+    steps = tokens // BLOCK
+
+    def loads(i):
+        span = pl.ds(pl.multiple_of(i * BLOCK, BLOCK), BLOCK)
+        return [
+            pltpu.make_async_copy(source.at[span], ref.at[span], sems.at[k * steps + i])
+            for k, (source, ref) in enumerate(((sources[0], vqk_ref), (sources[1], datt_ref)))
+        ]
+
+    late = [
+        pltpu.make_async_copy(source, ref, sems.at[2 * steps + k])
+        for k, (source, ref) in enumerate(((sources[2], dsil_ref), (sources[3], nt_ref)))
+    ]
+    stores = [
+        pltpu.make_async_copy(ref, target, sems.at[2 * steps + 2 + k])
+        for k, (ref, target) in enumerate(zip((dpre_ref, keep_ref, give_ref), targets))
+    ]
+    for i in range(steps):
+        for load in loads(i):
+            load.start()
+    for load in late:
+        load.start()
     ends = history_ends(len_ref)
     for ref in sums:
         ref[...] = jnp.zeros_like(ref)
@@ -182,6 +225,9 @@
     def rows_step(i, _):
         base = pl.multiple_of(i * BLOCK, BLOCK)
         span = pl.ds(base, BLOCK)
+        for load in loads(i):
+            load.wait()
+        kt[:, span] = vqk_ref[span, 2 * wide :].T
         start = history_start(ends, base + lax.broadcasted_iota(jnp.int32, (1, BLOCK), 1))
         place = base + lax.broadcasted_iota(jnp.int32, (BLOCK, BLOCK), 1)
 
@@ -204,27 +250,36 @@
                 uth = u * th
                 w = (u + uth) * allowed
                 ds = dw * ((half + half * th) * (one + (u - uth)))
-                parts.append((mm(w, da), tt_mm(ds, k), mm(ds, q)))
+                parts.append((mm(w, da), mm(kt[lo : lo + head, keys], ds), mm(ds, q)))
             for h in range(heads):
                 sums[3 * h][keys, :] += parts[h][0]
-                sums[3 * h + 1][span, :] += parts[h][1]
+                sums[3 * h + 1][:, span] += parts[h][1]
                 sums[3 * h + 2][keys, :] += parts[h][2]
             return 0
 
         lax.fori_loop(history_start(ends, base) // BLOCK, i + 1, keys_step, 0)
         return 0
 
-    lax.fori_loop(0, tokens // BLOCK, rows_step, 0)
+    lax.fori_loop(0, steps, rows_step, 0)
     put = one_hot_rows(slot_row, slots)
+    for load in late:
+        load.wait()
     for j in range(3):
         parts = [sums[3 * h + j][...].astype(BF) for h in range(heads)]
         cols = slice(j * wide, (j + 1) * wide)
-        slot_sum = mm(put, jnp.concatenate(parts, axis=1) if heads > 1 else parts[0])
+        if j == 1:
+            slot_sum = mm_t(put, jnp.concatenate(parts, axis=0))
+        else:
+            slot_sum = mm(put, jnp.concatenate(parts, axis=1))
         dpre_ref[:, cols] = (slot_sum * dsil_ref[:, cols].astype(F32)).astype(BF)
+    stores[0].start()
     half = nt_ref.shape[0] // 2
-    for ref, place in ((keep_ref, core_ref[0, 0]), (give_ref, 1 - core_ref[0, 0])):
+    for k, ref, place in ((2, give_ref, 1 - core_ref[0, 0]), (1, keep_ref, core_ref[0, 0])):
         span = pl.ds(pl.multiple_of(place * half, half), half)
         ref[...] = mm(nt_ref[span, :], dpre_ref[...]).astype(BF)
+        stores[k].start()
+    for store in stores:
+        store.wait()
 
 
 def slot_kernel(rows_ref, res_ref, win_ref, gate_ref, *refs):
@@ -266,43 +321,51 @@
     lax.fori_loop(0, out.shape[0] // height, step, 0)
 
 
-def call(kernel, outs, scratch, specs, flops, mib=MIB):
+def call(kernel, outs, scratch, specs, flops, mib=MIB, own_copies=0):
+    semaphores = [pltpu.SemaphoreType.DMA((own_copies,))] if own_copies else []
     return pl.pallas_call(
         kernel,
         out_shape=[jax.ShapeDtypeStruct(s, d) for s, d in outs],
         in_specs=specs,
-        out_specs=[VMEM] * len(outs),
-        scratch_shapes=[pltpu.VMEM(s, d) for s, d in scratch],
+        out_specs=[ANY if own_copies else VMEM] * len(outs),
+        scratch_shapes=[pltpu.VMEM(s, d) for s, d in scratch] + semaphores,
         compiler_params=pltpu.CompilerParams(vmem_limit_bytes=mib * 2**20),
         cost_estimate=pl.CostEstimate(flops=flops, bytes_accessed=10**7, transcendentals=0),
     )
 
 
 def call_first(order, tokens, slots, width):
-    wides = [(h1 - h0) * width // HEADS for h0, h1 in GROUPS]
+    loads = [((width, 4 * width), BF), ((width, width), BF), ((tokens, width), BF), ((tokens, width), BF)]
+    outs = [
+        ((tokens, width), BF), ((width, 2 * width), BF), ((width, slots), BF), ((slots, width), BF),
+        ((tokens, 3 * width), BF), ((tokens, width), BF), ((slots, 3 * width), BF),
+    ]
     return call(
         functools.partial(first_kernel, order),
-        [((tokens, width), BF), ((width, 2 * width), BF), ((width, slots), BF), ((slots, width), BF)]
-        + [((tokens, 3 * w), BF) for w in wides]
-        + [((tokens, w), BF) for w in wides]
-        + [((slots, 3 * w), BF) for w in wides],
-        [
+        outs,
+        loads + outs
+        + [
             ((slots, 4 * width), BF), ((tokens, width), BF), ((tokens, width), BF), ((BLOCK, width), F32),
             ((tokens, width), BF), ((tokens, width), BF), ((slots, width), BF),
         ],
-        [SMEM] + [VMEM] * 7,
+        [SMEM] + [VMEM] * 3 + [ANY] * 4,
         10**10,
+        own_copies=len(loads) + len(outs),
     )
 
 
 def call_attention(tokens, slots, width):
     head, grads = width // HEADS, 3 * width
+    loads = [((tokens, grads), BF), ((tokens, width), BF), ((slots, grads), BF), ((width, slots), BF)]
+    outs = [((slots, grads), BF)] + [((width // 2, grads), BF)] * 2
+    sums = [((tokens, head), F32), ((head, tokens), F32), ((tokens, head), F32)] * HEADS
     return call(
-        functools.partial(second_kernel, HEADS),
-        [((slots, grads), BF)] + [((width // 2, grads), BF)] * 2,
-        [((tokens, head), F32)] * (3 * HEADS),
-        [SMEM] * 2 + [VMEM] * 5,
+        second_kernel,
+        outs,
+        loads + outs + [((width, tokens), BF)] + sums,
+        [SMEM] * 2 + [VMEM] + [ANY] * 4,
         10**10,
+        own_copies=2 * (tokens // BLOCK) + 5,
     )
 
 
@@ -354,8 +417,18 @@
     me = lax.axis_index(AXES)
     early = exchange(early.reshape(plane, early.shape[0] // plane, early.shape[1]), PLANE)
     early = jnp.sum(early.astype(F32), axis=0).astype(BF)
+
     by_core = lambda first, second: (lambda d: d ^ (1 << (second if d & 1 else first)))
     upper = lambda first, second: (me >> jnp.where(me & 1 == 1, second, first)) & 1
+    bits = range(3, total.bit_length() - 1)
+
+    def sum_line(x):
+        for first, second in zip(bits, bits[::-1]):
+            got = swap(x, by_core(first, second))
+            x = (x.astype(F32) + got.astype(F32)).astype(BF)
+        return x
+
+    early = sum_line(early)
     got = other_place(give, "s0")
     x = (keep.astype(F32) + got.astype(F32)).astype(BF)
     for first, second in ((2, 1), (1, 2)):
@@ -365,11 +438,7 @@
         give = lax.dynamic_index_in_dim(halves, 1 - place, 0, keepdims=False)
         got = swap(give, by_core(first, second))
         x = (mine.astype(F32) + got.astype(F32)).astype(BF)
-    x = jnp.concatenate([early, x], axis=1)
-    bits = range(3, total.bit_length() - 1)
-    for first, second in zip(bits, bits[::-1]):
-        got = swap(x, by_core(first, second))
-        x = (x.astype(F32) + got.astype(F32)).astype(BF)
+    x = jnp.concatenate([early, sum_line(x)], axis=1)
     for first, second in ((1, 2), (2, 1)):
         got = swap(x, by_core(first, second))
         place = upper(first, second) == 1

time: 174 us -> 170 us (0.977)
  waiting for transfers between devices: 72 us -> 66.9 us
  starting transfers between devices: 19.8 us -> 22.7 us
  Pallas kernels: 56.6 us -> 54 us
    ppermute x6 -> x8, waiting for transfers between devices: 35.6 us -> 30.2 us  [swap(): lax.ppermute(x, AXES, [(d, partner(d)) for d in range(lax.axis_size(AXES))])]
    pallas_call x1, Pallas kernels: 18 us -> 16.1 us  [on_device(): call_attention(tokens, slots, width)]
    ppermute x6 -> x8, starting transfers between devices: 6.27 us -> 7.67 us  [swap(): lax.ppermute(x, AXES, [(d, partner(d)) for d in range(lax.axis_size(AXES))])]
  transfers between devices with their start and end apart: 17 -> 19, of which waited for: 12 -> 14; matrix products, arithmetic and copies ran while one was open for 2% -> 2% of each run, Pallas kernels for 9% -> 9%
where the time goes in v6:
time: 170 us; the launch traced here: 169 us
  waiting for transfers between devices  66.9 us (39%)
  Pallas kernels  54 us (32%)
  starting transfers between devices  22.7 us (13%)
  blocking collectives  13.7 us (8%)
  local copies, waits for them, and re-layouts  7.93 us (5%)
  other arithmetic  2.98 us (2%)
    ppermute x8, waiting for transfers between devices, swap(): lax.ppermute(x, AXES, [(d, partner(d)) for d in range(lax.axis_size(AXES))])  30.2 us
    all_to_all x3, waiting for transfers between devices, exchange(): return lax.all_to_all(x, axes, split_axis=0, concat_axis=0, tiled=True)  26.8 us
    pallas_call x1, Pallas kernels, on_device(): first(lengths, slot_row, slot_col, rows, in_weight, out_weight, out_grad,...  20.1 us
    pallas_call x1, Pallas kernels, on_device(): call_attention(tokens, slots, width)  16.1 us
    all_to_all x1, blocking collectives, exchange(): return lax.all_to_all(x, axes, split_axis=0, concat_axis=0, tiled=True)  13.7 us
    all_to_all x3, starting transfers between devices, exchange(): return lax.all_to_all(x, axes, split_axis=0, concat_axis=0, tiled=True)  12.1 us
    ppermute x8, waiting for transfers between devices, other_place(): return lax.ppermute(x, axis, [(i, i ^ 1) for i in range(size)])  9.87 us
    ppermute x8, starting transfers between devices, swap(): lax.ppermute(x, AXES, [(d, partner(d)) for d in range(lax.axis_size(AXES))])  7.67 us
  transfers between devices with their start and end apart: 19, of which 14 were waited for; matrix products, arithmetic and copies ran while one was open for 2% of the time, Pallas kernels for 9%

profile of v6, /device:TPU:0, one launch (start us, length us, event | category | flops | bytes accessed | tf_op | source)
XLA Modules:
  0.0 169.0 jit_solution(11283020319778697321)
XLA Ops:
  0.6 13.7 %all_to_all.27 = s32[8,1,64]{2,1,0:T(1,128)S(1)} all-to-all(s32[8,1,64]{2,1,0:T(1,128)} %bitcast.40), channel_id=1, replica_groups=mesh['e1'=4,'e0'=2,'s1'=2,'s0'=2] {'e1','e0'}, dimensions={0} | all-to-all | bytes 4096 | tf_op jit(solution)/shard_map/all_to_all | solution.py:399
  14.4 5.4 %gather_fusion = bf16[512,512]{1,0:T(8,128)(2,1)} fusion(bf16[4096,512]{1,0:T(8,128)(2,1)} %param.7, s32[1024]{0:T(1024)S(1)} %pad_clamp_fusion), kind=kCustom, calls=%fused_computation | custom fusion | bytes 1050624 | tf_op jit(solution)/shard_map/gather | solution.py:456
  19.8 3.5 %all-to-all-start.1 = ((bf16[8,64,512]{2,1,0:T(8,128)(2,1)}), bf16[8,64,512]{2,1,0:T(8,128)(2,1)S(1)}, u32[]{:S(2)}, u32[]{:S(2)}) async-start(bf16[8,64,512]{2,1,0:T(8,128)(2,1)} %bitcast.4), calls=%async_computation.1 | async-start | bytes 1048576 | tf_op jit(solution)/shard_map/all_to_all | solution.py:399
  24.4 3.7 %shard_map.102 = (bf16[1024,512]{1,0:T(8,128)(2,1)}, f32[512,512]{1,0:T(8,128)}) custom-call(s32[1,1024]{1,0:T(1,128)} %bitcast.36, bf16[512,512]{1,0:T(8,128)(2,1)} %refs_1_.1, bf16[1024,512]{1,0:T(8,128)(2,1)} %refs_2_.1), custom_call_target="tpu_custom_call" | custom-call | flops 1000000000 | bytes 10000000 | tf_op jit(solution)/shard_map/pallas_call | solution.py:463
  28.0 8.5 %all-to-all-done.1 = bf16[8,64,512]{2,1,0:T(8,128)(2,1)S(1)} async-done(((bf16[8,64,512]{2,1,0:T(8,128)(2,1)}), bf16[8,64,512]{2,1,0:T(8,128)(2,1)S(1)}, u32[]{:S(2)}, u32[]{:S(2)}) %all-to-all-start.1) | async-done | bytes 524320 | tf_op jit(solution)/shard_map/all_to_all | solution.py:399
  37.4 20.1 %shard_map.103 = (bf16[1024,512]{1,0:T(8,128)(2,1)}, bf16[512,1024]{1,0:T(8,128)(2,1)}, bf16[512,512]{1,0:T(8,128)(2,1)}, bf16[512,512]{1,0:T(8,128)(2,1)}, bf16...) custom-call(s32[1,8]{1,0:T(1,128)} %len_ref.3, s32[1,1024]{1,0:T(1,128)} %bitcast.37, ...), custom_call_target="tpu_custom_call" | custom-call | flops 10000000000 | bytes 10000000 | tf_op jit(solution)/shard_map/pallas_call | solution.py:467
  57.4 16.1 %shard_map.104 = (bf16[512,1536]{1,0:T(8,128)(2,1)}, bf16[256,1536]{1,0:T(8,128)(2,1)}, bf16[256,1536]{1,0:T(8,128)(2,1)}) custom-call(s32[1,8]{1,0:T(1,128)} %len_ref.3, s32[1,1]{1,0:T(1,128)} %bitcast.6.core_ref, s32[1,1024]{1,0:T(1,128)} %bitcast.38, bf16[1024,1536]{1,0:T(8,128)(2,1)} %get-tuple-element.24.refs_0_, ...), custom_call_target="tpu_custom_call" | custom-call | flops 10000000000 | bytes 10000000 | tf_op jit(solution)/shard_map/pallas_call | solution.py:471
  73.6 2.5 %collective-permute-done.8 = bf16[256,1536]{1,0:T(8,128)(2,1)S(1)} collective-permute-done((bf16[256,1536]{1,0:T(8,128)(2,1)}, bf16[256,1536]{1,0:T(8,128)(2,1)S(1)}, u32[]{:S(2)}, u32[]{:S(2)}) %collective-permute-start.8) | collective-permute-done | bytes 786464 | tf_op jit(solution)/shard_map/ppermute | solution.py:395
  76.1 1.3 add_convert_fusion
  77.5 1.5 collective-permute-start.9
  79.0 3.7 %all-to-all-start.3 = ((bf16[8,64,1024]{2,1,0:T(8,128)(2,1)}), bf16[8,64,1024]{2,1,0:T(8,128)(2,1)S(1)}, u32[]{:S(2)}, u32[]{:S(2)}) async-start(bf16[8,64,1024]{2,1,0:T(8,128)(2,1)} %bitcast.10), calls=%async_computation.3 | async-start | bytes 2097152 | tf_op jit(solution)/shard_map/all_to_all | solution.py:399
  82.8 2.5 %collective-permute-done.9 = bf16[128,1536]{1,0:T(8,128)(2,1)S(1)} collective-permute-done((bf16[128,1536]{1,0:T(8,128)(2,1)S(1)}, bf16[128,1536]{1,0:T(8,128)(2,1)S(1)}, u32[]{:S(2)}, u32[]{:S(2)}) %collective-permute-start.9) | collective-permute-done | bytes 393248 | tf_op jit(solution)/shard_map/ppermute | solution.py:403
  85.4 1.6 collective-permute-start.10
  87.1 10.5 %all-to-all-done.3 = bf16[8,64,1024]{2,1,0:T(8,128)(2,1)S(1)} async-done(((bf16[8,64,1024]{2,1,0:T(8,128)(2,1)}), bf16[8,64,1024]{2,1,0:T(8,128)(2,1)S(1)}, u32[]{:S(2)}, u32[]{:S(2)}) %all-to-all-start.3) | async-done | bytes 1048608 | tf_op jit(solution)/shard_map/all_to_all | solution.py:399
  98.0 1.1 collective-permute-done.10
  99.9 4.3 %collective-permute-done.6 = bf16[64,1024]{1,0:T(8,128)(2,1)S(1)} collective-permute-done((bf16[64,1024]{1,0:T(8,128)(2,1)S(1)}, bf16[64,1024]{1,0:T(8,128)(2,1)S(1)}, u32[]{:S(2)}, u32[]{:S(2)}) %collective-permute-start.6) | collective-permute-done | bytes 131104 | tf_op jit(solution)/shard_map/ppermute | solution.py:403
  104.7 5.1 %collective-permute-done.11 = bf16[64,1536]{1,0:T(8,128)(2,1)S(1)} collective-permute-done((bf16[64,1536]{1,0:T(8,128)(2,1)S(1)}, bf16[64,1536]{1,0:T(8,128)(2,1)S(1)}, u32[]{:S(2)}, u32[]{:S(2)}) %collective-permute-start.11) | collective-permute-done | bytes 196640 | tf_op jit(solution)/shard_map/ppermute | solution.py:403
  109.9 1.5 collective-permute-done.7
  111.5 5.6 %collective-permute-done.12 = bf16[64,1536]{1,0:T(8,128)(2,1)S(1)} collective-permute-done((bf16[64,1536]{1,0:T(8,128)(2,1)S(1)}, bf16[64,1536]{1,0:T(8,128)(2,1)S(1)}, u32[]{:S(2)}, u32[]{:S(2)}) %collective-permute-start.12) | collective-permute-done | bytes 196640 | tf_op jit(solution)/shard_map/ppermute | solution.py:403
  117.1 1.5 collective-permute-start.13
  118.6 8.0 %collective-permute-done.13 = bf16[64,2560]{1,0:T(8,128)(2,1)S(1)} collective-permute-done((bf16[64,2560]{1,0:T(8,128)(2,1)S(1)}, bf16[64,2560]{1,0:T(8,128)(2,1)S(1)}, u32[]{:S(2)}, u32[]{:S(2)}) %collective-permute-start.13) | collective-permute-done | bytes 327712 | tf_op jit(solution)/shard_map/ppermute | solution.py:403
  126.8 1.4 collective-permute-start.14
  128.3 5.0 %shard_map.105 = bf16[512,512]{1,0:T(8,128)(2,1)} custom-call(bf16[512,512]{1,0:T(8,128)(2,1)} %bitcast.31, f32[512,512]{1,0:T(8,128)} %get-tuple-element.22.res_ref, bf16[512,2048]{1,0:T(8,128)(2,1)} %win_ref.1, bf16[512,512]{1,0:T(8,128)(2,1)} %get-tuple-element.23.gate_ref, bf16[512,1536]{1,0:T(8,128)(2,1)} %get-tuple-element.28.refs_0_), custom_call_target="tpu_custom_call" | custom-call | flops 1000000000 | bytes 10000000 | tf_op jit(solution)/shard_map/pallas_call | solution.py:475
  133.3 4.9 %all-to-all-start.2 = ((bf16[8,64,512]{2,1,0:T(8,128)(2,1)}), bf16[8,64,512]{2,1,0:T(8,128)(2,1)S(1)}, u32[]{:S(2)}, u32[]{:S(2)}) async-start(bf16[8,64,512]{2,1,0:T(8,128)(2,1)} %bitcast.32), calls=%async_computation.2 | async-start | bytes 1048576 | tf_op jit(solution)/shard_map/all_to_all | solution.py:399
  138.2 2.1 %collective-permute-done.14 = bf16[128,2560]{1,0:T(8,128)(2,1)S(1)} collective-permute-done((bf16[128,2560]{1,0:T(8,128)(2,1)S(1)}, bf16[128,2560]{1,0:T(8,128)(2,1)S(1)}, u32[]{:S(2)}, u32[]{:S(2)}) %collective-permute-start.14) | collective-permute-done | bytes 655392 | tf_op jit(solution)/shard_map/ppermute | solution.py:403
  140.7 7.8 %all-to-all-done.2 = bf16[8,64,512]{2,1,0:T(8,128)(2,1)S(1)} async-done(((bf16[8,64,512]{2,1,0:T(8,128)(2,1)}), bf16[8,64,512]{2,1,0:T(8,128)(2,1)S(1)}, u32[]{:S(2)}, u32[]{:S(2)}) %all-to-all-start.2) | async-done | bytes 524320 | tf_op jit(solution)/shard_map/all_to_all | solution.py:399
  148.5 1.3 collective-permute-start.3
  152.0 5.8 %collective-permute-done.3.refs_5_ = bf16[512,512]{1,0:T(8,128)(2,1)} collective-permute-done((bf16[512,512]{1,0:T(8,128)(2,1)S(1)}, bf16[512,512]{1,0:T(8,128)(2,1)}, u32[]{:S(2)}, u32[]{:S(2)}) %collective-permute-start.3) | collective-permute-done | bytes 524320 | tf_op jit(solution)/shard_map/ppermute | solution.py:395
  158.3 1.6 collective-permute-done.2
  159.9 5.2 %shard_map.106 = f32[1024,512]{1,0:T(8,128)} custom-call(s32[1,512]{1,0:T(1,128)S(1)} %broadcast_subtract_fusion.3.refs_0_, s32[1,512]{1,0:T(1,128)S(1)} %broadcast_subtract_fusion.2.refs_1_, s32[1,512]{1,0:T(1,128)S(1)} %broadcast_subtract_fusion.1.refs_2_, s32[1,512]{1,0:T(1,128)S(1)} %broadcast_subtract_fusion.refs_3_, bf16[512,512]{1,0:T(8,128)(2,1)S(1)} %bitcast.27, ...), custom_call_target="tpu_custom_call" | custom-call | flops 1000000000 | bytes 10000000 | tf_op jit(solution)/shard_map/pallas_call | solution.py:487
  165.1 1.9 %shard_map.107 = (f32[512,2048]{1,0:T(8,128)}, f32[512,512]{1,0:T(8,128)}) custom-call(s32[1]{0:T(128)} %bitcast.9.place_ref, bf16[256,2560]{1,0:T(8,128)(2,1)S(1)} %pad_maximum_fusion.source), custom_call_target="tpu_custom_call" | custom-call | flops 100000000 | bytes 4000000 | tf_op jit(solution)/shard_map/pallas_call | solution.py:377
  167.0 2.0 %shard_map.108 = (f32[512,2048]{1,0:T(8,128)}, f32[512,512]{1,0:T(8,128)}) custom-call(s32[1]{0:T(128)S(6)} %sub.32.place_ref, bf16[256,2560]{1,0:T(8,128)(2,1)S(1)} %collective-permute-done.15.source, f32[512,2048]{1,0:T(8,128)} %get-tuple-element.32.refs_0_, f32[512,512]{1,0:T(8,128)} %get-tuple-element.33.refs_1_), custom_call_target="tpu_custom_call", output_to_operand_aliasing={{0}: (2, {}), {1}: (3, {})} | custom-call | flops 100000000 | bytes 4000000 | tf_op jit(solution)/shard_map/pallas_call | solution.py:377
  (45 shorter events, 7.4 us)
Async XLA Ops:
  14.4 8.9 %copy-start.1 = (s32[1024]{0:T(1024)S(1)}, s32[1024]{0:T(1024)}, u32[]{:S(2)}) copy-start(s32[1024]{0:T(1024)} %param.9) | copy-start | bytes 12292
  19.8 16.8 %all-to-all-start.1 = ((bf16[8,64,512]{2,1,0:T(8,128)(2,1)}), bf16[8,64,512]{2,1,0:T(8,128)(2,1)S(1)}, u32[]{:S(2)}, u32[]{:S(2)}) async-start(bf16[8,64,512]{2,1,0:T(8,128)(2,1)} %bitcast.4), calls=%async_computation.1 | async-start | bytes 1048576 | tf_op jit(solution)/shard_map/all_to_all | solution.py:399
  36.6 0.8 copy-start
  73.5 2.6 %collective-permute-start.8 = (bf16[256,1536]{1,0:T(8,128)(2,1)}, bf16[256,1536]{1,0:T(8,128)(2,1)S(1)}, u32[]{:S(2)}, u32[]{:S(2)}) collective-permute-start(bf16[256,1536]{1,0:T(8,128)(2,1)} %get-tuple-element.31), channel_id=1, source_target_pairs={{0,1},{1,0},{2,3},{3,2},{4,5},{5,4},{6,7},{7,6},{8,9},{9,8},{10,11... | collective-permute-start | bytes 2359304 | tf_op jit(solution)/shard_map/ppermute | solution.py:395
  77.5 7.8 %collective-permute-start.9 = (bf16[128,1536]{1,0:T(8,128)(2,1)S(1)}, bf16[128,1536]{1,0:T(8,128)(2,1)S(1)}, u32[]{:S(2)}, u32[]{:S(2)}) collective-permute-start(bf16[128,1536]{1,0:T(8,128)(2,1)S(1)} %dynamic-slice_bitcast_fusion), channel_id=1, source_target_pairs={{0,4},{1,3},{2,6},{3,1},{4,0},{5,7},{6,2},{7,5},{8,12},{9,11},{10,... | collective-permute-start | bytes 1179656 | tf_op jit(solution)/shard_map/ppermute | solution.py:403
  79.0 18.5 %all-to-all-start.3 = ((bf16[8,64,1024]{2,1,0:T(8,128)(2,1)}), bf16[8,64,1024]{2,1,0:T(8,128)(2,1)S(1)}, u32[]{:S(2)}, u32[]{:S(2)}) async-start(bf16[8,64,1024]{2,1,0:T(8,128)(2,1)} %bitcast.10), calls=%async_computation.3 | async-start | bytes 2097152 | tf_op jit(solution)/shard_map/all_to_all | solution.py:399
  85.4 13.6 %collective-permute-start.10 = (bf16[64,1536]{1,0:T(8,128)(2,1)S(1)}, bf16[64,1536]{1,0:T(8,128)(2,1)S(1)}, u32[]{:S(2)}, u32[]{:S(2)}) collective-permute-start(bf16[64,1536]{1,0:T(8,128)(2,1)S(1)} %dynamic-slice_bitcast_fusion.1), channel_id=1, source_target_pairs={{0,2},{1,5},{2,0},{3,7},{4,6},{5,1},{6,4},{7,3},{8,10},{9,13},{10,... | collective-permute-start | bytes 589832 | tf_op jit(solution)/shard_map/ppermute | solution.py:403
  97.7 6.5 %collective-permute-start.6 = (bf16[64,1024]{1,0:T(8,128)(2,1)S(1)}, bf16[64,1024]{1,0:T(8,128)(2,1)S(1)}, u32[]{:S(2)}, u32[]{:S(2)}) collective-permute-start(bf16[64,1024]{1,0:T(8,128)(2,1)S(1)} %reduce_sum.12), channel_id=1, source_target_pairs={{0,8},{1,17},{2,10},{3,19},{4,12},{5,21},{6,14},{7,23},{8,0},{9,25... | collective-permute-start | bytes 393224 | tf_op jit(solution)/shard_map/ppermute | solution.py:403
  99.1 10.7 %collective-permute-start.11 = (bf16[64,1536]{1,0:T(8,128)(2,1)S(1)}, bf16[64,1536]{1,0:T(8,128)(2,1)S(1)}, u32[]{:S(2)}, u32[]{:S(2)}) collective-permute-start(bf16[64,1536]{1,0:T(8,128)(2,1)S(1)} %fusion.1), channel_id=1, source_target_pairs={{0,8},{1,17},{2,10},{3,19},{4,12},{5,21},{6,14},{7,23},{8,0},{9,25... | collective-permute-start | bytes 589832 | tf_op jit(solution)/shard_map/ppermute | solution.py:403
  104.2 7.2 %collective-permute-start.7 = (bf16[64,1024]{1,0:T(8,128)(2,1)S(1)}, bf16[64,1024]{1,0:T(8,128)(2,1)S(1)}, u32[]{:S(2)}, u32[]{:S(2)}) collective-permute-start(bf16[64,1024]{1,0:T(8,128)(2,1)S(1)} %add_convert_fusion.4), channel_id=1, source_target_pairs={{0,16},{1,9},{2,18},{3,11},{4,20},{5,13},{6,22},{7,15},{8,24},{9,1... | collective-permute-start | bytes 393224 | tf_op jit(solution)/shard_map/ppermute | solution.py:403
  109.8 7.2 %collective-permute-start.12 = (bf16[64,1536]{1,0:T(8,128)(2,1)S(1)}, bf16[64,1536]{1,0:T(8,128)(2,1)S(1)}, u32[]{:S(2)}, u32[]{:S(2)}) collective-permute-start(bf16[64,1536]{1,0:T(8,128)(2,1)S(1)} %add_convert_fusion.2), channel_id=1, source_target_pairs={{0,16},{1,9},{2,18},{3,11},{4,20},{5,13},{6,22},{7,15},{8,24},{9,1... | collective-permute-start | bytes 589832 | tf_op jit(solution)/shard_map/ppermute | solution.py:403
  117.1 9.5 %collective-permute-start.13 = (bf16[64,2560]{1,0:T(8,128)(2,1)S(1)}, bf16[64,2560]{1,0:T(8,128)(2,1)S(1)}, u32[]{:S(2)}, u32[]{:S(2)}) collective-permute-start(bf16[64,2560]{1,0:T(8,128)(2,1)S(1)} %pad_maximum_fusion.2), channel_id=1, source_target_pairs={{0,2},{1,5},{2,0},{3,7},{4,6},{5,1},{6,4},{7,3},{8,10},{9,13},{10,... | collective-permute-start | bytes 983048 | tf_op jit(solution)/shard_map/ppermute | solution.py:403
  126.8 13.5 %collective-permute-start.14 = (bf16[128,2560]{1,0:T(8,128)(2,1)S(1)}, bf16[128,2560]{1,0:T(8,128)(2,1)S(1)}, u32[]{:S(2)}, u32[]{:S(2)}) collective-permute-start(bf16[128,2560]{1,0:T(8,128)(2,1)S(1)} %pad_maximum_fusion.1), channel_id=1, source_target_pairs={{0,4},{1,3},{2,6},{3,1},{4,0},{5,7},{6,2},{7,5},{8,12},{9,11},{10,... | collective-permute-start | bytes 1966088 | tf_op jit(solution)/shard_map/ppermute | solution.py:403
  133.3 15.2 %all-to-all-start.2 = ((bf16[8,64,512]{2,1,0:T(8,128)(2,1)}), bf16[8,64,512]{2,1,0:T(8,128)(2,1)S(1)}, u32[]{:S(2)}, u32[]{:S(2)}) async-start(bf16[8,64,512]{2,1,0:T(8,128)(2,1)} %bitcast.32), calls=%async_computation.2 | async-start | bytes 1048576 | tf_op jit(solution)/shard_map/all_to_all | solution.py:399
  140.6 26.4 %collective-permute-start.15 = (bf16[256,2560]{1,0:T(8,128)(2,1)S(1)}, bf16[256,2560]{1,0:T(8,128)(2,1)S(1)}, u32[]{:S(2)}, u32[]{:S(2)}) collective-permute-start(bf16[256,2560]{1,0:T(8,128)(2,1)S(1)} %pad_maximum_fusion.source), channel_id=1, source_target_pairs={{0,1},{1,0},{2,3},{3,2},{4,5},{5,4},{6,7},{7,6},{8,9},{9,8},{10,11... | collective-permute-start | bytes 3932168 | tf_op jit(solution)/shard_map/ppermute | solution.py:395
  148.5 9.3 %collective-permute-start.3 = (bf16[512,512]{1,0:T(8,128)(2,1)S(1)}, bf16[512,512]{1,0:T(8,128)(2,1)}, u32[]{:S(2)}, u32[]{:S(2)}) collective-permute-start(bf16[512,512]{1,0:T(8,128)(2,1)S(1)} %bitcast.25), channel_id=1, source_target_pairs={{0,2},{2,0},{1,3},{3,1},{4,6},{6,4},{5,7},{7,5},{8,10},{10,8},{9,1... | collective-permute-start | bytes 1572872 | tf_op jit(solution)/shard_map/ppermute | solution.py:395
  151.0 7.3 %collective-permute-start.1 = (s32[1,512]{1,0:T(1,128)S(1)}, s32[1,512]{1,0:T(1,128)S(1)}, u32[]{:S(2)}, u32[]{:S(2)}) collective-permute-start(s32[1,512]{1,0:T(1,128)S(1)} %reshape.91), channel_id=1, source_target_pairs={{0,1},{1,0},{2,3},{3,2},{4,5},{5,4},{6,7},{7,6},{8,9},{9,8},{10,11... | collective-permute-start | bytes 6152 | tf_op jit(solution)/shard_map/ppermute | solution.py:395
  151.0 6.8 %collective-permute-start = (s32[1,512]{1,0:T(1,128)S(1)}, s32[1,512]{1,0:T(1,128)S(1)}, u32[]{:S(2)}, u32[]{:S(2)}) collective-permute-start(s32[1,512]{1,0:T(1,128)S(1)} %reshape.91), channel_id=1, source_target_pairs={{0,2},{2,0},{1,3},{3,1},{4,6},{6,4},{5,7},{7,5},{8,10},{10,8},{9,1... | collective-permute-start | bytes 6152 | tf_op jit(solution)/shard_map/ppermute | solution.py:395
  151.8 8.1 %collective-permute-start.4 = (bf16[512,512]{1,0:T(8,128)(2,1)S(1)}, bf16[512,512]{1,0:T(8,128)(2,1)S(1)}, u32[]{:S(2)}, u32[]{:S(2)}) collective-permute-start(bf16[512,512]{1,0:T(8,128)(2,1)S(1)} %bitcast.26), channel_id=1, source_target_pairs={{0,1},{1,0},{2,3},{3,2},{4,5},{5,4},{6,7},{7,6},{8,9},{9,8},{10,11... | collective-permute-start | bytes 1572872 | tf_op jit(solution)/shard_map/ppermute | solution.py:395
  157.8 2.1 %collective-permute-start.5 = (bf16[512,512]{1,0:T(8,128)(2,1)}, bf16[512,512]{1,0:T(8,128)(2,1)S(1)}, u32[]{:S(2)}, u32[]{:S(2)}) collective-permute-start(bf16[512,512]{1,0:T(8,128)(2,1)} %collective-permute-done.3.refs_5_), channel_id=1, source_target_pairs={{0,1},{1,0},{2,3},{3,2},{4,5},{5,4},{6,7},{7,6},{8,9},{9,8},{10,11... | collective-permute-start | bytes 1572872 | tf_op jit(solution)/shard_map/ppermute | solution.py:395
  157.8 2.1 %collective-permute-start.2 = (s32[1,512]{1,0:T(1,128)S(1)}, s32[1,512]{1,0:T(1,128)S(1)}, u32[]{:S(2)}, u32[]{:S(2)}) collective-permute-start(s32[1,512]{1,0:T(1,128)S(1)} %collective-permute-done), channel_id=1, source_target_pairs={{0,1},{1,0},{2,3},{3,2},{4,5},{5,4},{6,7},{7,6},{8,9},{9,8},{10,11... | collective-permute-start | bytes 6152 | tf_op jit(solution)/shard_map/ppermute | solution.py:395

commit v7 on v6

--- a/solution.py
+++ b/solution.py
@@ -189,9 +189,10 @@
 
 
 def second_kernel(len_ref, core_ref, slot_row, *refs):
-    sources, targets = refs[:4], refs[4:7]
-    vqk_ref, datt_ref, dsil_ref, nt_ref, dpre_ref, keep_ref, give_ref, kt = refs[7:15]
-    sums, sems = refs[15:-1], refs[-1]
+    sources, targets = refs[:8], refs[8:11]
+    vqk_ref, datt_ref, dsil_ref, nt_ref, win_ref, rows_ref, res_ref, gate_ref = refs[11:19]
+    grad_ref, keep_ref, give_ref, dpre_ref, kt = refs[19:24]
+    sums, sems = refs[24:-1], refs[-1]
     heads, tokens = HEADS, datt_ref.shape[0]
     slots, wide = dpre_ref.shape[0], datt_ref.shape[1]
     head = wide // heads
@@ -207,11 +208,11 @@
 
     late = [
         pltpu.make_async_copy(source, ref, sems.at[2 * steps + k])
-        for k, (source, ref) in enumerate(((sources[2], dsil_ref), (sources[3], nt_ref)))
+        for k, (source, ref) in enumerate(zip(sources[2:], refs[13:19]))
     ]
     stores = [
-        pltpu.make_async_copy(ref, target, sems.at[2 * steps + 2 + k])
-        for k, (ref, target) in enumerate(zip((dpre_ref, keep_ref, give_ref), targets))
+        pltpu.make_async_copy(ref, target, sems.at[2 * steps + 6 + k])
+        for k, (ref, target) in enumerate(zip((grad_ref, keep_ref, give_ref), targets))
     ]
     for i in range(steps):
         for load in loads(i):
@@ -264,6 +265,7 @@
     put = one_hot_rows(slot_row, slots)
     for load in late:
         load.wait()
+    dn = mm_t(gate_ref[...], win_ref[:, :wide])
     for j in range(3):
         parts = [sums[3 * h + j][...].astype(BF) for h in range(heads)]
         cols = slice(j * wide, (j + 1) * wide)
@@ -271,7 +273,11 @@
             slot_sum = mm_t(put, jnp.concatenate(parts, axis=0))
         else:
             slot_sum = mm(put, jnp.concatenate(parts, axis=1))
-        dpre_ref[:, cols] = (slot_sum * dsil_ref[:, cols].astype(F32)).astype(BF)
+        dpre = (slot_sum * dsil_ref[:, cols].astype(F32)).astype(BF)
+        dpre_ref[:, cols] = dpre
+        dn = dn + mm_t(dpre, win_ref[:, (j + 1) * wide : (j + 2) * wide])
+    normed, inverse = center_rows(rows_ref[...].astype(F32))
+    grad_ref[...] = (center_back(dn, normed, inverse) + res_ref[...]).astype(BF)
     stores[0].start()
     half = nt_ref.shape[0] // 2
     for k, ref, place in ((2, give_ref, 1 - core_ref[0, 0]), (1, keep_ref, core_ref[0, 0])):
@@ -280,20 +286,6 @@
         stores[k].start()
     for store in stores:
         store.wait()
-
-
-def slot_kernel(rows_ref, res_ref, win_ref, gate_ref, *refs):
-    grad_ref = refs[-1]
-    width = rows_ref.shape[1]
-    head = width // HEADS
-    dn = mm_t(gate_ref[...], win_ref[:, :width])
-    for (h0, h1), ref in zip(GROUPS, refs):
-        wide = (h1 - h0) * head
-        for j in range(3):
-            first = (j + 1) * width + h0 * head
-            dn = dn + mm_t(ref[:, j * wide : (j + 1) * wide], win_ref[:, first : first + wide])
-    normed, inverse = center_rows(rows_ref[...].astype(F32))
-    grad_ref[...] = (center_back(dn, normed, inverse) + res_ref[...]).astype(BF)
 
 
 def lay_kernel(place_ref, source, *refs):
@@ -356,16 +348,19 @@
 
 def call_attention(tokens, slots, width):
     head, grads = width // HEADS, 3 * width
-    loads = [((tokens, grads), BF), ((tokens, width), BF), ((slots, grads), BF), ((width, slots), BF)]
-    outs = [((slots, grads), BF)] + [((width // 2, grads), BF)] * 2
+    loads = [
+        ((tokens, grads), BF), ((tokens, width), BF), ((slots, grads), BF), ((width, slots), BF),
+        ((width, 4 * width), BF), ((slots, width), BF), ((slots, width), F32), ((slots, width), BF),
+    ]
+    outs = [((slots, width), BF)] + [((width // 2, grads), BF)] * 2
     sums = [((tokens, head), F32), ((head, tokens), F32), ((tokens, head), F32)] * HEADS
     return call(
         second_kernel,
         outs,
-        loads + outs + [((width, tokens), BF)] + sums,
-        [SMEM] * 2 + [VMEM] + [ANY] * 4,
+        loads + outs + [((slots, grads), BF), ((width, tokens), BF)] + sums,
+        [SMEM] * 2 + [VMEM] + [ANY] * 8,
         10**10,
-        own_copies=2 * (tokens // BLOCK) + 5,
+        own_copies=2 * (tokens // BLOCK) + 9,
     )
 
 
@@ -468,14 +463,10 @@
     layer_out, wg, nt, dpre_gate = outs[:4]
     vqk, datt, dsil = (outs[4 + k * count : 4 + (k + 1) * count] for k in range(3))
 
-    dpre, keep, give = call_attention(tokens, slots, width)(
-        lengths, core, slot_row, vqk[0], datt[0], dsil[0], nt
+    slot_grad, keep, give = call_attention(tokens, slots, width)(
+        lengths, core, slot_row, vqk[0], datt[0], dsil[0], nt, in_weight, rows, res, dpre_gate
     )
     own, got = weight_sum(wg, keep, give)
-    (slot_grad,) = call(slot_kernel, [((slots, width), BF)], [], [VMEM] * (4 + count), 10**9)(
-        rows, res, in_weight, dpre_gate, dpre
-    )
-
     returned = exchange(slot_grad.reshape(requests.shape + (width,)), emb)
     arrays, places = [returned.reshape(slots, width)], [asked.reshape(1, slots)]
     for axis in ("s1", "s0"):

time: 170 us -> 168 us (0.988)
  Pallas kernels: 54 us -> 50.3 us
  waiting for transfers between devices: 66.9 us -> 69.5 us
    pallas_call x1 -> x0, Pallas kernels: 5.02 us -> none  [on_device(): call(slot_kernel, [((slots, width), BF)], [], [VMEM] * (4 + count), 10 ** 9)]
    all_to_all x3, waiting for transfers between devices: 26.8 us -> 23.9 us  [exchange(): return lax.all_to_all(x, axes, split_axis=0, concat_axis=0, tiled=True)]
    ppermute x8, waiting for transfers between devices: 30.2 us -> 33.1 us  [swap(): lax.ppermute(x, AXES, [(d, partner(d)) for d in range(lax.axis_size(AXES))])]
    ppermute x8, waiting for transfers between devices: 9.87 us -> 12.5 us  [other_place(): return lax.ppermute(x, axis, [(i, i ^ 1) for i in range(size)])]
  transfers between devices with their start and end apart: 19 -> 19, of which waited for: 14 -> 16; matrix products, arithmetic and copies ran while one was open for 2% -> 2% of each run, Pallas kernels for 9% -> 6%
where the time goes in v7:
time: 168 us
  waiting for transfers between devices  69.5 us (41%)
  Pallas kernels  50.3 us (30%)
  starting transfers between devices  22.5 us (13%)
  blocking collectives  13.7 us (8%)
  local copies, waits for them, and re-layouts  7.95 us (5%)
  other arithmetic  2.99 us (2%)
    ppermute x8, waiting for transfers between devices, swap(): lax.ppermute(x, AXES, [(d, partner(d)) for d in range(lax.axis_size(AXES))])  33.1 us
    all_to_all x3, waiting for transfers between devices, exchange(): return lax.all_to_all(x, axes, split_axis=0, concat_axis=0, tiled=True)  23.9 us
    pallas_call x1, Pallas kernels, on_device(): first(lengths, slot_row, slot_col, rows, in_weight, out_weight, out_grad,...  20.1 us
    pallas_call x1, Pallas kernels, on_device(): call_attention(tokens, slots, width)  17.5 us
    all_to_all x1, blocking collectives, exchange(): return lax.all_to_all(x, axes, split_axis=0, concat_axis=0, tiled=True)  13.7 us
    ppermute x8, waiting for transfers between devices, other_place(): return lax.ppermute(x, axis, [(i, i ^ 1) for i in range(size)])  12.5 us
    all_to_all x3, starting transfers between devices, exchange(): return lax.all_to_all(x, axes, split_axis=0, concat_axis=0, tiled=True)  12.1 us
    ppermute x8, starting transfers between devices, swap(): lax.ppermute(x, AXES, [(d, partner(d)) for d in range(lax.axis_size(AXES))])  7.72 us
  transfers between devices with their start and end apart: 19, of which 16 were waited for; matrix products, arithmetic and copies ran while one was open for 2% of the time, Pallas kernels for 6%

profile of v7, /device:TPU:0, one launch (start us, length us, event | category | flops | bytes accessed | tf_op | source)
XLA Modules:
  0.0 167.8 jit_solution(1304197570066362540)
XLA Ops:
  0.6 13.7 %all_to_all.27 = s32[8,1,64]{2,1,0:T(1,128)S(1)} all-to-all(s32[8,1,64]{2,1,0:T(1,128)} %bitcast.39), channel_id=1, replica_groups=mesh['e1'=4,'e0'=2,'s1'=2,'s0'=2] {'e1','e0'}, dimensions={0} | all-to-all | bytes 4096 | tf_op jit(solution)/shard_map/all_to_all | solution.py:394
  14.4 5.4 %gather_fusion = bf16[512,512]{1,0:T(8,128)(2,1)} fusion(bf16[4096,512]{1,0:T(8,128)(2,1)} %param.7, s32[1024]{0:T(1024)S(1)} %pad_clamp_fusion), kind=kCustom, calls=%fused_computation | custom fusion | bytes 1050624 | tf_op jit(solution)/shard_map/gather | solution.py:451
  19.8 3.5 %all-to-all-start.1 = ((bf16[8,64,512]{2,1,0:T(8,128)(2,1)}), bf16[8,64,512]{2,1,0:T(8,128)(2,1)S(1)}, u32[]{:S(2)}, u32[]{:S(2)}) async-start(bf16[8,64,512]{2,1,0:T(8,128)(2,1)} %bitcast.4), calls=%async_computation.1 | async-start | bytes 1048576 | tf_op jit(solution)/shard_map/all_to_all | solution.py:394
  23.3 1.0 copy.14.slot_col
  24.4 3.7 %shard_map.102 = (bf16[1024,512]{1,0:T(8,128)(2,1)}, f32[512,512]{1,0:T(8,128)}) custom-call(s32[1,1024]{1,0:T(1,128)} %bitcast.35, bf16[512,512]{1,0:T(8,128)(2,1)} %refs_1_.1, bf16[1024,512]{1,0:T(8,128)(2,1)} %refs_2_.1), custom_call_target="tpu_custom_call" | custom-call | flops 1000000000 | bytes 10000000 | tf_op jit(solution)/shard_map/pallas_call | solution.py:458
  28.0 8.6 %all-to-all-done.1 = bf16[8,64,512]{2,1,0:T(8,128)(2,1)S(1)} async-done(((bf16[8,64,512]{2,1,0:T(8,128)(2,1)}), bf16[8,64,512]{2,1,0:T(8,128)(2,1)S(1)}, u32[]{:S(2)}, u32[]{:S(2)}) %all-to-all-start.1) | async-done | bytes 524320 | tf_op jit(solution)/shard_map/all_to_all | solution.py:394
  37.4 20.1 %shard_map.103 = (bf16[1024,512]{1,0:T(8,128)(2,1)}, bf16[512,1024]{1,0:T(8,128)(2,1)}, bf16[512,512]{1,0:T(8,128)(2,1)}, bf16[512,512]{1,0:T(8,128)(2,1)}, bf16...) custom-call(s32[1,8]{1,0:T(1,128)} %len_ref.3, s32[1,1024]{1,0:T(1,128)} %bitcast.36, ...), custom_call_target="tpu_custom_call" | custom-call | flops 10000000000 | bytes 10000000 | tf_op jit(solution)/shard_map/pallas_call | solution.py:462
  57.5 17.5 %shard_map.104 = (bf16[512,512]{1,0:T(8,128)(2,1)}, bf16[256,1536]{1,0:T(8,128)(2,1)}, bf16[256,1536]{1,0:T(8,128)(2,1)}) custom-call(s32[1,8]{1,0:T(1,128)} %len_ref.3, s32[1,1]{1,0:T(1,128)} %bitcast.6.core_ref, s32[1,1024]{1,0:T(1,128)} %bitcast.37, bf16[1024,1536]{1,0:T(8,128)(2,1)} %get-tuple-element.22.refs_0_, ...), custom_call_target="tpu_custom_call" | custom-call | flops 10000000000 | bytes 10000000 | tf_op jit(solution)/shard_map/pallas_call | solution.py:466
  75.1 2.5 %collective-permute-done.8 = bf16[256,1536]{1,0:T(8,128)(2,1)S(1)} collective-permute-done((bf16[256,1536]{1,0:T(8,128)(2,1)}, bf16[256,1536]{1,0:T(8,128)(2,1)S(1)}, u32[]{:S(2)}, u32[]{:S(2)}) %collective-permute-start.8) | collective-permute-done | bytes 786464 | tf_op jit(solution)/shard_map/ppermute | solution.py:390
  77.5 1.3 add_convert_fusion
  78.9 1.5 collective-permute-start.9
  80.4 3.7 %all-to-all-start.3 = ((bf16[8,64,1024]{2,1,0:T(8,128)(2,1)}), bf16[8,64,1024]{2,1,0:T(8,128)(2,1)S(1)}, u32[]{:S(2)}, u32[]{:S(2)}) async-start(bf16[8,64,1024]{2,1,0:T(8,128)(2,1)} %bitcast.10), calls=%async_computation.3 | async-start | bytes 2097152 | tf_op jit(solution)/shard_map/all_to_all | solution.py:394
  84.2 2.6 %collective-permute-done.9 = bf16[128,1536]{1,0:T(8,128)(2,1)S(1)} collective-permute-done((bf16[128,1536]{1,0:T(8,128)(2,1)S(1)}, bf16[128,1536]{1,0:T(8,128)(2,1)S(1)}, u32[]{:S(2)}, u32[]{:S(2)}) %collective-permute-start.9) | collective-permute-done | bytes 393248 | tf_op jit(solution)/shard_map/ppermute | solution.py:398
  86.9 1.6 collective-permute-start.10
  88.5 10.5 %all-to-all-done.3 = bf16[8,64,1024]{2,1,0:T(8,128)(2,1)S(1)} async-done(((bf16[8,64,1024]{2,1,0:T(8,128)(2,1)}), bf16[8,64,1024]{2,1,0:T(8,128)(2,1)S(1)}, u32[]{:S(2)}, u32[]{:S(2)}) %all-to-all-start.3) | async-done | bytes 1048608 | tf_op jit(solution)/shard_map/all_to_all | solution.py:394
  99.3 1.1 collective-permute-done.10
  101.3 4.2 %collective-permute-done.6 = bf16[64,1024]{1,0:T(8,128)(2,1)S(1)} collective-permute-done((bf16[64,1024]{1,0:T(8,128)(2,1)S(1)}, bf16[64,1024]{1,0:T(8,128)(2,1)S(1)}, u32[]{:S(2)}, u32[]{:S(2)}) %collective-permute-start.6) | collective-permute-done | bytes 131104 | tf_op jit(solution)/shard_map/ppermute | solution.py:398
  106.1 5.0 %collective-permute-done.11 = bf16[64,1536]{1,0:T(8,128)(2,1)S(1)} collective-permute-done((bf16[64,1536]{1,0:T(8,128)(2,1)S(1)}, bf16[64,1536]{1,0:T(8,128)(2,1)S(1)}, u32[]{:S(2)}, u32[]{:S(2)}) %collective-permute-start.11) | collective-permute-done | bytes 196640 | tf_op jit(solution)/shard_map/ppermute | solution.py:398
  111.3 1.5 collective-permute-done.7
  112.9 5.6 %collective-permute-done.12 = bf16[64,1536]{1,0:T(8,128)(2,1)S(1)} collective-permute-done((bf16[64,1536]{1,0:T(8,128)(2,1)S(1)}, bf16[64,1536]{1,0:T(8,128)(2,1)S(1)}, u32[]{:S(2)}, u32[]{:S(2)}) %collective-permute-start.12) | collective-permute-done | bytes 196640 | tf_op jit(solution)/shard_map/ppermute | solution.py:398
  118.5 1.5 collective-permute-start.13
  120.0 8.0 %collective-permute-done.13 = bf16[64,2560]{1,0:T(8,128)(2,1)S(1)} collective-permute-done((bf16[64,2560]{1,0:T(8,128)(2,1)S(1)}, bf16[64,2560]{1,0:T(8,128)(2,1)S(1)}, u32[]{:S(2)}, u32[]{:S(2)}) %collective-permute-start.13) | collective-permute-done | bytes 327712 | tf_op jit(solution)/shard_map/ppermute | solution.py:398
  128.2 1.4 collective-permute-start.14
  129.7 4.9 %all-to-all-start.2 = ((bf16[8,64,512]{2,1,0:T(8,128)(2,1)}), bf16[8,64,512]{2,1,0:T(8,128)(2,1)S(1)}, u32[]{:S(2)}, u32[]{:S(2)}) async-start(bf16[8,64,512]{2,1,0:T(8,128)(2,1)} %bitcast.7), calls=%async_computation.2 | async-start | bytes 1048576 | tf_op jit(solution)/shard_map/all_to_all | solution.py:394
  134.5 5.0 %collective-permute-done.14 = bf16[128,2560]{1,0:T(8,128)(2,1)S(1)} collective-permute-done((bf16[128,2560]{1,0:T(8,128)(2,1)S(1)}, bf16[128,2560]{1,0:T(8,128)(2,1)S(1)}, u32[]{:S(2)}, u32[]{:S(2)}) %collective-permute-start.14) | collective-permute-done | bytes 655392 | tf_op jit(solution)/shard_map/ppermute | solution.py:398
  140.0 4.9 %all-to-all-done.2 = bf16[8,64,512]{2,1,0:T(8,128)(2,1)S(1)} async-done(((bf16[8,64,512]{2,1,0:T(8,128)(2,1)}), bf16[8,64,512]{2,1,0:T(8,128)(2,1)S(1)}, u32[]{:S(2)}, u32[]{:S(2)}) %all-to-all-start.2) | async-done | bytes 524320 | tf_op jit(solution)/shard_map/all_to_all | solution.py:394
  144.8 1.3 collective-permute-start.3
  148.1 7.8 %collective-permute-done = s32[1,512]{1,0:T(1,128)S(1)} collective-permute-done((s32[1,512]{1,0:T(1,128)S(1)}, s32[1,512]{1,0:T(1,128)S(1)}, u32[]{:S(2)}, u32[]{:S(2)}) %collective-permute-start) | collective-permute-done | bytes 2080 | tf_op jit(solution)/shard_map/ppermute | solution.py:390
  157.1 0.9 collective-permute-done.4.refs_6_
  158.7 5.2 %shard_map.105 = f32[1024,512]{1,0:T(8,128)} custom-call(s32[1,512]{1,0:T(1,128)S(1)} %broadcast_subtract_fusion.3.refs_0_, s32[1,512]{1,0:T(1,128)S(1)} %broadcast_subtract_fusion.2.refs_1_, s32[1,512]{1,0:T(1,128)S(1)} %broadcast_subtract_fusion.1.refs_2_, s32[1,512]{1,0:T(1,128)S(1)} %broadcast_subtract_fusion.refs_3_, bf16[512,512]{1,0:T(8,128)(2,1)S(1)} %bitcast.27, ...), custom_call_target="tpu_custom_call" | custom-call | flops 1000000000 | bytes 10000000 | tf_op jit(solution)/shard_map/pallas_call | solution.py:478
  163.9 1.9 %shard_map.106 = (f32[512,2048]{1,0:T(8,128)}, f32[512,512]{1,0:T(8,128)}) custom-call(s32[1]{0:T(128)} %bitcast.9.place_ref, bf16[256,2560]{1,0:T(8,128)(2,1)S(1)} %pad_maximum_fusion.source), custom_call_target="tpu_custom_call" | custom-call | flops 100000000 | bytes 4000000 | tf_op jit(solution)/shard_map/pallas_call | solution.py:372
  165.8 2.0 %shard_map.107 = (f32[512,2048]{1,0:T(8,128)}, f32[512,512]{1,0:T(8,128)}) custom-call(s32[1]{0:T(128)S(6)} %sub.32.place_ref, bf16[256,2560]{1,0:T(8,128)(2,1)S(1)} %collective-permute-done.15.source, f32[512,2048]{1,0:T(8,128)} %get-tuple-element.32.refs_0_, f32[512,512]{1,0:T(8,128)} %get-tuple-element.33.refs_1_), custom_call_target="tpu_custom_call", output_to_operand_aliasing={{0}: (2, {}), {1}: (3, {})} | custom-call | flops 100000000 | bytes 4000000 | tf_op jit(solution)/shard_map/pallas_call | solution.py:372
  (44 shorter events, 7.5 us)
Async XLA Ops:
  14.4 8.9 %copy-start.1 = (s32[1024]{0:T(1024)S(1)}, s32[1024]{0:T(1024)}, u32[]{:S(2)}) copy-start(s32[1024]{0:T(1024)} %param.9) | copy-start | bytes 12292
  19.8 16.8 %all-to-all-start.1 = ((bf16[8,64,512]{2,1,0:T(8,128)(2,1)}), bf16[8,64,512]{2,1,0:T(8,128)(2,1)S(1)}, u32[]{:S(2)}, u32[]{:S(2)}) async-start(bf16[8,64,512]{2,1,0:T(8,128)(2,1)} %bitcast.4), calls=%async_computation.1 | async-start | bytes 1048576 | tf_op jit(solution)/shard_map/all_to_all | solution.py:394
  36.6 0.8 copy-start
  75.0 2.6 %collective-permute-start.8 = (bf16[256,1536]{1,0:T(8,128)(2,1)}, bf16[256,1536]{1,0:T(8,128)(2,1)S(1)}, u32[]{:S(2)}, u32[]{:S(2)}) collective-permute-start(bf16[256,1536]{1,0:T(8,128)(2,1)} %get-tuple-element.31), channel_id=1, source_target_pairs={{0,1},{1,0},{2,3},{3,2},{4,5},{5,4},{6,7},{7,6},{8,9},{9,8},{10,11... | collective-permute-start | bytes 2359304 | tf_op jit(solution)/shard_map/ppermute | solution.py:390
  78.9 7.8 %collective-permute-start.9 = (bf16[128,1536]{1,0:T(8,128)(2,1)S(1)}, bf16[128,1536]{1,0:T(8,128)(2,1)S(1)}, u32[]{:S(2)}, u32[]{:S(2)}) collective-permute-start(bf16[128,1536]{1,0:T(8,128)(2,1)S(1)} %dynamic-slice_bitcast_fusion), channel_id=1, source_target_pairs={{0,4},{1,3},{2,6},{3,1},{4,0},{5,7},{6,2},{7,5},{8,12},{9,11},{10,... | collective-permute-start | bytes 1179656 | tf_op jit(solution)/shard_map/ppermute | solution.py:398
  80.4 18.5 %all-to-all-start.3 = ((bf16[8,64,1024]{2,1,0:T(8,128)(2,1)}), bf16[8,64,1024]{2,1,0:T(8,128)(2,1)S(1)}, u32[]{:S(2)}, u32[]{:S(2)}) async-start(bf16[8,64,1024]{2,1,0:T(8,128)(2,1)} %bitcast.10), calls=%async_computation.3 | async-start | bytes 2097152 | tf_op jit(solution)/shard_map/all_to_all | solution.py:394
  86.9 13.6 %collective-permute-start.10 = (bf16[64,1536]{1,0:T(8,128)(2,1)S(1)}, bf16[64,1536]{1,0:T(8,128)(2,1)S(1)}, u32[]{:S(2)}, u32[]{:S(2)}) collective-permute-start(bf16[64,1536]{1,0:T(8,128)(2,1)S(1)} %dynamic-slice_bitcast_fusion.1), channel_id=1, source_target_pairs={{0,2},{1,5},{2,0},{3,7},{4,6},{5,1},{6,4},{7,3},{8,10},{9,13},{10,... | collective-permute-start | bytes 589832 | tf_op jit(solution)/shard_map/ppermute | solution.py:398
  99.1 6.5 %collective-permute-start.6 = (bf16[64,1024]{1,0:T(8,128)(2,1)S(1)}, bf16[64,1024]{1,0:T(8,128)(2,1)S(1)}, u32[]{:S(2)}, u32[]{:S(2)}) collective-permute-start(bf16[64,1024]{1,0:T(8,128)(2,1)S(1)} %reduce_sum.12), channel_id=1, source_target_pairs={{0,8},{1,17},{2,10},{3,19},{4,12},{5,21},{6,14},{7,23},{8,0},{9,25... | collective-permute-start | bytes 393224 | tf_op jit(solution)/shard_map/ppermute | solution.py:398
  100.5 10.7 %collective-permute-start.11 = (bf16[64,1536]{1,0:T(8,128)(2,1)S(1)}, bf16[64,1536]{1,0:T(8,128)(2,1)S(1)}, u32[]{:S(2)}, u32[]{:S(2)}) collective-permute-start(bf16[64,1536]{1,0:T(8,128)(2,1)S(1)} %fusion.1), channel_id=1, source_target_pairs={{0,8},{1,17},{2,10},{3,19},{4,12},{5,21},{6,14},{7,23},{8,0},{9,25... | collective-permute-start | bytes 589832 | tf_op jit(solution)/shard_map/ppermute | solution.py:398
  105.6 7.2 %collective-permute-start.7 = (bf16[64,1024]{1,0:T(8,128)(2,1)S(1)}, bf16[64,1024]{1,0:T(8,128)(2,1)S(1)}, u32[]{:S(2)}, u32[]{:S(2)}) collective-permute-start(bf16[64,1024]{1,0:T(8,128)(2,1)S(1)} %add_convert_fusion.4), channel_id=1, source_target_pairs={{0,16},{1,9},{2,18},{3,11},{4,20},{5,13},{6,22},{7,15},{8,24},{9,1... | collective-permute-start | bytes 393224 | tf_op jit(solution)/shard_map/ppermute | solution.py:398
  111.2 7.2 %collective-permute-start.12 = (bf16[64,1536]{1,0:T(8,128)(2,1)S(1)}, bf16[64,1536]{1,0:T(8,128)(2,1)S(1)}, u32[]{:S(2)}, u32[]{:S(2)}) collective-permute-start(bf16[64,1536]{1,0:T(8,128)(2,1)S(1)} %add_convert_fusion.2), channel_id=1, source_target_pairs={{0,16},{1,9},{2,18},{3,11},{4,20},{5,13},{6,22},{7,15},{8,24},{9,1... | collective-permute-start | bytes 589832 | tf_op jit(solution)/shard_map/ppermute | solution.py:398
  118.5 9.5 %collective-permute-start.13 = (bf16[64,2560]{1,0:T(8,128)(2,1)S(1)}, bf16[64,2560]{1,0:T(8,128)(2,1)S(1)}, u32[]{:S(2)}, u32[]{:S(2)}) collective-permute-start(bf16[64,2560]{1,0:T(8,128)(2,1)S(1)} %pad_maximum_fusion.2), channel_id=1, source_target_pairs={{0,2},{1,5},{2,0},{3,7},{4,6},{5,1},{6,4},{7,3},{8,10},{9,13},{10,... | collective-permute-start | bytes 983048 | tf_op jit(solution)/shard_map/ppermute | solution.py:398
  128.2 11.4 %collective-permute-start.14 = (bf16[128,2560]{1,0:T(8,128)(2,1)S(1)}, bf16[128,2560]{1,0:T(8,128)(2,1)S(1)}, u32[]{:S(2)}, u32[]{:S(2)}) collective-permute-start(bf16[128,2560]{1,0:T(8,128)(2,1)S(1)} %pad_maximum_fusion.1), channel_id=1, source_target_pairs={{0,4},{1,3},{2,6},{3,1},{4,0},{5,7},{6,2},{7,5},{8,12},{9,11},{10,... | collective-permute-start | bytes 1966088 | tf_op jit(solution)/shard_map/ppermute | solution.py:398
  129.7 15.2 %all-to-all-start.2 = ((bf16[8,64,512]{2,1,0:T(8,128)(2,1)}), bf16[8,64,512]{2,1,0:T(8,128)(2,1)S(1)}, u32[]{:S(2)}, u32[]{:S(2)}) async-start(bf16[8,64,512]{2,1,0:T(8,128)(2,1)} %bitcast.7), calls=%async_computation.2 | async-start | bytes 1048576 | tf_op jit(solution)/shard_map/all_to_all | solution.py:394
  139.9 25.9 %collective-permute-start.15 = (bf16[256,2560]{1,0:T(8,128)(2,1)S(1)}, bf16[256,2560]{1,0:T(8,128)(2,1)S(1)}, u32[]{:S(2)}, u32[]{:S(2)}) collective-permute-start(bf16[256,2560]{1,0:T(8,128)(2,1)S(1)} %pad_maximum_fusion.source), channel_id=1, source_target_pairs={{0,1},{1,0},{2,3},{3,2},{4,5},{5,4},{6,7},{7,6},{8,9},{9,8},{10,11... | collective-permute-start | bytes 3932168 | tf_op jit(solution)/shard_map/ppermute | solution.py:390
  144.8 11.6 %collective-permute-start.3 = (bf16[512,512]{1,0:T(8,128)(2,1)S(1)}, bf16[512,512]{1,0:T(8,128)(2,1)}, u32[]{:S(2)}, u32[]{:S(2)}) collective-permute-start(bf16[512,512]{1,0:T(8,128)(2,1)S(1)} %bitcast.25), channel_id=1, source_target_pairs={{0,2},{2,0},{1,3},{3,1},{4,6},{6,4},{5,7},{7,5},{8,10},{10,8},{9,1... | collective-permute-start | bytes 1572872 | tf_op jit(solution)/shard_map/ppermute | solution.py:390
  147.4 8.5 %collective-permute-start = (s32[1,512]{1,0:T(1,128)S(1)}, s32[1,512]{1,0:T(1,128)S(1)}, u32[]{:S(2)}, u32[]{:S(2)}) collective-permute-start(s32[1,512]{1,0:T(1,128)S(1)} %reshape.91), channel_id=1, source_target_pairs={{0,2},{2,0},{1,3},{3,1},{4,6},{6,4},{5,7},{7,5},{8,10},{10,8},{9,1... | collective-permute-start | bytes 6152 | tf_op jit(solution)/shard_map/ppermute | solution.py:390
  148.1 8.3 %collective-permute-start.1 = (s32[1,512]{1,0:T(1,128)S(1)}, s32[1,512]{1,0:T(1,128)S(1)}, u32[]{:S(2)}, u32[]{:S(2)}) collective-permute-start(s32[1,512]{1,0:T(1,128)S(1)} %reshape.91), channel_id=1, source_target_pairs={{0,1},{1,0},{2,3},{3,2},{4,5},{5,4},{6,7},{7,6},{8,9},{9,8},{10,11... | collective-permute-start | bytes 6152 | tf_op jit(solution)/shard_map/ppermute | solution.py:390
  155.9 1.2 collective-permute-start.2
  155.9 2.0 %collective-permute-start.4 = (bf16[512,512]{1,0:T(8,128)(2,1)S(1)}, bf16[512,512]{1,0:T(8,128)(2,1)S(1)}, u32[]{:S(2)}, u32[]{:S(2)}) collective-permute-start(bf16[512,512]{1,0:T(8,128)(2,1)S(1)} %bitcast.26), channel_id=1, source_target_pairs={{0,1},{1,0},{2,3},{3,2},{4,5},{5,4},{6,7},{7,6},{8,9},{9,8},{10,11... | collective-permute-start | bytes 1572872 | tf_op jit(solution)/shard_map/ppermute | solution.py:390
  156.4 2.3 %collective-permute-start.5 = (bf16[512,512]{1,0:T(8,128)(2,1)}, bf16[512,512]{1,0:T(8,128)(2,1)S(1)}, u32[]{:S(2)}, u32[]{:S(2)}) collective-permute-start(bf16[512,512]{1,0:T(8,128)(2,1)} %collective-permute-done.3.refs_5_), channel_id=1, source_target_pairs={{0,1},{1,0},{2,3},{3,2},{4,5},{5,4},{6,7},{7,6},{8,9},{9,8},{10,11... | collective-permute-start | bytes 1572872 | tf_op jit(solution)/shard_map/ppermute | solution.py:390

commit v8 on v7

--- a/solution.py
+++ b/solution.py
@@ -67,6 +67,28 @@
 def one_hot_rows(slot_row, slots):
     at = lax.broadcasted_iota(jnp.int32, (slots, slot_row.shape[1]), 0)
     return jnp.where(slot_row[...] == at, 1.0, 0.0).astype(BF)
+
+
+def gather_kernel(asked_ref, table_ref, out_ref, total):
+    step, rows = pl.program_id(0), table_ref.shape[0]
+    lane = step * rows + lax.broadcasted_iota(jnp.int32, (asked_ref.shape[1], rows), 1)
+    columns = asked_ref[...].T
+    picks = [
+        jnp.where(columns[:, o : o + 1] == lane, 1.0, 0.0).astype(BF) for o in range(asked_ref.shape[0])
+    ]
+    part = mm(jnp.concatenate(picks, axis=0), table_ref[...])
+
+    @pl.when(step == 0)
+    def _():
+        total[...] = part
+
+    @pl.when(step > 0)
+    def _():
+        total[...] += part
+
+    @pl.when(step == pl.num_programs(0) - 1)
+    def _():
+        out_ref[...] = total[...].astype(BF)
 
 
 def early_kernel(slot_row, wout_ref, og_ref, dgated_ref, res_ref):
@@ -326,6 +348,20 @@
     )
 
 
+def gather(table, asked, steps=2):
+    slots, rows, width = asked.shape[0] * asked.shape[1], table.shape[0] // steps, table.shape[1]
+    return pl.pallas_call(
+        gather_kernel,
+        out_shape=jax.ShapeDtypeStruct((slots, width), BF),
+        grid=(steps,),
+        in_specs=[pl.BlockSpec(asked.shape, lambda i: (0, 0)), pl.BlockSpec((rows, width), lambda i: (i, 0))],
+        out_specs=pl.BlockSpec((slots, width), lambda i: (0, 0)),
+        scratch_shapes=[pltpu.VMEM((slots, width), F32)],
+        compiler_params=pltpu.CompilerParams(vmem_limit_bytes=MIB * 2**20),
+        cost_estimate=pl.CostEstimate(flops=10**9, bytes_accessed=10**7, transcendentals=0),
+    )(asked, table)
+
+
 def call_first(order, tokens, slots, width):
     loads = [((width, 4 * width), BF), ((width, width), BF), ((tokens, width), BF), ((tokens, width), BF)]
     outs = [
@@ -448,7 +484,7 @@
     slots = requests.shape[0] * requests.shape[1]
     tokens = event_slot.shape[0]
     asked = exchange(requests, emb)
-    found = item_table[asked]
+    found = gather(item_table, asked).reshape(asked.shape + (width,))
     fetched = exchange(found, emb)
     rows = fetched.reshape(slots, width)
     slot_row, slot_col = event_slot.reshape(1, tokens), event_slot.reshape(tokens, 1)

time: 168 us -> 167 us (level)
  local copies, waits for them, and re-layouts: 7.95 us -> 2.49 us
  Pallas kernels: 50.3 us -> 55.6 us
    gather x1 -> x0, local copies, waits for them, and re-layouts: 5.39 us -> none  [on_device(): found = item_table[asked]]
    pallas_call x0 -> x1, Pallas kernels: none -> 5.33 us  [gather(): pl.pallas_call(gather_kernel, out_shape=jax.ShapeDtypeStruct((slots, widt...]
where the time goes in v8:
time: 167 us; the launch traced here: 166 us
  waiting for transfers between devices  68.2 us (41%)
  Pallas kernels  55.6 us (33%)
  starting transfers between devices  22.6 us (14%)
  blocking collectives  13.7 us (8%)
  other arithmetic  2.97 us (2%)
  local copies, waits for them, and re-layouts  2.49 us (1%)
    ppermute x8, waiting for transfers between devices, swap(): lax.ppermute(x, AXES, [(d, partner(d)) for d in range(lax.axis_size(AXES))])  33 us
    all_to_all x3, waiting for transfers between devices, exchange(): return lax.all_to_all(x, axes, split_axis=0, concat_axis=0, tiled=True)  24 us
    pallas_call x1, Pallas kernels, on_device(): first(lengths, slot_row, slot_col, rows, in_weight, out_weight, out_grad,...  20.1 us
    pallas_call x1, Pallas kernels, on_device(): call_attention(tokens, slots, width)  17.5 us
    all_to_all x1, blocking collectives, exchange(): return lax.all_to_all(x, axes, split_axis=0, concat_axis=0, tiled=True)  13.7 us
    all_to_all x3, starting transfers between devices, exchange(): return lax.all_to_all(x, axes, split_axis=0, concat_axis=0, tiled=True)  12.1 us
    ppermute x8, waiting for transfers between devices, other_place(): return lax.ppermute(x, axis, [(i, i ^ 1) for i in range(size)])  11.1 us
    ppermute x8, starting transfers between devices, swap(): lax.ppermute(x, AXES, [(d, partner(d)) for d in range(lax.axis_size(AXES))])  7.79 us
  transfers between devices with their start and end apart: 19, of which 16 were waited for; matrix products, arithmetic and copies ran while one was open for 2% of the time, Pallas kernels for 6%

profile of v8, /device:TPU:0, one launch (start us, length us, event | category | flops | bytes accessed | tf_op | source)
XLA Modules:
  0.0 166.4 jit_solution(12984137136758726249)
XLA Ops:
  0.6 13.7 %all_to_all.26 = s32[8,1,64]{2,1,0:T(1,128)} all-to-all(s32[8,1,64]{2,1,0:T(1,128)} %bitcast.38), channel_id=1, replica_groups=mesh['e1'=4,'e0'=2,'s1'=2,'s0'=2] {'e1','e0'}, dimensions={0} | all-to-all | bytes 4096 | tf_op jit(solution)/shard_map/all_to_all | solution.py:430
  14.3 5.3 %shard_map.102 = bf16[512,512]{1,0:T(8,128)(2,1)} custom-call(s32[8,64]{1,0:T(8,128)} %bitcast.33, bf16[4096,512]{1,0:T(8,128)(2,1)} %table_ref.1), custom_call_target="tpu_custom_call" | custom-call | flops 1000000000 | bytes 10000000 | tf_op jit(solution)/shard_map/pallas_call | solution.py:353
  19.6 3.5 %all-to-all-start.1 = ((bf16[8,64,512]{2,1,0:T(8,128)(2,1)}), bf16[8,64,512]{2,1,0:T(8,128)(2,1)S(1)}, u32[]{:S(2)}, u32[]{:S(2)}) async-start(bf16[8,64,512]{2,1,0:T(8,128)(2,1)} %bitcast.28), calls=%async_computation.1 | async-start | bytes 1048576 | tf_op jit(solution)/shard_map/all_to_all | solution.py:430
  23.1 1.0 copy.14.slot_col
  24.2 3.7 %shard_map.103 = (bf16[1024,512]{1,0:T(8,128)(2,1)}, f32[512,512]{1,0:T(8,128)}) custom-call(s32[1,1024]{1,0:T(1,128)} %bitcast.34, bf16[512,512]{1,0:T(8,128)(2,1)} %refs_1_.1, bf16[1024,512]{1,0:T(8,128)(2,1)} %refs_2_.1), custom_call_target="tpu_custom_call" | custom-call | flops 1000000000 | bytes 10000000 | tf_op jit(solution)/shard_map/pallas_call | solution.py:494
  27.8 8.7 %all-to-all-done.1 = bf16[8,64,512]{2,1,0:T(8,128)(2,1)S(1)} async-done(((bf16[8,64,512]{2,1,0:T(8,128)(2,1)}), bf16[8,64,512]{2,1,0:T(8,128)(2,1)S(1)}, u32[]{:S(2)}, u32[]{:S(2)}) %all-to-all-start.1) | async-done | bytes 524320 | tf_op jit(solution)/shard_map/all_to_all | solution.py:430
  37.3 20.1 %shard_map.104 = (bf16[1024,512]{1,0:T(8,128)(2,1)}, bf16[512,1024]{1,0:T(8,128)(2,1)}, bf16[512,512]{1,0:T(8,128)(2,1)}, bf16[512,512]{1,0:T(8,128)(2,1)}, bf16...) custom-call(s32[1,8]{1,0:T(1,128)} %len_ref.3, s32[1,1024]{1,0:T(1,128)} %bitcast.35, ...), custom_call_target="tpu_custom_call" | custom-call | flops 10000000000 | bytes 10000000 | tf_op jit(solution)/shard_map/pallas_call | solution.py:498
  57.4 17.5 %shard_map.105 = (bf16[512,512]{1,0:T(8,128)(2,1)}, bf16[256,1536]{1,0:T(8,128)(2,1)}, bf16[256,1536]{1,0:T(8,128)(2,1)}) custom-call(s32[1,8]{1,0:T(1,128)} %len_ref.3, s32[1,1]{1,0:T(1,128)} %bitcast.6.core_ref, s32[1,1024]{1,0:T(1,128)} %bitcast.36, bf16[1024,1536]{1,0:T(8,128)(2,1)} %get-tuple-element.22.refs_0_, ...), custom_call_target="tpu_custom_call" | custom-call | flops 10000000000 | bytes 10000000 | tf_op jit(solution)/shard_map/pallas_call | solution.py:502
  75.0 2.5 %collective-permute-done.8 = bf16[256,1536]{1,0:T(8,128)(2,1)S(1)} collective-permute-done((bf16[256,1536]{1,0:T(8,128)(2,1)}, bf16[256,1536]{1,0:T(8,128)(2,1)S(1)}, u32[]{:S(2)}, u32[]{:S(2)}) %collective-permute-start.8) | collective-permute-done | bytes 786464 | tf_op jit(solution)/shard_map/ppermute | solution.py:426
  77.5 1.3 add_convert_fusion
  78.8 1.5 collective-permute-start.9
  80.4 3.7 %all-to-all-start.3 = ((bf16[8,64,1024]{2,1,0:T(8,128)(2,1)}), bf16[8,64,1024]{2,1,0:T(8,128)(2,1)S(1)}, u32[]{:S(2)}, u32[]{:S(2)}) async-start(bf16[8,64,1024]{2,1,0:T(8,128)(2,1)} %bitcast.10), calls=%async_computation.3 | async-start | bytes 2097152 | tf_op jit(solution)/shard_map/all_to_all | solution.py:430
  84.1 2.6 %collective-permute-done.9 = bf16[128,1536]{1,0:T(8,128)(2,1)S(1)} collective-permute-done((bf16[128,1536]{1,0:T(8,128)(2,1)S(1)}, bf16[128,1536]{1,0:T(8,128)(2,1)S(1)}, u32[]{:S(2)}, u32[]{:S(2)}) %collective-permute-start.9) | collective-permute-done | bytes 393248 | tf_op jit(solution)/shard_map/ppermute | solution.py:434
  86.8 1.6 collective-permute-start.10
  88.4 10.5 %all-to-all-done.3 = bf16[8,64,1024]{2,1,0:T(8,128)(2,1)S(1)} async-done(((bf16[8,64,1024]{2,1,0:T(8,128)(2,1)}), bf16[8,64,1024]{2,1,0:T(8,128)(2,1)S(1)}, u32[]{:S(2)}, u32[]{:S(2)}) %all-to-all-start.3) | async-done | bytes 1048608 | tf_op jit(solution)/shard_map/all_to_all | solution.py:430
  99.3 1.1 collective-permute-done.10
  101.3 4.2 %collective-permute-done.6 = bf16[64,1024]{1,0:T(8,128)(2,1)S(1)} collective-permute-done((bf16[64,1024]{1,0:T(8,128)(2,1)S(1)}, bf16[64,1024]{1,0:T(8,128)(2,1)S(1)}, u32[]{:S(2)}, u32[]{:S(2)}) %collective-permute-start.6) | collective-permute-done | bytes 131104 | tf_op jit(solution)/shard_map/ppermute | solution.py:434
  106.1 5.0 %collective-permute-done.11 = bf16[64,1536]{1,0:T(8,128)(2,1)S(1)} collective-permute-done((bf16[64,1536]{1,0:T(8,128)(2,1)S(1)}, bf16[64,1536]{1,0:T(8,128)(2,1)S(1)}, u32[]{:S(2)}, u32[]{:S(2)}) %collective-permute-start.11) | collective-permute-done | bytes 196640 | tf_op jit(solution)/shard_map/ppermute | solution.py:434
  111.2 1.6 collective-permute-done.7
  112.8 5.6 %collective-permute-done.12 = bf16[64,1536]{1,0:T(8,128)(2,1)S(1)} collective-permute-done((bf16[64,1536]{1,0:T(8,128)(2,1)S(1)}, bf16[64,1536]{1,0:T(8,128)(2,1)S(1)}, u32[]{:S(2)}, u32[]{:S(2)}) %collective-permute-start.12) | collective-permute-done | bytes 196640 | tf_op jit(solution)/shard_map/ppermute | solution.py:434
  118.4 1.5 collective-permute-start.13
  120.0 8.0 %collective-permute-done.13 = bf16[64,2560]{1,0:T(8,128)(2,1)S(1)} collective-permute-done((bf16[64,2560]{1,0:T(8,128)(2,1)S(1)}, bf16[64,2560]{1,0:T(8,128)(2,1)S(1)}, u32[]{:S(2)}, u32[]{:S(2)}) %collective-permute-start.13) | collective-permute-done | bytes 327712 | tf_op jit(solution)/shard_map/ppermute | solution.py:434
  128.1 1.4 collective-permute-start.14
  129.6 4.9 %all-to-all-start.2 = ((bf16[8,64,512]{2,1,0:T(8,128)(2,1)}), bf16[8,64,512]{2,1,0:T(8,128)(2,1)S(1)}, u32[]{:S(2)}, u32[]{:S(2)}) async-start(bf16[8,64,512]{2,1,0:T(8,128)(2,1)} %bitcast.7), calls=%async_computation.2 | async-start | bytes 1048576 | tf_op jit(solution)/shard_map/all_to_all | solution.py:430
  134.5 5.0 %collective-permute-done.14 = bf16[128,2560]{1,0:T(8,128)(2,1)S(1)} collective-permute-done((bf16[128,2560]{1,0:T(8,128)(2,1)S(1)}, bf16[128,2560]{1,0:T(8,128)(2,1)S(1)}, u32[]{:S(2)}, u32[]{:S(2)}) %collective-permute-start.14) | collective-permute-done | bytes 655392 | tf_op jit(solution)/shard_map/ppermute | solution.py:434
  139.9 4.9 %all-to-all-done.2 = bf16[8,64,512]{2,1,0:T(8,128)(2,1)S(1)} async-done(((bf16[8,64,512]{2,1,0:T(8,128)(2,1)}), bf16[8,64,512]{2,1,0:T(8,128)(2,1)S(1)}, u32[]{:S(2)}, u32[]{:S(2)}) %all-to-all-start.2) | async-done | bytes 524320 | tf_op jit(solution)/shard_map/all_to_all | solution.py:430
  144.8 1.4 collective-permute-start.3
  148.1 6.4 %collective-permute-done = s32[1,512]{1,0:T(1,128)S(1)} collective-permute-done((s32[1,512]{1,0:T(1,128)S(1)}, s32[1,512]{1,0:T(1,128)S(1)}, u32[]{:S(2)}, u32[]{:S(2)}) %collective-permute-start) | collective-permute-done | bytes 2080 | tf_op jit(solution)/shard_map/ppermute | solution.py:426
  155.6 0.9 collective-permute-done.4.refs_6_
  157.3 5.2 %shard_map.106 = f32[1024,512]{1,0:T(8,128)} custom-call(s32[1,512]{1,0:T(1,128)S(1)} %broadcast_subtract_fusion.3.refs_0_, s32[1,512]{1,0:T(1,128)S(1)} %broadcast_subtract_fusion.2.refs_1_, s32[1,512]{1,0:T(1,128)S(1)} %broadcast_subtract_fusion.1.refs_2_, s32[1,512]{1,0:T(1,128)S(1)} %broadcast_subtract_fusion.refs_3_, bf16[512,512]{1,0:T(8,128)(2,1)S(1)} %bitcast.25, ...), custom_call_target="tpu_custom_call" | custom-call | flops 1000000000 | bytes 10000000 | tf_op jit(solution)/shard_map/pallas_call | solution.py:514
  162.4 1.9 %shard_map.107 = (f32[512,2048]{1,0:T(8,128)}, f32[512,512]{1,0:T(8,128)}) custom-call(s32[1]{0:T(128)} %bitcast.9.place_ref, bf16[256,2560]{1,0:T(8,128)(2,1)S(1)} %pad_maximum_fusion.source), custom_call_target="tpu_custom_call" | custom-call | flops 100000000 | bytes 4000000 | tf_op jit(solution)/shard_map/pallas_call | solution.py:408
  164.4 2.0 %shard_map.108 = (f32[512,2048]{1,0:T(8,128)}, f32[512,512]{1,0:T(8,128)}) custom-call(s32[1]{0:T(128)S(6)} %sub.32.place_ref, bf16[256,2560]{1,0:T(8,128)(2,1)S(1)} %collective-permute-done.15.source, f32[512,2048]{1,0:T(8,128)} %get-tuple-element.32.refs_0_, f32[512,512]{1,0:T(8,128)} %get-tuple-element.33.refs_1_), custom_call_target="tpu_custom_call", output_to_operand_aliasing={{0}: (2, {}), {1}: (3, {})} | custom-call | flops 100000000 | bytes 4000000 | tf_op jit(solution)/shard_map/pallas_call | solution.py:408
  (43 shorter events, 7.4 us)
Async XLA Ops:
  14.3 8.8 %copy-start.2 = (s32[1024]{0:T(1024)S(1)}, s32[1024]{0:T(1024)}, u32[]{:S(2)}) copy-start(s32[1024]{0:T(1024)} %param.9) | copy-start | bytes 12292
  19.6 16.9 %all-to-all-start.1 = ((bf16[8,64,512]{2,1,0:T(8,128)(2,1)}), bf16[8,64,512]{2,1,0:T(8,128)(2,1)S(1)}, u32[]{:S(2)}, u32[]{:S(2)}) async-start(bf16[8,64,512]{2,1,0:T(8,128)(2,1)} %bitcast.28), calls=%async_computation.1 | async-start | bytes 1048576 | tf_op jit(solution)/shard_map/all_to_all | solution.py:430
  36.5 0.8 copy-start
  74.9 2.6 %collective-permute-start.8 = (bf16[256,1536]{1,0:T(8,128)(2,1)}, bf16[256,1536]{1,0:T(8,128)(2,1)S(1)}, u32[]{:S(2)}, u32[]{:S(2)}) collective-permute-start(bf16[256,1536]{1,0:T(8,128)(2,1)} %get-tuple-element.31), channel_id=1, source_target_pairs={{0,1},{1,0},{2,3},{3,2},{4,5},{5,4},{6,7},{7,6},{8,9},{9,8},{10,11... | collective-permute-start | bytes 2359304 | tf_op jit(solution)/shard_map/ppermute | solution.py:426
  78.8 7.8 %collective-permute-start.9 = (bf16[128,1536]{1,0:T(8,128)(2,1)S(1)}, bf16[128,1536]{1,0:T(8,128)(2,1)S(1)}, u32[]{:S(2)}, u32[]{:S(2)}) collective-permute-start(bf16[128,1536]{1,0:T(8,128)(2,1)S(1)} %dynamic-slice_bitcast_fusion), channel_id=1, source_target_pairs={{0,4},{1,3},{2,6},{3,1},{4,0},{5,7},{6,2},{7,5},{8,12},{9,11},{10,... | collective-permute-start | bytes 1179656 | tf_op jit(solution)/shard_map/ppermute | solution.py:434
  80.4 18.5 %all-to-all-start.3 = ((bf16[8,64,1024]{2,1,0:T(8,128)(2,1)}), bf16[8,64,1024]{2,1,0:T(8,128)(2,1)S(1)}, u32[]{:S(2)}, u32[]{:S(2)}) async-start(bf16[8,64,1024]{2,1,0:T(8,128)(2,1)} %bitcast.10), calls=%async_computation.3 | async-start | bytes 2097152 | tf_op jit(solution)/shard_map/all_to_all | solution.py:430
  86.8 13.6 %collective-permute-start.10 = (bf16[64,1536]{1,0:T(8,128)(2,1)S(1)}, bf16[64,1536]{1,0:T(8,128)(2,1)S(1)}, u32[]{:S(2)}, u32[]{:S(2)}) collective-permute-start(bf16[64,1536]{1,0:T(8,128)(2,1)S(1)} %dynamic-slice_bitcast_fusion.1), channel_id=1, source_target_pairs={{0,2},{1,5},{2,0},{3,7},{4,6},{5,1},{6,4},{7,3},{8,10},{9,13},{10,... | collective-permute-start | bytes 589832 | tf_op jit(solution)/shard_map/ppermute | solution.py:434
  99.1 6.4 %collective-permute-start.6 = (bf16[64,1024]{1,0:T(8,128)(2,1)S(1)}, bf16[64,1024]{1,0:T(8,128)(2,1)S(1)}, u32[]{:S(2)}, u32[]{:S(2)}) collective-permute-start(bf16[64,1024]{1,0:T(8,128)(2,1)S(1)} %reduce_sum.12), channel_id=1, source_target_pairs={{0,8},{1,17},{2,10},{3,19},{4,12},{5,21},{6,14},{7,23},{8,0},{9,25... | collective-permute-start | bytes 393224 | tf_op jit(solution)/shard_map/ppermute | solution.py:434
  100.4 10.6 %collective-permute-start.11 = (bf16[64,1536]{1,0:T(8,128)(2,1)S(1)}, bf16[64,1536]{1,0:T(8,128)(2,1)S(1)}, u32[]{:S(2)}, u32[]{:S(2)}) collective-permute-start(bf16[64,1536]{1,0:T(8,128)(2,1)S(1)} %fusion.1), channel_id=1, source_target_pairs={{0,8},{1,17},{2,10},{3,19},{4,12},{5,21},{6,14},{7,23},{8,0},{9,25... | collective-permute-start | bytes 589832 | tf_op jit(solution)/shard_map/ppermute | solution.py:434
  105.6 7.2 %collective-permute-start.7 = (bf16[64,1024]{1,0:T(8,128)(2,1)S(1)}, bf16[64,1024]{1,0:T(8,128)(2,1)S(1)}, u32[]{:S(2)}, u32[]{:S(2)}) collective-permute-start(bf16[64,1024]{1,0:T(8,128)(2,1)S(1)} %add_convert_fusion.4), channel_id=1, source_target_pairs={{0,16},{1,9},{2,18},{3,11},{4,20},{5,13},{6,22},{7,15},{8,24},{9,1... | collective-permute-start | bytes 393224 | tf_op jit(solution)/shard_map/ppermute | solution.py:434
  111.1 7.2 %collective-permute-start.12 = (bf16[64,1536]{1,0:T(8,128)(2,1)S(1)}, bf16[64,1536]{1,0:T(8,128)(2,1)S(1)}, u32[]{:S(2)}, u32[]{:S(2)}) collective-permute-start(bf16[64,1536]{1,0:T(8,128)(2,1)S(1)} %add_convert_fusion.2), channel_id=1, source_target_pairs={{0,16},{1,9},{2,18},{3,11},{4,20},{5,13},{6,22},{7,15},{8,24},{9,1... | collective-permute-start | bytes 589832 | tf_op jit(solution)/shard_map/ppermute | solution.py:434
  118.4 9.5 %collective-permute-start.13 = (bf16[64,2560]{1,0:T(8,128)(2,1)S(1)}, bf16[64,2560]{1,0:T(8,128)(2,1)S(1)}, u32[]{:S(2)}, u32[]{:S(2)}) collective-permute-start(bf16[64,2560]{1,0:T(8,128)(2,1)S(1)} %pad_maximum_fusion.2), channel_id=1, source_target_pairs={{0,2},{1,5},{2,0},{3,7},{4,6},{5,1},{6,4},{7,3},{8,10},{9,13},{10,... | collective-permute-start | bytes 983048 | tf_op jit(solution)/shard_map/ppermute | solution.py:434
  128.1 11.4 %collective-permute-start.14 = (bf16[128,2560]{1,0:T(8,128)(2,1)S(1)}, bf16[128,2560]{1,0:T(8,128)(2,1)S(1)}, u32[]{:S(2)}, u32[]{:S(2)}) collective-permute-start(bf16[128,2560]{1,0:T(8,128)(2,1)S(1)} %pad_maximum_fusion.1), channel_id=1, source_target_pairs={{0,4},{1,3},{2,6},{3,1},{4,0},{5,7},{6,2},{7,5},{8,12},{9,11},{10,... | collective-permute-start | bytes 1966088 | tf_op jit(solution)/shard_map/ppermute | solution.py:434
  129.6 15.2 %all-to-all-start.2 = ((bf16[8,64,512]{2,1,0:T(8,128)(2,1)}), bf16[8,64,512]{2,1,0:T(8,128)(2,1)S(1)}, u32[]{:S(2)}, u32[]{:S(2)}) async-start(bf16[8,64,512]{2,1,0:T(8,128)(2,1)} %bitcast.7), calls=%async_computation.2 | async-start | bytes 1048576 | tf_op jit(solution)/shard_map/all_to_all | solution.py:430
  139.7 6.9 %copy-start.1 = (s32[8,1,64]{2,1,0:T(1,128)S(1)}, s32[8,1,64]{2,1,0:T(1,128)}, u32[]{:S(2)}) copy-start(s32[8,1,64]{2,1,0:T(1,128)} %all_to_all.26) | copy-start | bytes 6148
  139.8 24.6 %collective-permute-start.15 = (bf16[256,2560]{1,0:T(8,128)(2,1)S(1)}, bf16[256,2560]{1,0:T(8,128)(2,1)S(1)}, u32[]{:S(2)}, u32[]{:S(2)}) collective-permute-start(bf16[256,2560]{1,0:T(8,128)(2,1)S(1)} %pad_maximum_fusion.source), channel_id=1, source_target_pairs={{0,1},{1,0},{2,3},{3,2},{4,5},{5,4},{6,7},{7,6},{8,9},{9,8},{10,11... | collective-permute-start | bytes 3932168 | tf_op jit(solution)/shard_map/ppermute | solution.py:426
  144.8 10.2 %collective-permute-start.3 = (bf16[512,512]{1,0:T(8,128)(2,1)S(1)}, bf16[512,512]{1,0:T(8,128)(2,1)}, u32[]{:S(2)}, u32[]{:S(2)}) collective-permute-start(bf16[512,512]{1,0:T(8,128)(2,1)S(1)} %bitcast.23), channel_id=1, source_target_pairs={{0,2},{2,0},{1,3},{3,1},{4,6},{6,4},{5,7},{7,5},{8,10},{10,8},{9,1... | collective-permute-start | bytes 1572872 | tf_op jit(solution)/shard_map/ppermute | solution.py:426
  147.4 7.0 %collective-permute-start = (s32[1,512]{1,0:T(1,128)S(1)}, s32[1,512]{1,0:T(1,128)S(1)}, u32[]{:S(2)}, u32[]{:S(2)}) collective-permute-start(s32[1,512]{1,0:T(1,128)S(1)} %reshape.67), channel_id=1, source_target_pairs={{0,2},{2,0},{1,3},{3,1},{4,6},{6,4},{5,7},{7,5},{8,10},{10,8},{9,1... | collective-permute-start | bytes 6152 | tf_op jit(solution)/shard_map/ppermute | solution.py:426
  148.0 6.9 %collective-permute-start.1 = (s32[1,512]{1,0:T(1,128)S(1)}, s32[1,512]{1,0:T(1,128)S(1)}, u32[]{:S(2)}, u32[]{:S(2)}) collective-permute-start(s32[1,512]{1,0:T(1,128)S(1)} %reshape.67), channel_id=1, source_target_pairs={{0,1},{1,0},{2,3},{3,2},{4,5},{5,4},{6,7},{7,6},{8,9},{9,8},{10,11... | collective-permute-start | bytes 6152 | tf_op jit(solution)/shard_map/ppermute | solution.py:426
  154.5 1.2 collective-permute-start.2
  154.5 2.0 %collective-permute-start.4 = (bf16[512,512]{1,0:T(8,128)(2,1)S(1)}, bf16[512,512]{1,0:T(8,128)(2,1)S(1)}, u32[]{:S(2)}, u32[]{:S(2)}) collective-permute-start(bf16[512,512]{1,0:T(8,128)(2,1)S(1)} %bitcast.24), channel_id=1, source_target_pairs={{0,1},{1,0},{2,3},{3,2},{4,5},{5,4},{6,7},{7,6},{8,9},{9,8},{10,11... | collective-permute-start | bytes 1572872 | tf_op jit(solution)/shard_map/ppermute | solution.py:426
  155.0 2.3 %collective-permute-start.5 = (bf16[512,512]{1,0:T(8,128)(2,1)}, bf16[512,512]{1,0:T(8,128)(2,1)S(1)}, u32[]{:S(2)}, u32[]{:S(2)}) collective-permute-start(bf16[512,512]{1,0:T(8,128)(2,1)} %collective-permute-done.3.refs_5_), channel_id=1, source_target_pairs={{0,1},{1,0},{2,3},{3,2},{4,5},{5,4},{6,7},{7,6},{8,9},{9,8},{10,11... | collective-permute-start | bytes 1572872 | tf_op jit(solution)/shard_map/ppermute | solution.py:426
